TPU v7x, 8 devices: a whole 2x2x1 slice. The times are simulated.
8 devices in a mesh: dp: 1 (over z), x: 8 (over y, x, core).
Axes of the slice: x: 2, y: 2, z: 1, core: 2. Of those that a mesh axis runs over, the one named last changes fastest.
Arguments:
- c_raw: bfloat16 [96, 6144, 512], P('dp', 'x')
- k_raw: bfloat16 [96, 6144, 64], P('dp', 'x')
- norm_gain: bfloat16 [512], replicated
- rope_cos: float32 [6144, 32], P('x')
- rope_sin: float32 [6144, 32], P('x')
- seq_lens: int32 [96], P('dp')
- q_lat: bfloat16 [96, 128, 512], P(('dp', 'x'))
- q_rope: bfloat16 [96, 128, 64], P(('dp', 'x'))
Outputs:
- output 1: bfloat16 [96, 6144, 512], P(('dp', 'x'))
- output 2: bfloat16 [96, 6144, 64], P(('dp', 'x'))
- output 3: bfloat16 [96, 128, 512], P(('dp', 'x'))
All inputs are finite; a program needn't handle non-finite values.
Results may differ from a plain program's by a relative error of at most 0.00562413.
Values are sent between devices in bfloat16 or wider.
A program may use at most 1 GiB of HBM per device.

v0:
```python
import functools

import jax
import jax.numpy as jnp
import numpy as np
from jax import lax
from jax.experimental import pallas as pl
from jax.experimental.pallas import tpu as pltpu
from jax.sharding import PartitionSpec as P

NORM_EPS = 1e-6
N = 8
CHIPS = 4
REQ = 12
SEQ = 768
RANK = 512
ROPE = 64
HEADS = 128
UNIT = 256
PER = SEQ // UNIT
PIECES = RANK // 128
HALVES = UNIT // 128
ROWS = PIECES * UNIT + HALVES * ROPE
SLOTS = 2 * REQ * PER
NONE = 10**6
ATTN_SCALE = (RANK + ROPE) ** -0.5
DEPTH = 2


class Plan:
    def __init__(self, chunks):
        self.chunks = chunks
        self.starts = np.cumsum([0] + [c[0] for c in chunks])[:-1]
        assert sum(c[0] for c in chunks) == SLOTS
        self.slot = np.full((N, CHIPS, SLOTS), NONE, np.int32)
        self.cap = np.zeros((N, CHIPS), np.int32)
        for s in range(N):
            for q in range(CHIPS):
                for chunk, start in zip(chunks, self.starts):
                    width = chunk[0]
                    if q == 0 or s in chunk[q + 1]:
                        self.slot[s, q, start : start + width] = self.cap[s, q] + np.arange(width)
                        self.cap[s, q] += width


ALL = (0, 1, 2, 3, 4, 5, 6, 7)
UP = (0, 1, 2, 3)
LOW = (4, 5, 6, 7)


NO_CHIP1 = (0, 1, 4, 5, 6, 7)
NO_3 = (0, 1, 2, 4, 5, 6, 7)


def direct(width):
    return width, "direct", ALL, ALL, ALL


def relay(width):
    return width, "relay", UP, ALL, UP


def no_chip1(width):
    return width, "direct", ALL, NO_CHIP1, NO_CHIP1


def no_3(width):
    return width, "direct", ALL, NO_3, NO_3


def end(width):
    return width, "direct", UP, ALL, UP


PLANS = (
    Plan([direct(4), direct(8), relay(7), no_chip1(5), relay(7), no_chip1(5), no_3(6)] + [direct(8)] * 3 + [end(4), end(2)]),
    Plan([direct(4), direct(8), relay(6), no_chip1(6), relay(4), no_3(6)] + [direct(8)] * 4 + [end(4), end(2)]),
    Plan([direct(4)] + [direct(8)] * 8 + [direct(4)]),
)


def norm_pack(width, start, tabs, c_raw, k_t, gain, cos_t, sin_t, after):
    steps = CHIPS * width

    def kernel(req_ref, unit_ref, ok_ref, c_ref, k_ref, g_ref, cos_ref, sin_ref, *refs):
        outs, (buf, sem) = refs[len(after) : len(after) + CHIPS], refs[-2:]
        n = pl.program_id(0)
        q, j = n // width, n % width
        ok_at = lambda m: ok_ref[m // width * SLOTS + start + m % width] > 0
        drain = lambda m: pltpu.make_async_copy(buf.at[m % 2], outs[0].at[0], sem.at[m % 2]).wait()
        slot = n % 2

        @pl.when((n >= 2) & ok_at(jnp.maximum(n - 2, 0)))
        def _():
            drain(n)

        @pl.when(ok_at(n))
        def _():
            key = k_ref[0].astype(jnp.float32)
            lo, hi = key[: ROPE // 2], key[ROPE // 2 :]
            cos, sin = cos_ref[...], sin_ref[...]
            rot = jnp.concatenate([lo * cos - hi * sin, hi * cos + lo * sin], axis=0).astype(jnp.bfloat16)
            for p in range(HALVES):
                at = PIECES * UNIT + p * ROPE
                buf[slot, at : at + ROPE, :] = rot[:, p * 128 : (p + 1) * 128]
                x = c_ref[0, p * 128 : (p + 1) * 128, :].astype(jnp.float32)
                inv = lax.rsqrt(jnp.mean(x * x, axis=-1, keepdims=True) + NORM_EPS)
                y = (x * inv * g_ref[...].astype(jnp.float32)).astype(jnp.bfloat16)
                for i in range(PIECES):
                    at = i * UNIT + p * 128
                    buf[slot, at : at + 128, :] = y[:, i * 128 : (i + 1) * 128]
            for mine in range(CHIPS):

                @pl.when(q == mine)
                def _(mine=mine):
                    pltpu.make_async_copy(buf.at[slot], outs[mine].at[j], sem.at[slot]).start()

        @pl.when(n == steps - 1)
        def _():
            @pl.when(ok_at(n - 1))
            def _():
                drain(n - 1)

            @pl.when(ok_at(n))
            def _():
                drain(n)

    def at(n):
        return n // width * SLOTS + start + n % width

    grid_spec = pltpu.PrefetchScalarGridSpec(
        num_scalar_prefetch=3,
        grid=(steps,),
        in_specs=[
            pl.BlockSpec((1, UNIT, RANK), lambda n, req, unit, ok: (req[at(n)], unit[at(n)], 0)),
            pl.BlockSpec((1, ROPE, UNIT), lambda n, req, unit, ok: (req[at(n)], 0, unit[at(n)])),
            pl.BlockSpec((1, RANK), lambda n, *_: (0, 0)),
            pl.BlockSpec((ROPE // 2, UNIT), lambda n, req, unit, ok: (0, unit[at(n)])),
            pl.BlockSpec((ROPE // 2, UNIT), lambda n, req, unit, ok: (0, unit[at(n)])),
        ]
        + [pl.BlockSpec(memory_space=pl.ANY)] * len(after),
        out_specs=[pl.BlockSpec(memory_space=pl.ANY)] * CHIPS,
        scratch_shapes=[pltpu.VMEM((2, ROWS, 128), jnp.bfloat16), pltpu.SemaphoreType.DMA((2,))],
    )
    return pl.pallas_call(
        kernel,
        grid_spec=grid_spec,
        out_shape=[jax.ShapeDtypeStruct((width, ROWS, 128), jnp.bfloat16)] * CHIPS,
        cost_estimate=pl.CostEstimate(flops=width * 10**8, bytes_accessed=width * 4 * 589824, transcendentals=0),
        name="norm_pack",
    )(*tabs, c_raw, k_t, gain, cos_t, sin_t, *after)


def attend(chunk, start, first, last, counts, codes, parts, q_lat, q_rope_t, caches, state):
    def kernel(count_ref, code_ref, *refs):
        part_refs, (qa_ref, qr_ref) = refs[:N], refs[N : N + 2]
        old_ref = None if first else refs[N + 4]
        outs = refs[N + (4 if first else 5) :]
        c_out, k_out, st_ref = outs[:3]
        buf, c_buf, k_buf, in_sem, c_sem, k_sem = outs[-6:]
        steps = count_ref[chunk]

        def fetch(n):
            code = code_ref[N * start + n]
            part, place = code // 2**22, code // 2**18 % 16
            for k in range(N):

                @pl.when(part == k)
                def _(k=k):
                    pltpu.make_async_copy(part_refs[k].at[place], buf.at[n % 3], in_sem.at[n % 3]).start()

        def drain(slot):
            pltpu.make_async_copy(c_buf.at[slot], c_out.at[0, pl.ds(0, UNIT), :], c_sem.at[slot]).wait()
            pltpu.make_async_copy(k_buf.at[slot], k_out.at[0, :, pl.ds(0, UNIT)], k_sem.at[slot]).wait()

        def step(n, _):
            code = code_ref[N * start + n]
            left, r = code // 2**9 % 2**9, code // 2**5 % 16
            at = pl.ds(pl.multiple_of(code % 2**5 * UNIT, UNIT), UNIT)
            slot = n % 2

            @pl.when(n + 2 < steps)
            def _():
                fetch(n + 2)

            pltpu.make_async_copy(part_refs[0].at[0], buf.at[n % 3], in_sem.at[n % 3]).wait()

            @pl.when(n >= 2)
            def _():
                drain(slot)

            row_ok = lax.broadcasted_iota(jnp.int32, (UNIT, 1), 0) < left
            lane_ok = lax.broadcasted_iota(jnp.int32, (1, UNIT), 1) < left
            for i in range(PIECES):
                piece = jnp.where(row_ok, buf[n % 3, i * UNIT : (i + 1) * UNIT, :].astype(jnp.float32), 0.0)
                c_buf[slot, :, i * 128 : (i + 1) * 128] = piece.astype(jnp.bfloat16)
            for p in range(HALVES):
                base = PIECES * UNIT + p * ROPE
                key = buf[n % 3, base : base + ROPE, :].astype(jnp.float32)
                key = jnp.where(lane_ok[:, p * 128 : (p + 1) * 128], key, 0.0)
                k_buf[slot, :, p * 128 : (p + 1) * 128] = key.astype(jnp.bfloat16)
            pltpu.make_async_copy(c_buf.at[slot], c_out.at[r, at, :], c_sem.at[slot]).start()
            pltpu.make_async_copy(k_buf.at[slot], k_out.at[r, :, at], k_sem.at[slot]).start()

            c = c_buf[slot]
            scores = lax.dot_general(qa_ref[r], c, (((1,), (1,)), ((), ())), preferred_element_type=jnp.float32)
            scores += lax.dot_general(qr_ref[r], k_buf[slot], (((0,), (0,)), ((), ())), preferred_element_type=jnp.float32)
            scores = jnp.where(lane_ok, scores * ATTN_SCALE, -1e30)
            l_old = st_ref[r, :, RANK : RANK + 1]
            m_old = st_ref[r, :, RANK + 128 : RANK + 129]
            m_new = jnp.maximum(m_old, jnp.max(scores, axis=-1, keepdims=True))
            weights = jnp.exp(scores - m_new)
            decay = jnp.exp(m_old - m_new)
            l_new = l_old * decay + jnp.sum(weights, axis=-1, keepdims=True)
            st_ref[r, :, RANK : RANK + 128] = jnp.broadcast_to(l_new, (HEADS, 128))
            st_ref[r, :, RANK + 128 :] = jnp.broadcast_to(m_new, (HEADS, 128))
            st_ref[r, :, :RANK] = st_ref[r, :, :RANK] * decay + jnp.dot(
                weights.astype(jnp.bfloat16), c, preferred_element_type=jnp.float32
            )
            return 0

        @pl.when(steps > 0)
        def _():
            fetch(0)

        @pl.when(steps > 1)
        def _():
            fetch(1)

        if first:
            st_ref[:, :, : RANK + 128] = jnp.zeros((REQ, HEADS, RANK + 128), jnp.float32)
            st_ref[:, :, RANK + 128 :] = jnp.full((REQ, HEADS, 128), -1e30, jnp.float32)
        else:
            st_ref[...] = old_ref[...]
        lax.fori_loop(0, steps, step, 0)

        @pl.when(steps > 1)
        def _():
            drain(steps % 2)

        @pl.when(steps > 0)
        def _():
            drain((steps + 1) % 2)

        if last:
            o_ref = outs[3]

            def finish(r, _):
                o_ref[r] = (st_ref[r, :, :RANK] / st_ref[r, :, RANK : RANK + 1]).astype(jnp.bfloat16)
                return 0

            lax.fori_loop(0, REQ, finish, 0)

    smem, vmem, anywhere = (pl.BlockSpec(memory_space=m) for m in (pltpu.SMEM, pltpu.VMEM, pl.ANY))
    state_shape = (REQ, HEADS, RANK + 256)
    in_specs = [smem] * 2 + [anywhere] * N + [vmem] * 2 + [anywhere] * 2
    operands = [counts, codes, *parts, q_lat, q_rope_t]
    aliases = {len(operands): 0, len(operands) + 1: 1}
    operands += list(caches)
    if not first:
        in_specs.append(vmem)
        operands.append(state)
    out_specs = [anywhere, anywhere, vmem]
    out_shape = [jax.ShapeDtypeStruct(c.shape, c.dtype) for c in caches] + [jax.ShapeDtypeStruct(state_shape, jnp.float32)]
    if last:
        out_specs.append(vmem)
        out_shape.append(jax.ShapeDtypeStruct((REQ, HEADS, RANK), jnp.bfloat16))
    return pl.pallas_call(
        kernel,
        in_specs=in_specs,
        out_specs=out_specs,
        out_shape=out_shape,
        scratch_shapes=[
            pltpu.VMEM((3, ROWS, 128), jnp.bfloat16),
            pltpu.VMEM((2, UNIT, RANK), jnp.bfloat16),
            pltpu.VMEM((2, ROPE, UNIT), jnp.bfloat16),
            pltpu.SemaphoreType.DMA((3,)),
            pltpu.SemaphoreType.DMA((2,)),
            pltpu.SemaphoreType.DMA((2,)),
        ],
        input_output_aliases=aliases,
        cost_estimate=pl.CostEstimate(flops=2 * 10**8, bytes_accessed=8 * 589824, transcendentals=0),
        name="attend",
    )(*operands)


def blank_caches(lens):
    def kernel(len_ref, c_ref, k_ref, c_zero, k_zero, c_sem, k_sem):
        c_zero[...] = jnp.zeros_like(c_zero)
        k_zero[...] = jnp.zeros_like(k_zero)

        def each(act):
            def block(n, _):
                r, s = n // N, n % N

                @pl.when(len_ref[r] < (s + 1) * SEQ)
                def _():
                    at = pl.ds(pl.multiple_of(s * SEQ, SEQ), SEQ)
                    act(pltpu.make_async_copy(c_zero, c_ref.at[r, at, :], c_sem.at[n]))
                    act(pltpu.make_async_copy(k_zero, k_ref.at[r, :, at], k_sem.at[n]))

                return 0

            lax.fori_loop(0, REQ * N, block, 0)

        each(lambda copy: copy.start())
        each(lambda copy: copy.wait())

    return pl.pallas_call(
        kernel,
        in_specs=[pl.BlockSpec(memory_space=pltpu.SMEM)],
        out_specs=[pl.BlockSpec(memory_space=pl.ANY)] * 2,
        out_shape=[
            jax.ShapeDtypeStruct((REQ, N * SEQ, RANK), jnp.bfloat16),
            jax.ShapeDtypeStruct((REQ, ROPE, N * SEQ), jnp.bfloat16),
        ],
        scratch_shapes=[
            pltpu.VMEM((SEQ, RANK), jnp.bfloat16),
            pltpu.VMEM((ROPE, SEQ), jnp.bfloat16),
            pltpu.SemaphoreType.DMA((REQ * N,)),
            pltpu.SemaphoreType.DMA((REQ * N,)),
        ],
        cost_estimate=pl.CostEstimate(flops=4 * 10**8, bytes_accessed=85 * 10**6, transcendentals=0),
        name="blank",
    )(lens)


def count_units(seq_lens):
    valid = jnp.clip(seq_lens[None, :] - SEQ * jnp.arange(N, dtype=jnp.int32)[:, None], 0, SEQ)
    left = valid.reshape(N, CHIPS, 2, REQ)[..., None] - UNIT * jnp.arange(PER, dtype=jnp.int32)
    left = left.transpose(0, 1, 3, 4, 2).reshape(N, CHIPS, SLOTS)
    return left


def split_place(place):
    return place // (2 * PER), place // 2 % PER, place % 2


def run_plan(plan, me, left, own_lens, c_raw, k_t, gain, cos_t, sin_t, q_lat, q_rope_t):
    chip = me // 2
    have = left > 0
    rank = jnp.cumsum(have.astype(jnp.int32), axis=-1)
    places = jnp.arange(SLOTS, dtype=jnp.int32)

    chips = chip ^ jnp.arange(CHIPS)
    mine = rank[me][chips]
    slot = jnp.asarray(plan.slot)[me]
    place = jnp.sum((mine[:, None, :] <= slot[:, :, None]).astype(jnp.int32), axis=-1)
    final = jnp.max(jnp.where(have[me][chips], places, 0), axis=-1, keepdims=True)
    held = jnp.minimum(place, final)
    req, unit, core = split_place(held)
    pack_tabs = [
        ((2 * chips[:, None] + core) * REQ + req).reshape(-1),
        unit.reshape(-1),
        (place < SLOTS).astype(jnp.int32).reshape(-1),
    ]

    part = jnp.arange(N)
    source = me ^ part
    theirs = rank[source, chip]
    slot = jnp.asarray(plan.slot)[source, part // 2]
    place = jnp.sum((theirs[:, None, :] <= slot[:, :, None]).astype(jnp.int32), axis=-1)
    req, unit, core = split_place(place)
    rows = jnp.sum(jnp.where(place[:, :, None] == places, left[source, chip][:, None, :], 0), axis=-1)
    rows = jnp.where(core == me % 2, jnp.minimum(rows, UNIT), 0)
    code = part[:, None] * 2**22 + rows * 2**9 + req * 2**5 + source[:, None] * PER + unit
    inside = np.concatenate([np.arange(c[0]) for c in plan.chunks]).astype(np.int32)
    code = jnp.where(rows > 0, code + jnp.asarray(inside) * 2**18, 0)
    code = jnp.concatenate([code[:, s : s + c[0]].reshape(-1) for c, s in zip(plan.chunks, plan.starts)])
    chunk_of = np.repeat(np.arange(len(plan.chunks)), [N * c[0] for c in plan.chunks])
    heads = (N * plan.starts)[chunk_of].astype(np.int32)
    same = jnp.asarray(chunk_of.astype(np.int32))[:, None] == jnp.asarray(chunk_of.astype(np.int32))[None, :]
    number = jnp.arange(N * SLOTS, dtype=jnp.int32)
    before = jnp.sum((same & (number[None, :] < number[:, None]) & (code > 0)[None, :]).astype(jnp.int32), axis=-1)
    goes_to = jnp.where(code > 0, jnp.asarray(heads) + before, -1)
    codes = jnp.sum(jnp.where(goes_to[None, :] == number[:, None], code[None, :], 0), axis=-1)
    in_chunk = jnp.asarray(chunk_of.astype(np.int32))[None, :] == jnp.arange(len(plan.chunks), dtype=jnp.int32)[:, None]
    counts = jnp.sum((in_chunk & (code > 0)[None, :]).astype(jnp.int32), axis=-1)

    pairs = lambda sources, hop: [(s, s ^ hop) for s in sources]

    def send(x, pairs):
        return lax.ppermute(x, "x", pairs)

    caches = blank_caches(own_lens)
    state = None
    landed, owns, twins = [], [], []
    count = len(plan.chunks)

    after = []
    for c, (width, kind, along, across, diagonal) in enumerate(plan.chunks):
        staged = norm_pack(width, int(plan.starts[c]), pack_tabs, c_raw, k_t, gain, cos_t, sin_t, after)
        after = [staged[0]]
        sends = list(staged)
        if c >= DEPTH:
            sends, landed[c - DEPTH] = lax.optimization_barrier((sends, landed[c - DEPTH]))
        owns.append(sends[0])
        twins.append(send(sends[0], pairs(ALL, 1)))
        lower = [(t, t ^ 1) for t in LOW]
        far = send(sends[3], pairs(ALL, 4) if kind == "relay" else pairs(diagonal, 6))
        near = send(sends[1], pairs(UP, 2) + lower if along == UP else pairs(ALL, 2))
        over = send(sends[2], pairs(across, 4))
        landed.append([near, over, far])
    for c, (_, kind, _, _, _) in enumerate(plan.chunks):
        near, over, far = landed[c]
        if kind == "relay":
            far = send(far, pairs(LOW, 2) + [(t, t ^ 1) for t in UP])
        parts = [owns[c], twins[c]]
        for x in (near, over, far):
            parts += [x, send(x, pairs(ALL, 1))]
        got = attend(c, int(plan.starts[c]), c == 0, c == count - 1, counts, codes, parts, q_lat, q_rope_t, caches, state)
        caches, state = got[:2], got[2]
    return caches[0], caches[1], got[3]


def local_step(c_raw, k_raw, norm_gain, rope_cos, rope_sin, seq_lens, q_lat, q_rope):
    me = lax.axis_index("x")
    left = count_units(seq_lens)
    need = jnp.sum((left > 0).astype(jnp.int32), axis=-1)
    fits = []
    for plan in PLANS:
        cap = np.stack([[plan.cap[s, (s // 2) ^ chip] for chip in range(CHIPS)] for s in range(N)])
        fits.append(jnp.all(need <= jnp.asarray(cap)))
    which = jnp.argmax(jnp.stack(fits)).astype(jnp.int32)
    own_lens = lax.dynamic_slice_in_dim(seq_lens, me * REQ, REQ)
    args = (me, left, own_lens, c_raw, jnp.swapaxes(k_raw, 1, 2), norm_gain[None, :], rope_cos.T, rope_sin.T, q_lat, jnp.swapaxes(q_rope, 1, 2))

    def branch(number, *args):
        return run_plan(PLANS[number], *args)

    branches = [functools.partial(branch, number) for number in range(len(PLANS))]
    c_cache, k_cache_t, o_lat = lax.switch(which, branches, *args) if len(PLANS) > 1 else branches[0](*args)
    return c_cache, jnp.swapaxes(k_cache_t, 1, 2), o_lat


def solution(mesh):
    seq_spec = P("dp", "x", None)
    req_spec = P(("dp", "x"), None, None)
    return jax.shard_map(
        local_step,
        mesh=mesh,
        in_specs=(seq_spec, seq_spec, P(None), P("x", None), P("x", None), P("dp"), req_spec, req_spec),
        out_specs=(req_spec, req_spec, req_spec),
        check_vma=False,
    )
```

profile of v0, /device:TPU:7, one launch (start us, length us, event | category | flops | bytes accessed | tf_op | source)
XLA Modules:
  0.0 1295.9 jit_solution(12813875653204685689)
XLA Ops:
  8.9 1285.8 %conditional.1 = (bf16[12,6144,512]{2,1,0:T(8,128)(2,1)}, bf16[12,64,6144]{2,1,0:T(8,128)(2,1)}, bf16[12,128,512]{2,1,0:T(8,128)(2,1)}) conditional(s32[]{:T(128)} %clamp.9, ((), s32[8,4,72]{0,2,1:T(8,128)S(1)}, s32[]{:T(128)}, (), (), /*index=5*/(), (), (), bf16[96,768,512]{2,1,0:T(8,128)(2,1)}, ...), branch_computations={%region_5.14_spmd, %region_14.23_spmd, %region_23.32_spmd} | conditional | flops 10003525632 | bytes 1058226688 | solution.py:432
  13.8 12.0 norm_pack.34
  30.0 15.2 %norm_pack.35 = (bf16[8,1152,128]{2,1,0:T(8,128)(2,1)}, bf16[8,1152,128]{2,1,0:T(8,128)(2,1)}, bf16[8,1152,128]{2,1,0:T(8,128)(2,1)}, bf16[8,1152,128]{2,1,0:T(8,128)(2,1)}) custom-call(s32[288]{0:T(512)} %get-tuple-element.831.req_ref, s32[288]{0:T(512)} %get-tuple-element.830.unit_ref, s32[288]{0:T(512)} %reshape.689.ok_ref, ...), custom_call_target="tpu_custom_call" | custom-call | flops 800000000 | bytes 18874368 | tf_op jit(solution)/shard_map/cond/branch_0_fun/norm_pack/pallas_call | solution.py:145
  45.2 4.7 norm_pack.36
  53.0 25.3 %collective-permute-done.24.refs_6_ = bf16[4,1152,128]{2,1,0:T(8,128)(2,1)} collective-permute-done((bf16[4,1152,128]{2,1,0:T(8,128)(2,1)}, bf16[4,1152,128]{2,1,0:T(8,128)(2,1)}, u32[]{:S(2)}, u32[]{:S(2)}) %collective-permute-start.24) | collective-permute-done | bytes 1179680 | tf_op jit(solution)/shard_map/cond/branch_0_fun/ppermute | solution.py:383
  87.5 45.6 %collective-permute-done.refs_2_ = bf16[8,1152,128]{2,1,0:T(8,128)(2,1)} collective-permute-done((bf16[8,1152,128]{2,1,0:T(8,128)(2,1)}, bf16[8,1152,128]{2,1,0:T(8,128)(2,1)}, u32[]{:S(2)}, u32[]{:S(2)}) %collective-permute-start) | collective-permute-done | bytes 2359328 | tf_op jit(solution)/shard_map/cond/branch_0_fun/ppermute | solution.py:383
  134.1 50.6 %collective-permute-done.1.refs_4_ = bf16[8,1152,128]{2,1,0:T(8,128)(2,1)} collective-permute-done((bf16[8,1152,128]{2,1,0:T(8,128)(2,1)}, bf16[8,1152,128]{2,1,0:T(8,128)(2,1)}, u32[]{:S(2)}, u32[]{:S(2)}) %collective-permute-start.1) | collective-permute-done | bytes 2359328 | tf_op jit(solution)/shard_map/cond/branch_0_fun/ppermute | solution.py:383
  187.0 4.6 norm_pack.37
  191.6 9.2 collective-permute-start.3
  202.2 27.1 %collective-permute-done.26.refs_4_ = bf16[7,1152,128]{2,1,0:T(8,128)(2,1)} collective-permute-done((bf16[7,1152,128]{2,1,0:T(8,128)(2,1)}, bf16[7,1152,128]{2,1,0:T(8,128)(2,1)}, u32[]{:S(2)}, u32[]{:S(2)}) %collective-permute-start.26) | collective-permute-done | bytes 2064416 | tf_op jit(solution)/shard_map/cond/branch_0_fun/ppermute | solution.py:383
  229.2 4.1 collective-permute-start.4
  233.3 40.1 %collective-permute-done.27 = bf16[7,1152,128]{2,1,0:T(8,128)(2,1)} collective-permute-done((bf16[7,1152,128]{2,1,0:T(8,128)(2,1)}, bf16[7,1152,128]{2,1,0:T(8,128)(2,1)}, u32[]{:S(2)}, u32[]{:S(2)}) %collective-permute-start.27) | collective-permute-done | bytes 2064416 | tf_op jit(solution)/shard_map/cond/branch_0_fun/ppermute | solution.py:383
  273.5 3.3 collective-permute-start.5
  277.9 57.0 %collective-permute-done.4.refs_4_ = bf16[5,1152,128]{2,1,0:T(8,128)(2,1)} collective-permute-done((bf16[5,1152,128]{2,1,0:T(8,128)(2,1)}, bf16[5,1152,128]{2,1,0:T(8,128)(2,1)}, u32[]{:S(2)}, u32[]{:S(2)}) %collective-permute-start.4) | collective-permute-done | bytes 1474592 | tf_op jit(solution)/shard_map/cond/branch_0_fun/ppermute | solution.py:383
  335.8 4.6 norm_pack.38
  340.4 3.8 collective-permute-start.76
  344.2 5.1 collective-permute-start.74
  349.3 4.6 norm_pack.39
  355.6 29.4 %collective-permute-done.76.refs_6_ = bf16[7,1152,128]{2,1,0:T(8,128)(2,1)} collective-permute-done((bf16[7,1152,128]{2,1,0:T(8,128)(2,1)}, bf16[7,1152,128]{2,1,0:T(8,128)(2,1)}, u32[]{:S(2)}, u32[]{:S(2)}) %collective-permute-start.76) | collective-permute-done | bytes 2064416 | tf_op jit(solution)/shard_map/cond/branch_0_fun/ppermute | solution.py:383
  386.5 5.9 collective-permute-start.71
  396.7 25.1 %collective-permute-start.7 = (bf16[5,1152,128]{2,1,0:T(8,128)(2,1)}, bf16[5,1152,128]{2,1,0:T(8,128)(2,1)}, u32[]{:S(2)}, u32[]{:S(2)}) collective-permute-start(bf16[5,1152,128]{2,1,0:T(8,128)(2,1)} %get-tuple-element.143), channel_id=1, source_target_pairs={{0,4},{1,5},{4,0},{5,1},{6,2},{7,3}} | collective-permute-start | bytes 4423688 | tf_op jit(solution)/shard_map/cond/branch_0_fun/ppermute | solution.py:383
  421.8 4.7 collective-permute-done.29.refs_4_
  429.3 73.0 %collective-permute-done.30 = bf16[7,1152,128]{2,1,0:T(8,128)(2,1)} collective-permute-done((bf16[7,1152,128]{2,1,0:T(8,128)(2,1)}, bf16[7,1152,128]{2,1,0:T(8,128)(2,1)}, u32[]{:S(2)}, u32[]{:S(2)}) %collective-permute-start.30) | collective-permute-done | bytes 2064416 | tf_op jit(solution)/shard_map/cond/branch_0_fun/ppermute | solution.py:383
  502.3 9.6 collective-permute-start.72
  511.9 4.6 norm_pack.40
  516.5 15.5 %collective-permute-done.7.refs_4_ = bf16[5,1152,128]{2,1,0:T(8,128)(2,1)} collective-permute-done((bf16[5,1152,128]{2,1,0:T(8,128)(2,1)}, bf16[5,1152,128]{2,1,0:T(8,128)(2,1)}, u32[]{:S(2)}, u32[]{:S(2)}) %collective-permute-start.7) | collective-permute-done | bytes 1474592 | tf_op jit(solution)/shard_map/cond/branch_0_fun/ppermute | solution.py:383
  532.9 5.4 collective-permute-start.32
  538.3 4.6 norm_pack.41
  542.9 5.9 collective-permute-start.61
  554.1 8.9 collective-permute-start.67
  566.6 8.9 collective-permute-start.33
  575.5 6.2 collective-permute-start.56
  581.7 65.1 %collective-permute-done.33.refs_6_ = bf16[6,1152,128]{2,1,0:T(8,128)(2,1)S(1)} collective-permute-done((bf16[6,1152,128]{2,1,0:T(8,128)(2,1)}, bf16[6,1152,128]{2,1,0:T(8,128)(2,1)S(1)}, u32[]{:S(2)}, u32[]{:S(2)}) %collective-permute-start.33) | collective-permute-done | bytes 1769504 | tf_op jit(solution)/shard_map/cond/branch_0_fun/ppermute | solution.py:383
  649.8 7.2 collective-permute-start.66
  659.5 4.6 norm_pack.42
  664.8 86.6 %collective-permute-done.10.refs_4_ = bf16[8,1152,128]{2,1,0:T(8,128)(2,1)} collective-permute-done((bf16[8,1152,128]{2,1,0:T(8,128)(2,1)}, bf16[8,1152,128]{2,1,0:T(8,128)(2,1)}, u32[]{:S(2)}, u32[]{:S(2)}) %collective-permute-start.10) | collective-permute-done | bytes 2359328 | tf_op jit(solution)/shard_map/cond/branch_0_fun/ppermute | solution.py:383
  751.3 4.3 collective-permute-start.68
  755.6 4.5 collective-permute-done.9.refs_2_
  764.4 4.6 norm_pack.43
  769.1 17.3 %collective-permute-start.36 = (bf16[8,1152,128]{2,1,0:T(8,128)(2,1)}, bf16[8,1152,128]{2,1,0:T(8,128)(2,1)S(1)}, u32[]{:S(2)}, u32[]{:S(2)}) collective-permute-start(bf16[8,1152,128]{2,1,0:T(8,128)(2,1)} %get-tuple-element.186), channel_id=1, source_target_pairs={{0,6},{1,7},{2,4},{3,5},{4,2},{5,3},{6,0},{7,1}} | collective-permute-start | bytes 7077896 | tf_op jit(solution)/shard_map/cond/branch_0_fun/ppermute | solution.py:383
  787.4 23.3 %collective-permute-done.34.refs_2_ = bf16[8,1152,128]{2,1,0:T(8,128)(2,1)} collective-permute-done((bf16[8,1152,128]{2,1,0:T(8,128)(2,1)}, bf16[8,1152,128]{2,1,0:T(8,128)(2,1)}, u32[]{:S(2)}, u32[]{:S(2)}) %collective-permute-start.34) | collective-permute-done | bytes 2359328 | tf_op jit(solution)/shard_map/cond/branch_0_fun/ppermute | solution.py:383
  812.1 54.5 %collective-permute-done.35.refs_4_ = bf16[8,1152,128]{2,1,0:T(8,128)(2,1)} collective-permute-done((bf16[8,1152,128]{2,1,0:T(8,128)(2,1)}, bf16[8,1152,128]{2,1,0:T(8,128)(2,1)}, u32[]{:S(2)}, u32[]{:S(2)}) %collective-permute-start.35) | collective-permute-done | bytes 2359328 | tf_op jit(solution)/shard_map/cond/branch_0_fun/ppermute | solution.py:383
  874.1 4.6 norm_pack.44
  879.1 41.5 %collective-permute-done.12.refs_2_ = bf16[8,1152,128]{2,1,0:T(8,128)(2,1)} collective-permute-done((bf16[8,1152,128]{2,1,0:T(8,128)(2,1)}, bf16[8,1152,128]{2,1,0:T(8,128)(2,1)}, u32[]{:S(2)}, u32[]{:S(2)}) %collective-permute-start.12) | collective-permute-done | bytes 2359328 | tf_op jit(solution)/shard_map/cond/branch_0_fun/ppermute | solution.py:383
  922.1 49.8 %collective-permute-done.13.refs_4_ = bf16[8,1152,128]{2,1,0:T(8,128)(2,1)} collective-permute-done((bf16[8,1152,128]{2,1,0:T(8,128)(2,1)}, bf16[8,1152,128]{2,1,0:T(8,128)(2,1)}, u32[]{:S(2)}, u32[]{:S(2)}) %collective-permute-start.13) | collective-permute-done | bytes 2359328 | tf_op jit(solution)/shard_map/cond/branch_0_fun/ppermute | solution.py:383
  974.9 4.6 norm_pack.45
  980.0 18.7 %collective-permute-done.40.refs_4_ = bf16[4,1152,128]{2,1,0:T(8,128)(2,1)} collective-permute-done((bf16[4,1152,128]{2,1,0:T(8,128)(2,1)}, bf16[4,1152,128]{2,1,0:T(8,128)(2,1)}, u32[]{:S(2)}, u32[]{:S(2)}) %collective-permute-start.40) | collective-permute-done | bytes 1179680 | tf_op jit(solution)/shard_map/cond/branch_0_fun/ppermute | solution.py:383
  999.4 23.6 %collective-permute-done.42.refs_6_ = bf16[4,1152,128]{2,1,0:T(8,128)(2,1)} collective-permute-done((bf16[4,1152,128]{2,1,0:T(8,128)(2,1)}, bf16[4,1152,128]{2,1,0:T(8,128)(2,1)}, u32[]{:S(2)}, u32[]{:S(2)}) %collective-permute-start.42) | collective-permute-done | bytes 1179680 | tf_op jit(solution)/shard_map/cond/branch_0_fun/ppermute | solution.py:383
  1024.9 7.6 collective-permute-done.18.refs_4_
  1033.8 16.4 %collective-permute-done.20.refs_6_ = bf16[2,1152,128]{2,1,0:T(8,128)(2,1)} collective-permute-done((bf16[2,1152,128]{2,1,0:T(8,128)(2,1)}, bf16[2,1152,128]{2,1,0:T(8,128)(2,1)}, u32[]{:S(2)}, u32[]{:S(2)}) %collective-permute-start.20) | collective-permute-done | bytes 589856 | tf_op jit(solution)/shard_map/cond/branch_0_fun/ppermute | solution.py:383
  1050.2 3.1 collective-permute-start.51
  1068.3 13.8 %blank.3 = (bf16[12,6144,512]{2,1,0:T(8,128)(2,1)}, bf16[12,64,6144]{2,1,0:T(8,128)(2,1)}) custom-call(s32[12]{0:T(128)S(1)} %copy-done.83), custom_call_target="tpu_custom_call" | custom-call | flops 400000000 | bytes 85000000 | tf_op jit(solution)/shard_map/cond/branch_0_fun/blank/pallas_call | solution.py:309
  1083.0 23.4 %attend.34 = (bf16[12,6144,512]{2,1,0:T(8,128)(2,1)}, bf16[12,64,6144]{2,1,0:T(8,128)(2,1)}, f32[12,128,768]{2,1,0:T(8,128)}) custom-call(s32[12]{0:T(128)} %convert_reduce_fusion.3.count_ref, s32[576]{0:T(1024)} %select_reduce_fusion.code_ref, bf16[4,1152,128]{2,1,0:T(8,128)(2,1)} %get-tuple-element.109.refs_0_, ...), custom_call_target="tpu_custom_call", output_to_operand_aliasing={{0}: (12, {}), {1}: (13, {})} | custom-call | flops 200000000 | bytes 4718592 | tf_op jit(solution)/shard_map/cond/branch_0_fun/attend/pallas_call | solution.py:268
  1106.4 33.3 %attend.35 = (bf16[12,6144,512]{2,1,0:T(8,128)(2,1)}, bf16[12,64,6144]{2,1,0:T(8,128)(2,1)}, f32[12,128,768]{2,1,0:T(8,128)}) custom-call(s32[12]{0:T(128)} %convert_reduce_fusion.3.count_ref, s32[576]{0:T(1024)} %select_reduce_fusion.code_ref, bf16[8,1152,128]{2,1,0:T(8,128)(2,1)} %get-tuple-element.110.refs_0_, ...), custom_call_target="tpu_custom_call", output_to_operand_aliasing={{0}: (12, {}), {1}: (13, {})} | custom-call | flops 200000000 | bytes 4718592 | tf_op jit(solution)/shard_map/cond/branch_0_fun/attend/pallas_call | solution.py:268
  1139.7 16.1 %attend.36 = (bf16[12,6144,512]{2,1,0:T(8,128)(2,1)}, bf16[12,64,6144]{2,1,0:T(8,128)(2,1)}, f32[12,128,768]{2,1,0:T(8,128)}) custom-call(s32[12]{0:T(128)} %convert_reduce_fusion.3.count_ref, s32[576]{0:T(1024)} %select_reduce_fusion.code_ref, bf16[7,1152,128]{2,1,0:T(8,128)(2,1)} %get-tuple-element.219.refs_0_, ...), custom_call_target="tpu_custom_call", output_to_operand_aliasing={{0}: (12, {}), {1}: (13, {})} | custom-call | flops 200000000 | bytes 4718592 | tf_op jit(solution)/shard_map/cond/branch_0_fun/attend/pallas_call | solution.py:268
  1155.8 14.1 %attend.37 = (bf16[12,6144,512]{2,1,0:T(8,128)(2,1)}, bf16[12,64,6144]{2,1,0:T(8,128)(2,1)}, f32[12,128,768]{2,1,0:T(8,128)}) custom-call(s32[12]{0:T(128)} %convert_reduce_fusion.3.count_ref, s32[576]{0:T(1024)} %select_reduce_fusion.code_ref, bf16[5,1152,128]{2,1,0:T(8,128)(2,1)} %get-tuple-element.215.refs_0_, ...), custom_call_target="tpu_custom_call", output_to_operand_aliasing={{0}: (12, {}), {1}: (13, {})} | custom-call | flops 200000000 | bytes 4718592 | tf_op jit(solution)/shard_map/cond/branch_0_fun/attend/pallas_call | solution.py:268
  1169.9 15.4 %attend.38 = (bf16[12,6144,512]{2,1,0:T(8,128)(2,1)}, bf16[12,64,6144]{2,1,0:T(8,128)(2,1)}, f32[12,128,768]{2,1,0:T(8,128)}) custom-call(s32[12]{0:T(128)} %convert_reduce_fusion.3.count_ref, s32[576]{0:T(1024)} %select_reduce_fusion.code_ref, bf16[7,1152,128]{2,1,0:T(8,128)(2,1)} %get-tuple-element.211.refs_0_, ...), custom_call_target="tpu_custom_call", output_to_operand_aliasing={{0}: (12, {}), {1}: (13, {})} | custom-call | flops 200000000 | bytes 4718592 | tf_op jit(solution)/shard_map/cond/branch_0_fun/attend/pallas_call | solution.py:268
  1185.3 14.8 %attend.39 = (bf16[12,6144,512]{2,1,0:T(8,128)(2,1)}, bf16[12,64,6144]{2,1,0:T(8,128)(2,1)}, f32[12,128,768]{2,1,0:T(8,128)}) custom-call(s32[12]{0:T(128)} %convert_reduce_fusion.3.count_ref, s32[576]{0:T(1024)} %select_reduce_fusion.code_ref, bf16[5,1152,128]{2,1,0:T(8,128)(2,1)} %get-tuple-element.207.refs_0_, ...), custom_call_target="tpu_custom_call", output_to_operand_aliasing={{0}: (12, {}), {1}: (13, {})} | custom-call | flops 200000000 | bytes 4718592 | tf_op jit(solution)/shard_map/cond/branch_0_fun/attend/pallas_call | solution.py:268
  1200.1 17.5 %attend.40 = (bf16[12,6144,512]{2,1,0:T(8,128)(2,1)}, bf16[12,64,6144]{2,1,0:T(8,128)(2,1)}, f32[12,128,768]{2,1,0:T(8,128)}) custom-call(s32[12]{0:T(128)} %convert_reduce_fusion.3.count_ref, s32[576]{0:T(1024)} %select_reduce_fusion.code_ref, bf16[6,1152,128]{2,1,0:T(8,128)(2,1)} %get-tuple-element.203.refs_0_, ...), custom_call_target="tpu_custom_call", output_to_operand_aliasing={{0}: (12, {}), {1}: (13, {})} | custom-call | flops 200000000 | bytes 4718592 | tf_op jit(solution)/shard_map/cond/branch_0_fun/attend/pallas_call | solution.py:268
  1217.6 23.0 %attend.41 = (bf16[12,6144,512]{2,1,0:T(8,128)(2,1)}, bf16[12,64,6144]{2,1,0:T(8,128)(2,1)}, f32[12,128,768]{2,1,0:T(8,128)}) custom-call(s32[12]{0:T(128)} %convert_reduce_fusion.3.count_ref, s32[576]{0:T(1024)} %select_reduce_fusion.code_ref, bf16[8,1152,128]{2,1,0:T(8,128)(2,1)} %get-tuple-element.199.refs_0_, ...), custom_call_target="tpu_custom_call", output_to_operand_aliasing={{0}: (12, {}), {1}: (13, {})} | custom-call | flops 200000000 | bytes 4718592 | tf_op jit(solution)/shard_map/cond/branch_0_fun/attend/pallas_call | solution.py:268
  1240.5 17.5 %attend.42 = (bf16[12,6144,512]{2,1,0:T(8,128)(2,1)}, bf16[12,64,6144]{2,1,0:T(8,128)(2,1)}, f32[12,128,768]{2,1,0:T(8,128)}) custom-call(s32[12]{0:T(128)} %convert_reduce_fusion.3.count_ref, s32[576]{0:T(1024)} %select_reduce_fusion.code_ref, bf16[8,1152,128]{2,1,0:T(8,128)(2,1)} %get-tuple-element.195.refs_0_, ...), custom_call_target="tpu_custom_call", output_to_operand_aliasing={{0}: (12, {}), {1}: (13, {})} | custom-call | flops 200000000 | bytes 4718592 | tf_op jit(solution)/shard_map/cond/branch_0_fun/attend/pallas_call | solution.py:268
  1258.0 14.8 %attend.43 = (bf16[12,6144,512]{2,1,0:T(8,128)(2,1)}, bf16[12,64,6144]{2,1,0:T(8,128)(2,1)}, f32[12,128,768]{2,1,0:T(8,128)}) custom-call(s32[12]{0:T(128)} %convert_reduce_fusion.3.count_ref, s32[576]{0:T(1024)} %select_reduce_fusion.code_ref, bf16[8,1152,128]{2,1,0:T(8,128)(2,1)} %get-tuple-element.191.refs_0_, ...), custom_call_target="tpu_custom_call", output_to_operand_aliasing={{0}: (12, {}), {1}: (13, {})} | custom-call | flops 200000000 | bytes 4718592 | tf_op jit(solution)/shard_map/cond/branch_0_fun/attend/pallas_call | solution.py:268
  1272.8 7.3 attend.44
  1280.1 8.2 attend.45
  (263 shorter events, 100.7 us)
Async XLA Ops:
  26.1 52.2 %collective-permute-start.24 = (bf16[4,1152,128]{2,1,0:T(8,128)(2,1)}, bf16[4,1152,128]{2,1,0:T(8,128)(2,1)}, u32[]{:S(2)}, u32[]{:S(2)}) collective-permute-start(bf16[4,1152,128]{2,1,0:T(8,128)(2,1)} %get-tuple-element.174), channel_id=1, source_target_pairs={{0,6},{1,7},{2,4},{3,5},{4,2},{5,3},{6,0},{7,1}} | collective-permute-start | bytes 3538952 | tf_op jit(solution)/shard_map/cond/branch_0_fun/ppermute | solution.py:383
  28.4 53.3 %collective-permute-start.82 = (bf16[4,1152,128]{2,1,0:T(8,128)(2,1)}, bf16[4,1152,128]{2,1,0:T(8,128)(2,1)}, u32[]{:S(2)}, u32[]{:S(2)}) collective-permute-start(bf16[4,1152,128]{2,1,0:T(8,128)(2,1)} %get-tuple-element.109.refs_0_), channel_id=1, source_target_pairs={{0,1},{1,0},{2,3},{3,2},{4,5},{5,4},{6,7},{7,6}} | collective-permute-start | bytes 3538952 | tf_op jit(solution)/shard_map/cond/branch_0_fun/ppermute | solution.py:383
  80.0 53.1 %collective-permute-start = (bf16[8,1152,128]{2,1,0:T(8,128)(2,1)}, bf16[8,1152,128]{2,1,0:T(8,128)(2,1)}, u32[]{:S(2)}, u32[]{:S(2)}) collective-permute-start(bf16[8,1152,128]{2,1,0:T(8,128)(2,1)} %get-tuple-element.136), channel_id=1, source_target_pairs={{0,2},{1,3},{2,0},{3,1},{4,6},{5,7},{6,4},{7,5}} | collective-permute-start | bytes 7077896 | tf_op jit(solution)/shard_map/cond/branch_0_fun/ppermute | solution.py:383
  81.5 103.1 %collective-permute-start.1 = (bf16[8,1152,128]{2,1,0:T(8,128)(2,1)}, bf16[8,1152,128]{2,1,0:T(8,128)(2,1)}, u32[]{:S(2)}, u32[]{:S(2)}) collective-permute-start(bf16[8,1152,128]{2,1,0:T(8,128)(2,1)} %get-tuple-element.137), channel_id=1, source_target_pairs={{0,4},{1,5},{2,6},{3,7},{4,0},{5,1},{6,2},{7,3}} | collective-permute-start | bytes 7077896 | tf_op jit(solution)/shard_map/cond/branch_0_fun/ppermute | solution.py:383
  81.8 102.9 %collective-permute-start.2 = (bf16[8,1152,128]{2,1,0:T(8,128)(2,1)}, bf16[8,1152,128]{2,1,0:T(8,128)(2,1)}, u32[]{:S(2)}, u32[]{:S(2)}) collective-permute-start(bf16[8,1152,128]{2,1,0:T(8,128)(2,1)} %get-tuple-element.138), channel_id=1, source_target_pairs={{0,6},{1,7},{2,4},{3,5},{4,2},{5,3},{6,0},{7,1}} | collective-permute-start | bytes 7077896 | tf_op jit(solution)/shard_map/cond/branch_0_fun/ppermute | solution.py:383
  84.4 107.2 %collective-permute-start.78 = (bf16[8,1152,128]{2,1,0:T(8,128)(2,1)S(1)}, bf16[8,1152,128]{2,1,0:T(8,128)(2,1)}, u32[]{:S(2)}, u32[]{:S(2)}) collective-permute-start(bf16[8,1152,128]{2,1,0:T(8,128)(2,1)S(1)} %copy-done.12), channel_id=1, source_target_pairs={{0,1},{1,0},{2,3},{3,2},{4,5},{5,4},{6,7},{7,6}} | collective-permute-start | bytes 7077896 | tf_op jit(solution)/shard_map/cond/branch_0_fun/ppermute | solution.py:383
  86.5 114.4 %collective-permute-start.25 = (bf16[7,1152,128]{2,1,0:T(8,128)(2,1)}, bf16[7,1152,128]{2,1,0:T(8,128)(2,1)}, u32[]{:S(2)}, u32[]{:S(2)}) collective-permute-start(bf16[7,1152,128]{2,1,0:T(8,128)(2,1)} %get-tuple-element.175), channel_id=1, source_target_pairs={{0,2},{1,3},{2,0},{3,1},{4,5},{5,4},{6,7},{7,6}} | collective-permute-start | bytes 6193160 | tf_op jit(solution)/shard_map/cond/branch_0_fun/ppermute | solution.py:383
  133.1 96.1 %collective-permute-start.26 = (bf16[7,1152,128]{2,1,0:T(8,128)(2,1)}, bf16[7,1152,128]{2,1,0:T(8,128)(2,1)}, u32[]{:S(2)}, u32[]{:S(2)}) collective-permute-start(bf16[7,1152,128]{2,1,0:T(8,128)(2,1)} %get-tuple-element.176), channel_id=1, source_target_pairs={{0,4},{1,5},{2,6},{3,7},{4,0},{5,1},{6,2},{7,3}} | collective-permute-start | bytes 6193160 | tf_op jit(solution)/shard_map/cond/branch_0_fun/ppermute | solution.py:383
  184.6 88.8 %collective-permute-start.27 = (bf16[7,1152,128]{2,1,0:T(8,128)(2,1)}, bf16[7,1152,128]{2,1,0:T(8,128)(2,1)}, u32[]{:S(2)}, u32[]{:S(2)}) collective-permute-start(bf16[7,1152,128]{2,1,0:T(8,128)(2,1)} %get-tuple-element.177), channel_id=1, source_target_pairs={{0,4},{1,5},{2,6},{3,7},{4,0},{5,1},{6,2},{7,3}} | collective-permute-start | bytes 6193160 | tf_op jit(solution)/shard_map/cond/branch_0_fun/ppermute | solution.py:383
  184.6 92.1 %collective-permute-start.73 = (bf16[7,1152,128]{2,1,0:T(8,128)(2,1)}, bf16[7,1152,128]{2,1,0:T(8,128)(2,1)}, u32[]{:S(2)}, u32[]{:S(2)}) collective-permute-start(bf16[7,1152,128]{2,1,0:T(8,128)(2,1)} %get-tuple-element.219.refs_0_), channel_id=1, source_target_pairs={{0,1},{1,0},{2,3},{3,2},{4,5},{5,4},{6,7},{7,6}} | collective-permute-start | bytes 6193160 | tf_op jit(solution)/shard_map/cond/branch_0_fun/ppermute | solution.py:383
  191.6 86.2 %collective-permute-start.3 = (bf16[5,1152,128]{2,1,0:T(8,128)(2,1)}, bf16[5,1152,128]{2,1,0:T(8,128)(2,1)S(1)}, u32[]{:S(2)}, u32[]{:S(2)}) collective-permute-start(bf16[5,1152,128]{2,1,0:T(8,128)(2,1)} %get-tuple-element.139), channel_id=1, source_target_pairs={{0,2},{1,3},{2,0},{3,1},{4,6},{5,7},{6,4},{7,5}} | collective-permute-start | bytes 4423688 | tf_op jit(solution)/shard_map/cond/branch_0_fun/ppermute | solution.py:383
  200.9 148.4 %collective-permute-start.79 = (bf16[8,1152,128]{2,1,0:T(8,128)(2,1)}, bf16[8,1152,128]{2,1,0:T(8,128)(2,1)}, u32[]{:S(2)}, u32[]{:S(2)}) collective-permute-start(bf16[8,1152,128]{2,1,0:T(8,128)(2,1)} %collective-permute-done.refs_2_), channel_id=1, source_target_pairs={{0,1},{1,0},{2,3},{3,2},{4,5},{5,4},{6,7},{7,6}} | collective-permute-start | bytes 7077896 | tf_op jit(solution)/shard_map/cond/branch_0_fun/ppermute | solution.py:383
  229.2 105.7 %collective-permute-start.4 = (bf16[5,1152,128]{2,1,0:T(8,128)(2,1)}, bf16[5,1152,128]{2,1,0:T(8,128)(2,1)}, u32[]{:S(2)}, u32[]{:S(2)}) collective-permute-start(bf16[5,1152,128]{2,1,0:T(8,128)(2,1)} %get-tuple-element.140), channel_id=1, source_target_pairs={{0,4},{1,5},{4,0},{5,1},{6,2},{7,3}} | collective-permute-start | bytes 4423688 | tf_op jit(solution)/shard_map/cond/branch_0_fun/ppermute | solution.py:383
  273.5 66.9 %collective-permute-start.5 = (bf16[5,1152,128]{2,1,0:T(8,128)(2,1)}, bf16[5,1152,128]{2,1,0:T(8,128)(2,1)}, u32[]{:S(2)}, u32[]{:S(2)}) collective-permute-start(bf16[5,1152,128]{2,1,0:T(8,128)(2,1)} %get-tuple-element.141), channel_id=1, source_target_pairs={{0,6},{1,7},{4,2},{5,3},{6,0},{7,1}} | collective-permute-start | bytes 4423688 | tf_op jit(solution)/shard_map/cond/branch_0_fun/ppermute | solution.py:383
  276.8 67.4 %collective-permute-start.69 = (bf16[5,1152,128]{2,1,0:T(8,128)(2,1)}, bf16[5,1152,128]{2,1,0:T(8,128)(2,1)}, u32[]{:S(2)}, u32[]{:S(2)}) collective-permute-start(bf16[5,1152,128]{2,1,0:T(8,128)(2,1)} %get-tuple-element.215.refs_0_), channel_id=1, source_target_pairs={{0,1},{1,0},{2,3},{3,2},{4,5},{5,4},{6,7},{7,6}} | collective-permute-start | bytes 4423688 | tf_op jit(solution)/shard_map/cond/branch_0_fun/ppermute | solution.py:383
  277.8 76.1 %collective-permute-start.80 = (bf16[8,1152,128]{2,1,0:T(8,128)(2,1)}, bf16[8,1152,128]{2,1,0:T(8,128)(2,1)}, u32[]{:S(2)}, u32[]{:S(2)}) collective-permute-start(bf16[8,1152,128]{2,1,0:T(8,128)(2,1)} %collective-permute-done.1.refs_4_), channel_id=1, source_target_pairs={{0,1},{1,0},{2,3},{3,2},{4,5},{5,4},{6,7},{7,6}} | collective-permute-start | bytes 7077896 | tf_op jit(solution)/shard_map/cond/branch_0_fun/ppermute | solution.py:383
  340.4 44.6 %collective-permute-start.76 = (bf16[7,1152,128]{2,1,0:T(8,128)(2,1)}, bf16[7,1152,128]{2,1,0:T(8,128)(2,1)}, u32[]{:S(2)}, u32[]{:S(2)}) collective-permute-start(bf16[7,1152,128]{2,1,0:T(8,128)(2,1)} %collective-permute-done.27), channel_id=1, source_target_pairs={{4,6},{5,7},{6,4},{7,5},{0,1},{1,0},{2,3},{3,2}} | collective-permute-start | bytes 6193160 | tf_op jit(solution)/shard_map/cond/branch_0_fun/ppermute | solution.py:383
  344.2 40.8 %collective-permute-start.74 = (bf16[7,1152,128]{2,1,0:T(8,128)(2,1)}, bf16[7,1152,128]{2,1,0:T(8,128)(2,1)}, u32[]{:S(2)}, u32[]{:S(2)}) collective-permute-start(bf16[7,1152,128]{2,1,0:T(8,128)(2,1)} %collective-permute-done.25.refs_2_), channel_id=1, source_target_pairs={{0,1},{1,0},{2,3},{3,2},{4,5},{5,4},{6,7},{7,6}} | collective-permute-start | bytes 6193160 | tf_op jit(solution)/shard_map/cond/branch_0_fun/ppermute | solution.py:383
  349.3 37.2 %collective-permute-start.75 = (bf16[7,1152,128]{2,1,0:T(8,128)(2,1)}, bf16[7,1152,128]{2,1,0:T(8,128)(2,1)}, u32[]{:S(2)}, u32[]{:S(2)}) collective-permute-start(bf16[7,1152,128]{2,1,0:T(8,128)(2,1)} %collective-permute-done.26.refs_4_), channel_id=1, source_target_pairs={{0,1},{1,0},{2,3},{3,2},{4,5},{5,4},{6,7},{7,6}} | collective-permute-start | bytes 6193160 | tf_op jit(solution)/shard_map/cond/branch_0_fun/ppermute | solution.py:383
  353.9 38.5 %collective-permute-start.70 = (bf16[5,1152,128]{2,1,0:T(8,128)(2,1)}, bf16[5,1152,128]{2,1,0:T(8,128)(2,1)S(1)}, u32[]{:S(2)}, u32[]{:S(2)}) collective-permute-start(bf16[5,1152,128]{2,1,0:T(8,128)(2,1)} %copy-done.42), channel_id=1, source_target_pairs={{0,1},{1,0},{2,3},{3,2},{4,5},{5,4},{6,7},{7,6}} | collective-permute-start | bytes 4423688 | tf_op jit(solution)/shard_map/cond/branch_0_fun/ppermute | solution.py:383
  355.6 40.4 %collective-permute-start.28 = (bf16[7,1152,128]{2,1,0:T(8,128)(2,1)}, bf16[7,1152,128]{2,1,0:T(8,128)(2,1)}, u32[]{:S(2)}, u32[]{:S(2)}) collective-permute-start(bf16[7,1152,128]{2,1,0:T(8,128)(2,1)} %get-tuple-element.178), channel_id=1, source_target_pairs={{0,2},{1,3},{2,0},{3,1},{4,5},{5,4},{6,7},{7,6}} | collective-permute-start | bytes 6193160 | tf_op jit(solution)/shard_map/cond/branch_0_fun/ppermute | solution.py:383
  385.0 41.4 %collective-permute-start.29 = (bf16[7,1152,128]{2,1,0:T(8,128)(2,1)}, bf16[7,1152,128]{2,1,0:T(8,128)(2,1)}, u32[]{:S(2)}, u32[]{:S(2)}) collective-permute-start(bf16[7,1152,128]{2,1,0:T(8,128)(2,1)} %get-tuple-element.179), channel_id=1, source_target_pairs={{0,4},{1,5},{2,6},{3,7},{4,0},{5,1},{6,2},{7,3}} | collective-permute-start | bytes 6193160 | tf_op jit(solution)/shard_map/cond/branch_0_fun/ppermute | solution.py:383
  385.1 117.3 %collective-permute-start.30 = (bf16[7,1152,128]{2,1,0:T(8,128)(2,1)}, bf16[7,1152,128]{2,1,0:T(8,128)(2,1)}, u32[]{:S(2)}, u32[]{:S(2)}) collective-permute-start(bf16[7,1152,128]{2,1,0:T(8,128)(2,1)} %get-tuple-element.180), channel_id=1, source_target_pairs={{0,4},{1,5},{2,6},{3,7},{4,0},{5,1},{6,2},{7,3}} | collective-permute-start | bytes 6193160 | tf_op jit(solution)/shard_map/cond/branch_0_fun/ppermute | solution.py:383
  392.4 119.4 %collective-permute-start.6 = (bf16[5,1152,128]{2,1,0:T(8,128)(2,1)}, bf16[5,1152,128]{2,1,0:T(8,128)(2,1)}, u32[]{:S(2)}, u32[]{:S(2)}) collective-permute-start(bf16[5,1152,128]{2,1,0:T(8,128)(2,1)} %get-tuple-element.142), channel_id=1, source_target_pairs={{0,2},{1,3},{2,0},{3,1},{4,6},{5,7},{6,4},{7,5}} | collective-permute-start | bytes 4423688 | tf_op jit(solution)/shard_map/cond/branch_0_fun/ppermute | solution.py:383
  395.6 153.2 %collective-permute-start.64 = (bf16[7,1152,128]{2,1,0:T(8,128)(2,1)S(1)}, bf16[7,1152,128]{2,1,0:T(8,128)(2,1)}, u32[]{:S(2)}, u32[]{:S(2)}) collective-permute-start(bf16[7,1152,128]{2,1,0:T(8,128)(2,1)S(1)} %copy-done.18), channel_id=1, source_target_pairs={{0,1},{1,0},{2,3},{3,2},{4,5},{5,4},{6,7},{7,6}} | collective-permute-start | bytes 6193160 | tf_op jit(solution)/shard_map/cond/branch_0_fun/ppermute | solution.py:383
  396.7 135.4 %collective-permute-start.7 = (bf16[5,1152,128]{2,1,0:T(8,128)(2,1)}, bf16[5,1152,128]{2,1,0:T(8,128)(2,1)}, u32[]{:S(2)}, u32[]{:S(2)}) collective-permute-start(bf16[5,1152,128]{2,1,0:T(8,128)(2,1)} %get-tuple-element.143), channel_id=1, source_target_pairs={{0,4},{1,5},{4,0},{5,1},{6,2},{7,3}} | collective-permute-start | bytes 4423688 | tf_op jit(solution)/shard_map/cond/branch_0_fun/ppermute | solution.py:383
  426.5 106.4 %collective-permute-start.8 = (bf16[5,1152,128]{2,1,0:T(8,128)(2,1)}, bf16[5,1152,128]{2,1,0:T(8,128)(2,1)}, u32[]{:S(2)}, u32[]{:S(2)}) collective-permute-start(bf16[5,1152,128]{2,1,0:T(8,128)(2,1)} %get-tuple-element.144), channel_id=1, source_target_pairs={{0,6},{1,7},{4,2},{5,3},{6,0},{7,1}} | collective-permute-start | bytes 4423688 | tf_op jit(solution)/shard_map/cond/branch_0_fun/ppermute | solution.py:383
  502.3 40.6 %collective-permute-start.72 = (bf16[5,1152,128]{2,1,0:T(8,128)(2,1)}, bf16[5,1152,128]{2,1,0:T(8,128)(2,1)}, u32[]{:S(2)}, u32[]{:S(2)}) collective-permute-start(bf16[5,1152,128]{2,1,0:T(8,128)(2,1)} %collective-permute-done.5.refs_6_), channel_id=1, source_target_pairs={{0,1},{1,0},{2,3},{3,2},{4,5},{5,4},{6,7},{7,6}} | collective-permute-start | bytes 4423688 | tf_op jit(solution)/shard_map/cond/branch_0_fun/ppermute | solution.py:383
  511.9 37.0 %collective-permute-start.60 = (bf16[5,1152,128]{2,1,0:T(8,128)(2,1)}, bf16[5,1152,128]{2,1,0:T(8,128)(2,1)}, u32[]{:S(2)}, u32[]{:S(2)}) collective-permute-start(bf16[5,1152,128]{2,1,0:T(8,128)(2,1)} %get-tuple-element.207.refs_0_), channel_id=1, source_target_pairs={{0,1},{1,0},{2,3},{3,2},{4,5},{5,4},{6,7},{7,6}} | collective-permute-start | bytes 4423688 | tf_op jit(solution)/shard_map/cond/branch_0_fun/ppermute | solution.py:383
  532.0 34.5 %collective-permute-start.31 = (bf16[6,1152,128]{2,1,0:T(8,128)(2,1)}, bf16[6,1152,128]{2,1,0:T(8,128)(2,1)}, u32[]{:S(2)}, u32[]{:S(2)}) collective-permute-start(bf16[6,1152,128]{2,1,0:T(8,128)(2,1)} %get-tuple-element.181), channel_id=1, source_target_pairs={{0,2},{1,3},{2,0},{3,1},{4,6},{5,7},{6,4},{7,5}} | collective-permute-start | bytes 5308424 | tf_op jit(solution)/shard_map/cond/branch_0_fun/ppermute | solution.py:383
  532.9 42.6 %collective-permute-start.32 = (bf16[6,1152,128]{2,1,0:T(8,128)(2,1)}, bf16[6,1152,128]{2,1,0:T(8,128)(2,1)}, u32[]{:S(2)}, u32[]{:S(2)}) collective-permute-start(bf16[6,1152,128]{2,1,0:T(8,128)(2,1)} %get-tuple-element.182), channel_id=1, source_target_pairs={{0,4},{1,5},{2,6},{4,0},{5,1},{6,2},{7,3}} | collective-permute-start | bytes 5308424 | tf_op jit(solution)/shard_map/cond/branch_0_fun/ppermute | solution.py:383
  552.0 104.9 %collective-permute-start.77 = (bf16[7,1152,128]{2,1,0:T(8,128)(2,1)}, bf16[7,1152,128]{2,1,0:T(8,128)(2,1)S(1)}, u32[]{:S(2)}, u32[]{:S(2)}) collective-permute-start(bf16[7,1152,128]{2,1,0:T(8,128)(2,1)} %collective-permute-done.76.refs_6_), channel_id=1, source_target_pairs={{0,1},{1,0},{2,3},{3,2},{4,5},{5,4},{6,7},{7,6}} | collective-permute-start | bytes 6193160 | tf_op jit(solution)/shard_map/cond/branch_0_fun/ppermute | solution.py:383
  554.1 103.2 %collective-permute-start.67 = (bf16[7,1152,128]{2,1,0:T(8,128)(2,1)}, bf16[7,1152,128]{2,1,0:T(8,128)(2,1)S(1)}, u32[]{:S(2)}, u32[]{:S(2)}) collective-permute-start(bf16[7,1152,128]{2,1,0:T(8,128)(2,1)} %collective-permute-done.30), channel_id=1, source_target_pairs={{4,6},{5,7},{6,4},{7,5},{0,1},{1,0},{2,3},{3,2}} | collective-permute-start | bytes 6193160 | tf_op jit(solution)/shard_map/cond/branch_0_fun/ppermute | solution.py:383
  563.1 96.1 %collective-permute-start.65 = (bf16[7,1152,128]{2,1,0:T(8,128)(2,1)}, bf16[7,1152,128]{2,1,0:T(8,128)(2,1)}, u32[]{:S(2)}, u32[]{:S(2)}) collective-permute-start(bf16[7,1152,128]{2,1,0:T(8,128)(2,1)} %collective-permute-done.28.refs_2_), channel_id=1, source_target_pairs={{0,1},{1,0},{2,3},{3,2},{4,5},{5,4},{6,7},{7,6}} | collective-permute-start | bytes 6193160 | tf_op jit(solution)/shard_map/cond/branch_0_fun/ppermute | solution.py:383
  566.6 80.2 %collective-permute-start.33 = (bf16[6,1152,128]{2,1,0:T(8,128)(2,1)}, bf16[6,1152,128]{2,1,0:T(8,128)(2,1)S(1)}, u32[]{:S(2)}, u32[]{:S(2)}) collective-permute-start(bf16[6,1152,128]{2,1,0:T(8,128)(2,1)} %get-tuple-element.183), channel_id=1, source_target_pairs={{0,6},{1,7},{2,4},{4,2},{5,3},{6,0},{7,1}} | collective-permute-start | bytes 5308424 | tf_op jit(solution)/shard_map/cond/branch_0_fun/ppermute | solution.py:383
  575.5 74.3 %collective-permute-start.56 = (bf16[6,1152,128]{2,1,0:T(8,128)(2,1)}, bf16[6,1152,128]{2,1,0:T(8,128)(2,1)S(1)}, u32[]{:S(2)}, u32[]{:S(2)}) collective-permute-start(bf16[6,1152,128]{2,1,0:T(8,128)(2,1)} %get-tuple-element.203.refs_0_), channel_id=1, source_target_pairs={{0,1},{1,0},{2,3},{3,2},{4,5},{5,4},{6,7},{7,6}} | collective-permute-start | bytes 5308424 | tf_op jit(solution)/shard_map/cond/branch_0_fun/ppermute | solution.py:383
  646.8 104.5 %collective-permute-start.10 = (bf16[8,1152,128]{2,1,0:T(8,128)(2,1)}, bf16[8,1152,128]{2,1,0:T(8,128)(2,1)}, u32[]{:S(2)}, u32[]{:S(2)}) collective-permute-start(bf16[8,1152,128]{2,1,0:T(8,128)(2,1)} %get-tuple-element.146), channel_id=1, source_target_pairs={{0,4},{1,5},{2,6},{3,7},{4,0},{5,1},{6,2},{7,3}} | collective-permute-start | bytes 7077896 | tf_op jit(solution)/shard_map/cond/branch_0_fun/ppermute | solution.py:383
  657.0 98.6 %collective-permute-start.11 = (bf16[8,1152,128]{2,1,0:T(8,128)(2,1)}, bf16[8,1152,128]{2,1,0:T(8,128)(2,1)}, u32[]{:S(2)}, u32[]{:S(2)}) collective-permute-start(bf16[8,1152,128]{2,1,0:T(8,128)(2,1)} %get-tuple-element.147), channel_id=1, source_target_pairs={{0,6},{1,7},{2,4},{3,5},{4,2},{5,3},{6,0},{7,1}} | collective-permute-start | bytes 7077896 | tf_op jit(solution)/shard_map/cond/branch_0_fun/ppermute | solution.py:383
  658.3 101.9 %collective-permute-start.9 = (bf16[8,1152,128]{2,1,0:T(8,128)(2,1)}, bf16[8,1152,128]{2,1,0:T(8,128)(2,1)}, u32[]{:S(2)}, u32[]{:S(2)}) collective-permute-start(bf16[8,1152,128]{2,1,0:T(8,128)(2,1)} %get-tuple-element.145), channel_id=1, source_target_pairs={{0,2},{1,3},{2,0},{3,1},{4,6},{5,7},{6,4},{7,5}} | collective-permute-start | bytes 7077896 | tf_op jit(solution)/shard_map/cond/branch_0_fun/ppermute | solution.py:383
  659.2 102.4 %collective-permute-start.52 = (bf16[8,1152,128]{2,1,0:T(8,128)(2,1)}, bf16[8,1152,128]{2,1,0:T(8,128)(2,1)}, u32[]{:S(2)}, u32[]{:S(2)}) collective-permute-start(bf16[8,1152,128]{2,1,0:T(8,128)(2,1)} %get-tuple-element.199.refs_0_), channel_id=1, source_target_pairs={{0,1},{1,0},{2,3},{3,2},{4,5},{5,4},{6,7},{7,6}} | collective-permute-start | bytes 7077896 | tf_op jit(solution)/shard_map/cond/branch_0_fun/ppermute | solution.py:383
  664.2 146.5 %collective-permute-start.34 = (bf16[8,1152,128]{2,1,0:T(8,128)(2,1)}, bf16[8,1152,128]{2,1,0:T(8,128)(2,1)}, u32[]{:S(2)}, u32[]{:S(2)}) collective-permute-start(bf16[8,1152,128]{2,1,0:T(8,128)(2,1)} %get-tuple-element.184), channel_id=1, source_target_pairs={{0,2},{1,3},{2,0},{3,1},{4,6},{5,7},{6,4},{7,5}} | collective-permute-start | bytes 7077896 | tf_op jit(solution)/shard_map/cond/branch_0_fun/ppermute | solution.py:383
  751.3 36.0 %collective-permute-start.68 = (bf16[7,1152,128]{2,1,0:T(8,128)(2,1)}, bf16[7,1152,128]{2,1,0:T(8,128)(2,1)}, u32[]{:S(2)}, u32[]{:S(2)}) collective-permute-start(bf16[7,1152,128]{2,1,0:T(8,128)(2,1)} %copy-done.29), channel_id=1, source_target_pairs={{0,1},{1,0},{2,3},{3,2},{4,5},{5,4},{6,7},{7,6}} | collective-permute-start | bytes 6193160 | tf_op jit(solution)/shard_map/cond/branch_0_fun/ppermute | solution.py:383
  762.2 104.3 %collective-permute-start.35 = (bf16[8,1152,128]{2,1,0:T(8,128)(2,1)}, bf16[8,1152,128]{2,1,0:T(8,128)(2,1)}, u32[]{:S(2)}, u32[]{:S(2)}) collective-permute-start(bf16[8,1152,128]{2,1,0:T(8,128)(2,1)} %get-tuple-element.185), channel_id=1, source_target_pairs={{0,4},{1,5},{2,6},{3,7},{4,0},{5,1},{6,2},{7,3}} | collective-permute-start | bytes 7077896 | tf_op jit(solution)/shard_map/cond/branch_0_fun/ppermute | solution.py:383
  769.1 98.4 %collective-permute-start.36 = (bf16[8,1152,128]{2,1,0:T(8,128)(2,1)}, bf16[8,1152,128]{2,1,0:T(8,128)(2,1)S(1)}, u32[]{:S(2)}, u32[]{:S(2)}) collective-permute-start(bf16[8,1152,128]{2,1,0:T(8,128)(2,1)} %get-tuple-element.186), channel_id=1, source_target_pairs={{0,6},{1,7},{2,4},{3,5},{4,2},{5,3},{6,0},{7,1}} | collective-permute-start | bytes 7077896 | tf_op jit(solution)/shard_map/cond/branch_0_fun/ppermute | solution.py:383
  786.3 82.1 %collective-permute-start.48 = (bf16[8,1152,128]{2,1,0:T(8,128)(2,1)S(1)}, bf16[8,1152,128]{2,1,0:T(8,128)(2,1)S(1)}, u32[]{:S(2)}, u32[]{:S(2)}) collective-permute-start(bf16[8,1152,128]{2,1,0:T(8,128)(2,1)S(1)} %copy-done.17), channel_id=1, source_target_pairs={{0,1},{1,0},{2,3},{3,2},{4,5},{5,4},{6,7},{7,6}} | collective-permute-start | bytes 7077896 | tf_op jit(solution)/shard_map/cond/branch_0_fun/ppermute | solution.py:383
  787.3 83.1 %collective-permute-start.53 = (bf16[8,1152,128]{2,1,0:T(8,128)(2,1)}, bf16[8,1152,128]{2,1,0:T(8,128)(2,1)S(1)}, u32[]{:S(2)}, u32[]{:S(2)}) collective-permute-start(bf16[8,1152,128]{2,1,0:T(8,128)(2,1)} %collective-permute-done.9.refs_2_), channel_id=1, source_target_pairs={{0,1},{1,0},{2,3},{3,2},{4,5},{5,4},{6,7},{7,6}} | collective-permute-start | bytes 7077896 | tf_op jit(solution)/shard_map/cond/branch_0_fun/ppermute | solution.py:383
  810.7 63.2 %collective-permute-start.54 = (bf16[8,1152,128]{2,1,0:T(8,128)(2,1)}, bf16[8,1152,128]{2,1,0:T(8,128)(2,1)}, u32[]{:S(2)}, u32[]{:S(2)}) collective-permute-start(bf16[8,1152,128]{2,1,0:T(8,128)(2,1)} %collective-permute-done.10.refs_4_), channel_id=1, source_target_pairs={{0,1},{1,0},{2,3},{3,2},{4,5},{5,4},{6,7},{7,6}} | collective-permute-start | bytes 7077896 | tf_op jit(solution)/shard_map/cond/branch_0_fun/ppermute | solution.py:383
  867.5 53.1 %collective-permute-start.12 = (bf16[8,1152,128]{2,1,0:T(8,128)(2,1)}, bf16[8,1152,128]{2,1,0:T(8,128)(2,1)}, u32[]{:S(2)}, u32[]{:S(2)}) collective-permute-start(bf16[8,1152,128]{2,1,0:T(8,128)(2,1)} %get-tuple-element.148), channel_id=1, source_target_pairs={{0,2},{1,3},{2,0},{3,1},{4,6},{5,7},{6,4},{7,5}} | collective-permute-start | bytes 7077896 | tf_op jit(solution)/shard_map/cond/branch_0_fun/ppermute | solution.py:383
  868.9 102.9 %collective-permute-start.13 = (bf16[8,1152,128]{2,1,0:T(8,128)(2,1)}, bf16[8,1152,128]{2,1,0:T(8,128)(2,1)}, u32[]{:S(2)}, u32[]{:S(2)}) collective-permute-start(bf16[8,1152,128]{2,1,0:T(8,128)(2,1)} %get-tuple-element.149), channel_id=1, source_target_pairs={{0,4},{1,5},{2,6},{3,7},{4,0},{5,1},{6,2},{7,3}} | collective-permute-start | bytes 7077896 | tf_op jit(solution)/shard_map/cond/branch_0_fun/ppermute | solution.py:383
  871.8 101.4 %collective-permute-start.14 = (bf16[8,1152,128]{2,1,0:T(8,128)(2,1)}, bf16[8,1152,128]{2,1,0:T(8,128)(2,1)}, u32[]{:S(2)}, u32[]{:S(2)}) collective-permute-start(bf16[8,1152,128]{2,1,0:T(8,128)(2,1)} %get-tuple-element.150), channel_id=1, source_target_pairs={{0,6},{1,7},{2,4},{3,5},{4,2},{5,3},{6,0},{7,1}} | collective-permute-start | bytes 7077896 | tf_op jit(solution)/shard_map/cond/branch_0_fun/ppermute | solution.py:383
  873.9 101.0 %collective-permute-start.44 = (bf16[8,1152,128]{2,1,0:T(8,128)(2,1)}, bf16[8,1152,128]{2,1,0:T(8,128)(2,1)}, u32[]{:S(2)}, u32[]{:S(2)}) collective-permute-start(bf16[8,1152,128]{2,1,0:T(8,128)(2,1)} %get-tuple-element.191.refs_0_), channel_id=1, source_target_pairs={{0,1},{1,0},{2,3},{3,2},{4,5},{5,4},{6,7},{7,6}} | collective-permute-start | bytes 7077896 | tf_op jit(solution)/shard_map/cond/branch_0_fun/ppermute | solution.py:383
  878.9 100.6 %collective-permute-start.38 = (bf16[4,1152,128]{2,1,0:T(8,128)(2,1)}, bf16[4,1152,128]{2,1,0:T(8,128)(2,1)}, u32[]{:S(2)}, u32[]{:S(2)}) collective-permute-start(bf16[4,1152,128]{2,1,0:T(8,128)(2,1)} %get-tuple-element.188), channel_id=1, source_target_pairs={{0,2},{1,3},{2,0},{3,1},{4,5},{5,4},{6,7},{7,6}} | collective-permute-start | bytes 3538952 | tf_op jit(solution)/shard_map/cond/branch_0_fun/ppermute | solution.py:383
  920.6 78.1 %collective-permute-start.40 = (bf16[4,1152,128]{2,1,0:T(8,128)(2,1)}, bf16[4,1152,128]{2,1,0:T(8,128)(2,1)}, u32[]{:S(2)}, u32[]{:S(2)}) collective-permute-start(bf16[4,1152,128]{2,1,0:T(8,128)(2,1)} %get-tuple-element.189), channel_id=1, source_target_pairs={{0,4},{1,5},{2,6},{3,7},{4,0},{5,1},{6,2},{7,3}} | collective-permute-start | bytes 3538952 | tf_op jit(solution)/shard_map/cond/branch_0_fun/ppermute | solution.py:383
  971.9 51.1 %collective-permute-start.42 = (bf16[4,1152,128]{2,1,0:T(8,128)(2,1)}, bf16[4,1152,128]{2,1,0:T(8,128)(2,1)}, u32[]{:S(2)}, u32[]{:S(2)}) collective-permute-start(bf16[4,1152,128]{2,1,0:T(8,128)(2,1)} %get-tuple-element.190), channel_id=1, source_target_pairs={{0,6},{1,7},{2,4},{3,5}} | collective-permute-start | bytes 3538952 | tf_op jit(solution)/shard_map/cond/branch_0_fun/ppermute | solution.py:383
  973.2 51.2 %collective-permute-start.37 = (bf16[4,1152,128]{2,1,0:T(8,128)(2,1)}, bf16[4,1152,128]{2,1,0:T(8,128)(2,1)}, u32[]{:S(2)}, u32[]{:S(2)}) collective-permute-start(bf16[4,1152,128]{2,1,0:T(8,128)(2,1)} %get-tuple-element.187.refs_0_), channel_id=1, source_target_pairs={{0,1},{1,0},{2,3},{3,2},{4,5},{5,4},{6,7},{7,6}} | collective-permute-start | bytes 3538952 | tf_op jit(solution)/shard_map/cond/branch_0_fun/ppermute | solution.py:383
  974.8 79.0 %collective-permute-start.49 = (bf16[8,1152,128]{2,1,0:T(8,128)(2,1)}, bf16[8,1152,128]{2,1,0:T(8,128)(2,1)}, u32[]{:S(2)}, u32[]{:S(2)}) collective-permute-start(bf16[8,1152,128]{2,1,0:T(8,128)(2,1)} %collective-permute-done.34.refs_2_), channel_id=1, source_target_pairs={{0,1},{1,0},{2,3},{3,2},{4,5},{5,4},{6,7},{7,6}} | collective-permute-start | bytes 7077896 | tf_op jit(solution)/shard_map/cond/branch_0_fun/ppermute | solution.py:383
  979.5 44.9 %collective-permute-start.16 = (bf16[2,1152,128]{2,1,0:T(8,128)(2,1)}, bf16[2,1152,128]{2,1,0:T(8,128)(2,1)}, u32[]{:S(2)}, u32[]{:S(2)}) collective-permute-start(bf16[2,1152,128]{2,1,0:T(8,128)(2,1)} %get-tuple-element.152), channel_id=1, source_target_pairs={{0,2},{1,3},{2,0},{3,1},{4,5},{5,4},{6,7},{7,6}} | collective-permute-start | bytes 1769480 | tf_op jit(solution)/shard_map/cond/branch_0_fun/ppermute | solution.py:383
  998.7 33.8 %collective-permute-start.18 = (bf16[2,1152,128]{2,1,0:T(8,128)(2,1)}, bf16[2,1152,128]{2,1,0:T(8,128)(2,1)}, u32[]{:S(2)}, u32[]{:S(2)}) collective-permute-start(bf16[2,1152,128]{2,1,0:T(8,128)(2,1)} %get-tuple-element.153), channel_id=1, source_target_pairs={{0,4},{1,5},{2,6},{3,7},{4,0},{5,1},{6,2},{7,3}} | collective-permute-start | bytes 1769480 | tf_op jit(solution)/shard_map/cond/branch_0_fun/ppermute | solution.py:383
  1024.4 32.3 %collective-permute-start.50 = (bf16[8,1152,128]{2,1,0:T(8,128)(2,1)}, bf16[8,1152,128]{2,1,0:T(8,128)(2,1)}, u32[]{:S(2)}, u32[]{:S(2)}) collective-permute-start(bf16[8,1152,128]{2,1,0:T(8,128)(2,1)} %collective-permute-done.35.refs_4_), channel_id=1, source_target_pairs={{0,1},{1,0},{2,3},{3,2},{4,5},{5,4},{6,7},{7,6}} | collective-permute-start | bytes 7077896 | tf_op jit(solution)/shard_map/cond/branch_0_fun/ppermute | solution.py:383
  1056.6 216.2 %collective-permute-start.43 = (bf16[4,1152,128]{2,1,0:T(8,128)(2,1)}, bf16[4,1152,128]{2,1,0:T(8,128)(2,1)}, u32[]{:S(2)}, u32[]{:S(2)}) collective-permute-start(bf16[4,1152,128]{2,1,0:T(8,128)(2,1)} %collective-permute-done.42.refs_6_), channel_id=1, source_target_pairs={{0,1},{1,0},{2,3},{3,2},{4,5},{5,4},{6,7},{7,6}} | collective-permute-start | bytes 3538952 | tf_op jit(solution)/shard_map/cond/branch_0_fun/ppermute | solution.py:383
  1059.4 220.7 %collective-permute-start.15 = (bf16[2,1152,128]{2,1,0:T(8,128)(2,1)}, bf16[2,1152,128]{2,1,0:T(8,128)(2,1)}, u32[]{:S(2)}, u32[]{:S(2)}) collective-permute-start(bf16[2,1152,128]{2,1,0:T(8,128)(2,1)} %get-tuple-element.151.refs_0_), channel_id=1, source_target_pairs={{0,1},{1,0},{2,3},{3,2},{4,5},{5,4},{6,7},{7,6}} | collective-permute-start | bytes 1769480 | tf_op jit(solution)/shard_map/cond/branch_0_fun/ppermute | solution.py:383
  1061.2 218.9 %collective-permute-start.17 = (bf16[2,1152,128]{2,1,0:T(8,128)(2,1)}, bf16[2,1152,128]{2,1,0:T(8,128)(2,1)}, u32[]{:S(2)}, u32[]{:S(2)}) collective-permute-start(bf16[2,1152,128]{2,1,0:T(8,128)(2,1)} %collective-permute-done.16.refs_2_), channel_id=1, source_target_pairs={{0,1},{1,0},{2,3},{3,2},{4,5},{5,4},{6,7},{7,6}} | collective-permute-start | bytes 1769480 | tf_op jit(solution)/shard_map/cond/branch_0_fun/ppermute | solution.py:383
  1064.5 215.6 %collective-permute-start.19 = (bf16[2,1152,128]{2,1,0:T(8,128)(2,1)}, bf16[2,1152,128]{2,1,0:T(8,128)(2,1)}, u32[]{:S(2)}, u32[]{:S(2)}) collective-permute-start(bf16[2,1152,128]{2,1,0:T(8,128)(2,1)} %collective-permute-done.18.refs_4_), channel_id=1, source_target_pairs={{0,1},{1,0},{2,3},{3,2},{4,5},{5,4},{6,7},{7,6}} | collective-permute-start | bytes 1769480 | tf_op jit(solution)/shard_map/cond/branch_0_fun/ppermute | solution.py:383
  1067.9 212.2 %collective-permute-start.21 = (bf16[2,1152,128]{2,1,0:T(8,128)(2,1)}, bf16[2,1152,128]{2,1,0:T(8,128)(2,1)}, u32[]{:S(2)}, u32[]{:S(2)}) collective-permute-start(bf16[2,1152,128]{2,1,0:T(8,128)(2,1)} %collective-permute-done.20.refs_6_), channel_id=1, source_target_pairs={{0,1},{1,0},{2,3},{3,2},{4,5},{5,4},{6,7},{7,6}} | collective-permute-start | bytes 1769480 | tf_op jit(solution)/shard_map/cond/branch_0_fun/ppermute | solution.py:383
  (52 other events, 2257.9 us)
where the time goes:
time: 1310 us; the launch traced here: 1300 us
  waiting for transfers between devices  782 us (60%)
  Pallas kernels  292 us (22%)
  starting transfers between devices  188 us (14%)
  local copies, waits for them, and re-layouts  13.9 us (1%)
    ppermute x86, waiting for transfers between devices, send(): return lax.ppermute(x, 'x', pairs)  782 us
    pallas_call x12, Pallas kernels, attend(): pl.pallas_call(kernel, in_specs=in_specs, out_specs=out_specs, out_shape=...  205 us
    ppermute x86, starting transfers between devices, send(): return lax.ppermute(x, 'x', pairs)  188 us
    pallas_call x12, Pallas kernels, norm_pack(): pl.pallas_call(kernel, grid_spec=grid_spec, out_shape=[jax.ShapeDtypeStru...  73.3 us
  transfers between devices with their start and end apart: 86, of which 32 were waited for; matrix products, arithmetic and copies ran while one was open for 0% of the time, Pallas kernels for 21%

commit v1 on v0

--- a/solution.py
+++ b/solution.py
@@ -1,5 +1,3 @@
-import functools
-
 import jax
 import jax.numpy as jnp
 import numpy as np
@@ -72,21 +70,20 @@
     return width, "direct", UP, ALL, UP
 
 
-PLANS = (
-    Plan([direct(4), direct(8), relay(7), no_chip1(5), relay(7), no_chip1(5), no_3(6)] + [direct(8)] * 3 + [end(4), end(2)]),
-    Plan([direct(4), direct(8), relay(6), no_chip1(6), relay(4), no_3(6)] + [direct(8)] * 4 + [end(4), end(2)]),
-    Plan([direct(4)] + [direct(8)] * 8 + [direct(4)]),
+PLAN = Plan(
+    [direct(2), direct(4), direct(6), relay(6), no_chip1(6), relay(4), no_3(6)] + [direct(8)] * 4 + [end(4), end(2)]
 )
-
-
-def norm_pack(width, start, tabs, c_raw, k_t, gain, cos_t, sin_t, after):
+EXTRA = 4
+
+
+def norm_pack(width, start, stride, tabs, c_raw, k_t, gain, cos_t, sin_t, after):
     steps = CHIPS * width
 
     def kernel(req_ref, unit_ref, ok_ref, c_ref, k_ref, g_ref, cos_ref, sin_ref, *refs):
         outs, (buf, sem) = refs[len(after) : len(after) + CHIPS], refs[-2:]
         n = pl.program_id(0)
         q, j = n // width, n % width
-        ok_at = lambda m: ok_ref[m // width * SLOTS + start + m % width] > 0
+        ok_at = lambda m: ok_ref[m // width * stride + start + m % width] > 0
         drain = lambda m: pltpu.make_async_copy(buf.at[m % 2], outs[0].at[0], sem.at[m % 2]).wait()
         slot = n % 2
 
@@ -126,7 +123,7 @@
                 drain(n)
 
     def at(n):
-        return n // width * SLOTS + start + n % width
+        return n // width * stride + start + n % width
 
     grid_spec = pltpu.PrefetchScalarGridSpec(
         num_scalar_prefetch=3,
@@ -151,19 +148,21 @@
     )(*tabs, c_raw, k_t, gain, cos_t, sin_t, *after)
 
 
-def attend(chunk, start, first, last, counts, codes, parts, q_lat, q_rope_t, caches, state):
+def attend(chunk, start, first, counts, codes, parts, q_lat, q_rope_t, caches, state):
+    total = len(parts)
+
     def kernel(count_ref, code_ref, *refs):
-        part_refs, (qa_ref, qr_ref) = refs[:N], refs[N : N + 2]
-        old_ref = None if first else refs[N + 4]
-        outs = refs[N + (4 if first else 5) :]
+        part_refs, (qa_ref, qr_ref) = refs[:total], refs[total : total + 2]
+        old_ref = None if first else refs[total + 4]
+        outs = refs[total + (4 if first else 5) :]
         c_out, k_out, st_ref = outs[:3]
         buf, c_buf, k_buf, in_sem, c_sem, k_sem = outs[-6:]
         steps = count_ref[chunk]
 
         def fetch(n):
-            code = code_ref[N * start + n]
+            code = code_ref[start + n]
             part, place = code // 2**22, code // 2**18 % 16
-            for k in range(N):
+            for k in range(total):
 
                 @pl.when(part == k)
                 def _(k=k):
@@ -174,7 +173,7 @@
             pltpu.make_async_copy(k_buf.at[slot], k_out.at[0, :, pl.ds(0, UNIT)], k_sem.at[slot]).wait()
 
         def step(n, _):
-            code = code_ref[N * start + n]
+            code = code_ref[start + n]
             left, r = code // 2**9 % 2**9, code // 2**5 % 16
             at = pl.ds(pl.multiple_of(code % 2**5 * UNIT, UNIT), UNIT)
             slot = n % 2
@@ -242,18 +241,9 @@
         def _():
             drain((steps + 1) % 2)
 
-        if last:
-            o_ref = outs[3]
-
-            def finish(r, _):
-                o_ref[r] = (st_ref[r, :, :RANK] / st_ref[r, :, RANK : RANK + 1]).astype(jnp.bfloat16)
-                return 0
-
-            lax.fori_loop(0, REQ, finish, 0)
-
     smem, vmem, anywhere = (pl.BlockSpec(memory_space=m) for m in (pltpu.SMEM, pltpu.VMEM, pl.ANY))
     state_shape = (REQ, HEADS, RANK + 256)
-    in_specs = [smem] * 2 + [anywhere] * N + [vmem] * 2 + [anywhere] * 2
+    in_specs = [smem] * 2 + [anywhere] * total + [vmem] * 2 + [anywhere] * 2
     operands = [counts, codes, *parts, q_lat, q_rope_t]
     aliases = {len(operands): 0, len(operands) + 1: 1}
     operands += list(caches)
@@ -262,9 +252,6 @@
         operands.append(state)
     out_specs = [anywhere, anywhere, vmem]
     out_shape = [jax.ShapeDtypeStruct(c.shape, c.dtype) for c in caches] + [jax.ShapeDtypeStruct(state_shape, jnp.float32)]
-    if last:
-        out_specs.append(vmem)
-        out_shape.append(jax.ShapeDtypeStruct((REQ, HEADS, RANK), jnp.bfloat16))
     return pl.pallas_call(
         kernel,
         in_specs=in_specs,
@@ -336,100 +323,128 @@
     return place // (2 * PER), place // 2 % PER, place % 2
 
 
-def run_plan(plan, me, left, own_lens, c_raw, k_t, gain, cos_t, sin_t, q_lat, q_rope_t):
-    chip = me // 2
+def pack_tables(me, left, slot):
     have = left > 0
-    rank = jnp.cumsum(have.astype(jnp.int32), axis=-1)
     places = jnp.arange(SLOTS, dtype=jnp.int32)
-
-    chips = chip ^ jnp.arange(CHIPS)
-    mine = rank[me][chips]
-    slot = jnp.asarray(plan.slot)[me]
-    place = jnp.sum((mine[:, None, :] <= slot[:, :, None]).astype(jnp.int32), axis=-1)
-    final = jnp.max(jnp.where(have[me][chips], places, 0), axis=-1, keepdims=True)
-    held = jnp.minimum(place, final)
-    req, unit, core = split_place(held)
-    pack_tabs = [
-        ((2 * chips[:, None] + core) * REQ + req).reshape(-1),
-        unit.reshape(-1),
-        (place < SLOTS).astype(jnp.int32).reshape(-1),
-    ]
-
+    chips = me // 2 ^ jnp.arange(CHIPS)
+    mine = have[me][chips]
+    rank = jnp.sum((mine[:, None, :] & (places[None, :] <= places[:, None])).astype(jnp.int32), axis=-1)
+    place = jnp.sum((rank[:, None, :] <= slot[:, :, None]).astype(jnp.int32), axis=-1)
+    final = jnp.max(jnp.where(mine, places, 0), axis=-1, keepdims=True)
+    req, unit, core = split_place(jnp.minimum(place, final))
+    req = (2 * chips[:, None] + core) * REQ + req
+    return [req.reshape(-1), unit.reshape(-1), (place < SLOTS).astype(jnp.int32).reshape(-1)]
+
+
+def attend_tables(me, left, slot, widths, runs):
+    places = jnp.arange(SLOTS, dtype=jnp.int32)
     part = jnp.arange(N)
     source = me ^ part
-    theirs = rank[source, chip]
-    slot = jnp.asarray(plan.slot)[source, part // 2]
-    place = jnp.sum((theirs[:, None, :] <= slot[:, :, None]).astype(jnp.int32), axis=-1)
+    theirs = left[source, me // 2]
+    rank = jnp.sum(((theirs > 0)[:, None, :] & (places[None, :] <= places[:, None])).astype(jnp.int32), axis=-1)
+    place = jnp.sum((rank[:, None, :] <= slot[:, :, None]).astype(jnp.int32), axis=-1)
     req, unit, core = split_place(place)
-    rows = jnp.sum(jnp.where(place[:, :, None] == places, left[source, chip][:, None, :], 0), axis=-1)
+    rows = jnp.sum(jnp.where(place[:, :, None] == places, theirs[:, None, :], 0), axis=-1)
     rows = jnp.where(core == me % 2, jnp.minimum(rows, UNIT), 0)
+    starts = np.cumsum([0] + list(widths))[:-1]
+    inside = np.concatenate([np.arange(w) for w in widths])
+    depth = np.concatenate([np.full(w, i) for run in runs for i, w in enumerate(widths[c] for c in run)])
     code = part[:, None] * 2**22 + rows * 2**9 + req * 2**5 + source[:, None] * PER + unit
-    inside = np.concatenate([np.arange(c[0]) for c in plan.chunks]).astype(np.int32)
-    code = jnp.where(rows > 0, code + jnp.asarray(inside) * 2**18, 0)
-    code = jnp.concatenate([code[:, s : s + c[0]].reshape(-1) for c, s in zip(plan.chunks, plan.starts)])
-    chunk_of = np.repeat(np.arange(len(plan.chunks)), [N * c[0] for c in plan.chunks])
-    heads = (N * plan.starts)[chunk_of].astype(np.int32)
-    same = jnp.asarray(chunk_of.astype(np.int32))[:, None] == jnp.asarray(chunk_of.astype(np.int32))[None, :]
-    number = jnp.arange(N * SLOTS, dtype=jnp.int32)
+    code = jnp.where(rows > 0, code + jnp.asarray((inside * 2**18 + depth * N * 2**22).astype(np.int32)), 0)
+    code = jnp.concatenate([code[:, s : s + w].reshape(-1) for w, s in zip(widths, starts)])
+    sizes = [N * sum(widths[c] for c in run) for run in runs]
+    first = np.cumsum([0] + sizes)[:-1]
+    run_of = np.repeat(np.arange(len(runs)), sizes).astype(np.int32)
+    same = jnp.asarray(run_of)[:, None] == jnp.asarray(run_of)[None, :]
+    number = jnp.arange(len(run_of), dtype=jnp.int32)
     before = jnp.sum((same & (number[None, :] < number[:, None]) & (code > 0)[None, :]).astype(jnp.int32), axis=-1)
-    goes_to = jnp.where(code > 0, jnp.asarray(heads) + before, -1)
+    goes_to = jnp.where(code > 0, jnp.asarray(first[run_of].astype(np.int32)) + before, -1)
     codes = jnp.sum(jnp.where(goes_to[None, :] == number[:, None], code[None, :], 0), axis=-1)
-    in_chunk = jnp.asarray(chunk_of.astype(np.int32))[None, :] == jnp.arange(len(plan.chunks), dtype=jnp.int32)[:, None]
-    counts = jnp.sum((in_chunk & (code > 0)[None, :]).astype(jnp.int32), axis=-1)
-
-    pairs = lambda sources, hop: [(s, s ^ hop) for s in sources]
-
-    def send(x, pairs):
-        return lax.ppermute(x, "x", pairs)
-
+    in_run = jnp.asarray(run_of)[None, :] == jnp.arange(len(runs), dtype=jnp.int32)[:, None]
+    return codes, jnp.sum((in_run & (code > 0)[None, :]).astype(jnp.int32), axis=-1), first
+
+
+def pairs(sources, hop):
+    return [(s, s ^ hop) for s in sources]
+
+
+def send(x, pairs):
+    return lax.ppermute(x, "x", pairs)
+
+
+def runs_of(count):
+    return [(c,) for c in range(count - 2)] + [(count - 2, count - 1)]
+
+
+def run_plan(me, left, own_lens, weights, q_lat, q_rope_t):
+    plan = PLAN
+    widths = [chunk[0] for chunk in plan.chunks]
+    count = len(widths)
+    runs = runs_of(count)
+    pack_tabs = pack_tables(me, left, jnp.asarray(plan.slot)[me])
+    part = jnp.arange(N)
+    codes, counts, first = attend_tables(me, left, jnp.asarray(plan.slot)[me ^ part, part // 2], widths, runs)
     caches = blank_caches(own_lens)
-    state = None
     landed, owns, twins = [], [], []
-    count = len(plan.chunks)
-
     after = []
     for c, (width, kind, along, across, diagonal) in enumerate(plan.chunks):
-        staged = norm_pack(width, int(plan.starts[c]), pack_tabs, c_raw, k_t, gain, cos_t, sin_t, after)
+        staged = norm_pack(width, int(plan.starts[c]), SLOTS, pack_tabs, *weights, after)
         after = [staged[0]]
         sends = list(staged)
         if c >= DEPTH:
             sends, landed[c - DEPTH] = lax.optimization_barrier((sends, landed[c - DEPTH]))
         owns.append(sends[0])
         twins.append(send(sends[0], pairs(ALL, 1)))
-        lower = [(t, t ^ 1) for t in LOW]
         far = send(sends[3], pairs(ALL, 4) if kind == "relay" else pairs(diagonal, 6))
-        near = send(sends[1], pairs(UP, 2) + lower if along == UP else pairs(ALL, 2))
+        near = send(sends[1], pairs(UP, 2) + pairs(LOW, 1) if along == UP else pairs(ALL, 2))
         over = send(sends[2], pairs(across, 4))
         landed.append([near, over, far])
-    for c, (_, kind, _, _, _) in enumerate(plan.chunks):
-        near, over, far = landed[c]
-        if kind == "relay":
-            far = send(far, pairs(LOW, 2) + [(t, t ^ 1) for t in UP])
-        parts = [owns[c], twins[c]]
-        for x in (near, over, far):
-            parts += [x, send(x, pairs(ALL, 1))]
-        got = attend(c, int(plan.starts[c]), c == 0, c == count - 1, counts, codes, parts, q_lat, q_rope_t, caches, state)
-        caches, state = got[:2], got[2]
-    return caches[0], caches[1], got[3]
+    state = None
+    for number, run in enumerate(runs):
+        parts = []
+        for c in run:
+            near, over, far = landed[c]
+            if plan.chunks[c][1] == "relay":
+                far = send(far, pairs(LOW, 2) + pairs(UP, 1))
+            parts += [owns[c], twins[c]]
+            for x in (near, over, far):
+                parts += [x, send(x, pairs(ALL, 1))]
+        *caches, state = attend(number, int(first[number]), number == 0, counts, codes, parts, q_lat, q_rope_t, caches, state)
+    return caches[0], caches[1], state
+
+
+def run_extra(step, me, left, weights, q_lat, q_rope_t, caches, state):
+    cap = jnp.asarray(PLAN.cap)
+    more = step * EXTRA + jnp.arange(EXTRA, dtype=jnp.int32)
+    part = jnp.arange(N)
+    slot = cap[me][:, None] + more
+    staged = norm_pack(EXTRA, 0, EXTRA, pack_tables(me, left, slot), *weights, [])
+    slot = cap[me ^ part, part // 2][:, None] + more
+    codes, counts, _ = attend_tables(me, left, slot, [EXTRA], [(0,)])
+    parts = []
+    for q, x in enumerate(staged):
+        x = lax.ppermute(x, "x", pairs(ALL, 2 * q)) if q else x
+        parts += [x, lax.ppermute(x, "x", pairs(ALL, 1))]
+    return attend(0, 0, False, counts, codes, parts, q_lat, q_rope_t, caches, state)
 
 
 def local_step(c_raw, k_raw, norm_gain, rope_cos, rope_sin, seq_lens, q_lat, q_rope):
     me = lax.axis_index("x")
     left = count_units(seq_lens)
+    own_lens = lax.dynamic_slice_in_dim(seq_lens, me * REQ, REQ)
+    weights = (c_raw, jnp.swapaxes(k_raw, 1, 2), norm_gain[None, :], rope_cos.T, rope_sin.T)
+    q_rope_t = jnp.swapaxes(q_rope, 1, 2)
+    c_cache, k_cache_t, state = run_plan(me, left, own_lens, weights, q_lat, q_rope_t)
     need = jnp.sum((left > 0).astype(jnp.int32), axis=-1)
-    fits = []
-    for plan in PLANS:
-        cap = np.stack([[plan.cap[s, (s // 2) ^ chip] for chip in range(CHIPS)] for s in range(N)])
-        fits.append(jnp.all(need <= jnp.asarray(cap)))
-    which = jnp.argmax(jnp.stack(fits)).astype(jnp.int32)
-    own_lens = lax.dynamic_slice_in_dim(seq_lens, me * REQ, REQ)
-    args = (me, left, own_lens, c_raw, jnp.swapaxes(k_raw, 1, 2), norm_gain[None, :], rope_cos.T, rope_sin.T, q_lat, jnp.swapaxes(q_rope, 1, 2))
-
-    def branch(number, *args):
-        return run_plan(PLANS[number], *args)
-
-    branches = [functools.partial(branch, number) for number in range(len(PLANS))]
-    c_cache, k_cache_t, o_lat = lax.switch(which, branches, *args) if len(PLANS) > 1 else branches[0](*args)
+    cap = np.stack([[PLAN.cap[s, (s // 2) ^ chip] for chip in range(CHIPS)] for s in range(N)])
+    steps = (jnp.maximum(jnp.max(need - jnp.asarray(cap)), 0) + EXTRA - 1) // EXTRA
+
+    def body(carry):
+        step, *caches, state = carry
+        return step + 1, *run_extra(step, me, left, weights, q_lat, q_rope_t, caches, state)
+
+    _, c_cache, k_cache_t, state = lax.while_loop(lambda carry: carry[0] < steps, body, (jnp.int32(0), c_cache, k_cache_t, state))
+    o_lat = (state[:, :, :RANK] / state[:, :, RANK : RANK + 1]).astype(jnp.bfloat16)
     return c_cache, jnp.swapaxes(k_cache_t, 1, 2), o_lat
 
 

time: 1310 us -> 1330 us (1.015)
  the two profiles are of different devices: /device:TPU:7 before, /device:TPU:0 now
where the time goes in v1:
time: 1330 us; the launch traced here: 1310 us
  waiting for transfers between devices  811 us (61%)
  Pallas kernels  407 us (31%)
  starting transfers between devices  64.5 us (5%)
  local copies, waits for them, and re-layouts  19.7 us (1%)
    ppermute x93, waiting for transfers between devices, send(): return lax.ppermute(x, 'x', pairs)  811 us
    pallas_call x13, Pallas kernels, norm_pack(): pl.pallas_call(kernel, grid_spec=grid_spec, out_shape=[jax.ShapeDtypeStru...  202 us
    pallas_call x12, Pallas kernels, attend(): pl.pallas_call(kernel, in_specs=in_specs, out_specs=out_specs, out_shape=...  190 us
    ppermute x93, starting transfers between devices, send(): return lax.ppermute(x, 'x', pairs)  64.5 us
  transfers between devices with their start and end apart: 93, of which 33 were waited for; matrix products, arithmetic and copies ran while one was open for 1% of the time, Pallas kernels for 30%

profile of v1, /device:TPU:0, one launch (start us, length us, event | category | flops | bytes accessed | tf_op | source)
XLA Modules:
  0.0 1312.7 jit_solution(6051375213495899541)
XLA Ops:
  7.3 6.8 norm_pack.20
  14.1 3.3 collective-permute-start.29
  17.5 11.6 norm_pack.21
  34.4 16.8 %norm_pack.22 = (bf16[6,1152,128]{2,1,0:T(8,128)(2,1)}, bf16[6,1152,128]{2,1,0:T(8,128)(2,1)}, bf16[6,1152,128]{2,1,0:T(8,128)(2,1)}, bf16[6,1152,128]{2,1,0:T(8,128)(2,1)}) custom-call(s32[288]{0:T(512)} %get-tuple-element.1323.req_ref, s32[288]{0:T(512)} %get-tuple-element.1322.unit_ref, s32[288]{0:T(512)} %reshape.785.ok_ref, ...), custom_call_target="tpu_custom_call" | custom-call | flops 600000000 | bytes 14155776 | tf_op jit(solution)/shard_map/norm_pack/pallas_call | solution.py:142
  51.2 56.1 %collective-permute-done.30.refs_4_ = bf16[2,1152,128]{2,1,0:T(8,128)(2,1)S(1)} collective-permute-done((bf16[2,1152,128]{2,1,0:T(8,128)(2,1)}, bf16[2,1152,128]{2,1,0:T(8,128)(2,1)S(1)}, u32[]{:S(2)}, u32[]{:S(2)}) %collective-permute-start.30) | collective-permute-done | bytes 589856 | tf_op jit(solution)/shard_map/ppermute | solution.py:372
  108.9 16.7 %norm_pack.23 = (bf16[6,1152,128]{2,1,0:T(8,128)(2,1)}, bf16[6,1152,128]{2,1,0:T(8,128)(2,1)}, bf16[6,1152,128]{2,1,0:T(8,128)(2,1)}, bf16[6,1152,128]{2,1,0:T(8,128)(2,1)}) custom-call(s32[288]{0:T(512)} %get-tuple-element.1323.req_ref, s32[288]{0:T(512)} %get-tuple-element.1322.unit_ref, s32[288]{0:T(512)} %reshape.785.ok_ref, ...), custom_call_target="tpu_custom_call" | custom-call | flops 600000000 | bytes 14155776 | tf_op jit(solution)/shard_map/norm_pack/pallas_call | solution.py:142
  126.7 2.9 collective-permute-done.98.refs_5_
  136.3 35.1 %collective-permute-done.32.refs_2_ = bf16[6,1152,128]{2,1,0:T(8,128)(2,1)} collective-permute-done((bf16[6,1152,128]{2,1,0:T(8,128)(2,1)}, bf16[6,1152,128]{2,1,0:T(8,128)(2,1)}, u32[]{:S(2)}, u32[]{:S(2)}) %collective-permute-start.32) | collective-permute-done | bytes 1769504 | tf_op jit(solution)/shard_map/ppermute | solution.py:372
  171.4 39.6 %collective-permute-done.33.refs_4_ = bf16[6,1152,128]{2,1,0:T(8,128)(2,1)} collective-permute-done((bf16[6,1152,128]{2,1,0:T(8,128)(2,1)}, bf16[6,1152,128]{2,1,0:T(8,128)(2,1)}, u32[]{:S(2)}, u32[]{:S(2)}) %collective-permute-start.33) | collective-permute-done | bytes 1769504 | tf_op jit(solution)/shard_map/ppermute | solution.py:372
  211.1 16.6 %norm_pack.24 = (bf16[6,1152,128]{2,1,0:T(8,128)(2,1)}, bf16[6,1152,128]{2,1,0:T(8,128)(2,1)}, bf16[6,1152,128]{2,1,0:T(8,128)(2,1)}, bf16[6,1152,128]{2,1,0:T(8,128)(2,1)}) custom-call(s32[288]{0:T(512)} %get-tuple-element.1323.req_ref, s32[288]{0:T(512)} %get-tuple-element.1322.unit_ref, s32[288]{0:T(512)} %reshape.785.ok_ref, ...), custom_call_target="tpu_custom_call" | custom-call | flops 600000000 | bytes 14155776 | tf_op jit(solution)/shard_map/norm_pack/pallas_call | solution.py:142
  228.2 18.4 %collective-permute-done.10.refs_2_ = bf16[6,1152,128]{2,1,0:T(8,128)(2,1)} collective-permute-done((bf16[6,1152,128]{2,1,0:T(8,128)(2,1)}, bf16[6,1152,128]{2,1,0:T(8,128)(2,1)}, u32[]{:S(2)}, u32[]{:S(2)}) %collective-permute-start.10) | collective-permute-done | bytes 1769504 | tf_op jit(solution)/shard_map/ppermute | solution.py:372
  246.6 2.3 collective-permute-done.11.refs_4_
  249.0 37.0 %collective-permute-done.12 = bf16[6,1152,128]{2,1,0:T(8,128)(2,1)} collective-permute-done((bf16[6,1152,128]{2,1,0:T(8,128)(2,1)}, bf16[6,1152,128]{2,1,0:T(8,128)(2,1)}, u32[]{:S(2)}, u32[]{:S(2)}) %collective-permute-start.12) | collective-permute-done | bytes 1769504 | tf_op jit(solution)/shard_map/ppermute | solution.py:372
  287.1 2.5 collective-permute-start.36
  289.6 4.9 collective-permute-start.37
  294.5 11.6 norm_pack.25
  306.2 21.5 %collective-permute-done.35.refs_2_ = bf16[6,1152,128]{2,1,0:T(8,128)(2,1)} collective-permute-done((bf16[6,1152,128]{2,1,0:T(8,128)(2,1)}, bf16[6,1152,128]{2,1,0:T(8,128)(2,1)}, u32[]{:S(2)}, u32[]{:S(2)}) %collective-permute-start.35) | collective-permute-done | bytes 1769504 | tf_op jit(solution)/shard_map/ppermute | solution.py:372
  328.0 40.6 %collective-permute-done.36.refs_4_ = bf16[6,1152,128]{2,1,0:T(8,128)(2,1)} collective-permute-done((bf16[6,1152,128]{2,1,0:T(8,128)(2,1)}, bf16[6,1152,128]{2,1,0:T(8,128)(2,1)}, u32[]{:S(2)}, u32[]{:S(2)}) %collective-permute-start.36) | collective-permute-done | bytes 1769504 | tf_op jit(solution)/shard_map/ppermute | solution.py:372
  369.2 18.9 %collective-permute-done.13.refs_2_ = bf16[4,1152,128]{2,1,0:T(8,128)(2,1)S(1)} collective-permute-done((bf16[4,1152,128]{2,1,0:T(8,128)(2,1)}, bf16[4,1152,128]{2,1,0:T(8,128)(2,1)S(1)}, u32[]{:S(2)}, u32[]{:S(2)}) %collective-permute-start.13) | collective-permute-done | bytes 1179680 | tf_op jit(solution)/shard_map/ppermute | solution.py:372
  388.1 5.8 collective-permute-done.14.refs_4_
  393.9 23.5 %collective-permute-done.15 = bf16[4,1152,128]{2,1,0:T(8,128)(2,1)} collective-permute-done((bf16[4,1152,128]{2,1,0:T(8,128)(2,1)}, bf16[4,1152,128]{2,1,0:T(8,128)(2,1)}, u32[]{:S(2)}, u32[]{:S(2)}) %collective-permute-start.15) | collective-permute-done | bytes 1179680 | tf_op jit(solution)/shard_map/ppermute | solution.py:372
  417.4 16.6 %norm_pack.26 = (bf16[6,1152,128]{2,1,0:T(8,128)(2,1)}, bf16[6,1152,128]{2,1,0:T(8,128)(2,1)}, bf16[6,1152,128]{2,1,0:T(8,128)(2,1)}, bf16[6,1152,128]{2,1,0:T(8,128)(2,1)}) custom-call(s32[288]{0:T(512)} %get-tuple-element.1323.req_ref, s32[288]{0:T(512)} %get-tuple-element.1322.unit_ref, s32[288]{0:T(512)} %reshape.785.ok_ref, ...), custom_call_target="tpu_custom_call" | custom-call | flops 600000000 | bytes 14155776 | tf_op jit(solution)/shard_map/norm_pack/pallas_call | solution.py:142
  434.1 21.6 %norm_pack.27 = (bf16[8,1152,128]{2,1,0:T(8,128)(2,1)}, bf16[8,1152,128]{2,1,0:T(8,128)(2,1)}, bf16[8,1152,128]{2,1,0:T(8,128)(2,1)}, bf16[8,1152,128]{2,1,0:T(8,128)(2,1)}) custom-call(s32[288]{0:T(512)} %get-tuple-element.1323.req_ref, s32[288]{0:T(512)} %get-tuple-element.1322.unit_ref, s32[288]{0:T(512)} %reshape.785.ok_ref, ...), custom_call_target="tpu_custom_call" | custom-call | flops 800000000 | bytes 18874368 | tf_op jit(solution)/shard_map/norm_pack/pallas_call | solution.py:142
  459.4 3.7 collective-permute-done.75.refs_3_
  464.9 5.2 collective-permute-start.39
  470.2 3.1 collective-permute-start.40
  473.8 30.5 %collective-permute-done.38.refs_2_ = bf16[6,1152,128]{2,1,0:T(8,128)(2,1)} collective-permute-done((bf16[6,1152,128]{2,1,0:T(8,128)(2,1)}, bf16[6,1152,128]{2,1,0:T(8,128)(2,1)}, u32[]{:S(2)}, u32[]{:S(2)}) %collective-permute-start.38) | collective-permute-done | bytes 1769504 | tf_op jit(solution)/shard_map/ppermute | solution.py:372
  505.4 42.0 %collective-permute-done.39.refs_4_ = bf16[6,1152,128]{2,1,0:T(8,128)(2,1)} collective-permute-done((bf16[6,1152,128]{2,1,0:T(8,128)(2,1)}, bf16[6,1152,128]{2,1,0:T(8,128)(2,1)}, u32[]{:S(2)}, u32[]{:S(2)}) %collective-permute-start.39) | collective-permute-done | bytes 1769504 | tf_op jit(solution)/shard_map/ppermute | solution.py:372
  547.4 2.6 collective-permute-start.18
  550.4 21.6 %norm_pack.28 = (bf16[8,1152,128]{2,1,0:T(8,128)(2,1)}, bf16[8,1152,128]{2,1,0:T(8,128)(2,1)}, bf16[8,1152,128]{2,1,0:T(8,128)(2,1)}, bf16[8,1152,128]{2,1,0:T(8,128)(2,1)}) custom-call(s32[288]{0:T(512)} %get-tuple-element.1323.req_ref, s32[288]{0:T(512)} %get-tuple-element.1322.unit_ref, s32[288]{0:T(512)} %reshape.785.ok_ref, ...), custom_call_target="tpu_custom_call" | custom-call | flops 800000000 | bytes 18874368 | tf_op jit(solution)/shard_map/norm_pack/pallas_call | solution.py:142
  572.1 19.3 %collective-permute-done.16.refs_2_ = bf16[8,1152,128]{2,1,0:T(8,128)(2,1)} collective-permute-done((bf16[8,1152,128]{2,1,0:T(8,128)(2,1)}, bf16[8,1152,128]{2,1,0:T(8,128)(2,1)}, u32[]{:S(2)}, u32[]{:S(2)}) %collective-permute-start.16) | collective-permute-done | bytes 2359328 | tf_op jit(solution)/shard_map/ppermute | solution.py:372
  591.4 59.4 %collective-permute-done.17.refs_4_ = bf16[8,1152,128]{2,1,0:T(8,128)(2,1)} collective-permute-done((bf16[8,1152,128]{2,1,0:T(8,128)(2,1)}, bf16[8,1152,128]{2,1,0:T(8,128)(2,1)}, u32[]{:S(2)}, u32[]{:S(2)}) %collective-permute-start.17) | collective-permute-done | bytes 2359328 | tf_op jit(solution)/shard_map/ppermute | solution.py:372
  651.7 21.6 %norm_pack.29 = (bf16[8,1152,128]{2,1,0:T(8,128)(2,1)}, bf16[8,1152,128]{2,1,0:T(8,128)(2,1)}, bf16[8,1152,128]{2,1,0:T(8,128)(2,1)}, bf16[8,1152,128]{2,1,0:T(8,128)(2,1)}) custom-call(s32[288]{0:T(512)} %get-tuple-element.1323.req_ref, s32[288]{0:T(512)} %get-tuple-element.1322.unit_ref, s32[288]{0:T(512)} %reshape.785.ok_ref, ...), custom_call_target="tpu_custom_call" | custom-call | flops 800000000 | bytes 18874368 | tf_op jit(solution)/shard_map/norm_pack/pallas_call | solution.py:142
  676.8 28.4 %collective-permute-done.41.refs_2_ = bf16[8,1152,128]{2,1,0:T(8,128)(2,1)} collective-permute-done((bf16[8,1152,128]{2,1,0:T(8,128)(2,1)}, bf16[8,1152,128]{2,1,0:T(8,128)(2,1)}, u32[]{:S(2)}, u32[]{:S(2)}) %collective-permute-start.41) | collective-permute-done | bytes 2359328 | tf_op jit(solution)/shard_map/ppermute | solution.py:372
  705.5 50.8 %collective-permute-done.42.refs_4_ = bf16[8,1152,128]{2,1,0:T(8,128)(2,1)} collective-permute-done((bf16[8,1152,128]{2,1,0:T(8,128)(2,1)}, bf16[8,1152,128]{2,1,0:T(8,128)(2,1)}, u32[]{:S(2)}, u32[]{:S(2)}) %collective-permute-start.42) | collective-permute-done | bytes 2359328 | tf_op jit(solution)/shard_map/ppermute | solution.py:372
  756.9 49.5 %collective-permute-done.19.refs_2_ = bf16[8,1152,128]{2,1,0:T(8,128)(2,1)} collective-permute-done((bf16[8,1152,128]{2,1,0:T(8,128)(2,1)}, bf16[8,1152,128]{2,1,0:T(8,128)(2,1)}, u32[]{:S(2)}, u32[]{:S(2)}) %collective-permute-start.19) | collective-permute-done | bytes 2359328 | tf_op jit(solution)/shard_map/ppermute | solution.py:372
  806.4 50.4 %collective-permute-done.20.refs_4_ = bf16[8,1152,128]{2,1,0:T(8,128)(2,1)} collective-permute-done((bf16[8,1152,128]{2,1,0:T(8,128)(2,1)}, bf16[8,1152,128]{2,1,0:T(8,128)(2,1)}, u32[]{:S(2)}, u32[]{:S(2)}) %collective-permute-start.20) | collective-permute-done | bytes 2359328 | tf_op jit(solution)/shard_map/ppermute | solution.py:372
  857.3 21.6 %norm_pack.30 = (bf16[8,1152,128]{2,1,0:T(8,128)(2,1)}, bf16[8,1152,128]{2,1,0:T(8,128)(2,1)}, bf16[8,1152,128]{2,1,0:T(8,128)(2,1)}, bf16[8,1152,128]{2,1,0:T(8,128)(2,1)}) custom-call(s32[288]{0:T(512)} %get-tuple-element.1323.req_ref, s32[288]{0:T(512)} %get-tuple-element.1322.unit_ref, s32[288]{0:T(512)} %reshape.785.ok_ref, ...), custom_call_target="tpu_custom_call" | custom-call | flops 800000000 | bytes 18874368 | tf_op jit(solution)/shard_map/norm_pack/pallas_call | solution.py:142
  878.9 11.6 norm_pack.31
  891.1 5.4 collective-permute-start.27
  896.5 23.1 %collective-permute-done.23.refs_2_ = bf16[4,1152,128]{2,1,0:T(8,128)(2,1)S(1)} collective-permute-done((bf16[4,1152,128]{2,1,0:T(8,128)(2,1)}, bf16[4,1152,128]{2,1,0:T(8,128)(2,1)S(1)}, u32[]{:S(2)}, u32[]{:S(2)}) %collective-permute-start.23) | collective-permute-done | bytes 1179680 | tf_op jit(solution)/shard_map/ppermute | solution.py:372
  919.6 22.8 %collective-permute-done.25.refs_4_ = bf16[4,1152,128]{2,1,0:T(8,128)(2,1)} collective-permute-done((bf16[4,1152,128]{2,1,0:T(8,128)(2,1)}, bf16[4,1152,128]{2,1,0:T(8,128)(2,1)}, u32[]{:S(2)}, u32[]{:S(2)}) %collective-permute-start.25) | collective-permute-done | bytes 1179680 | tf_op jit(solution)/shard_map/ppermute | solution.py:372
  944.4 2.5 collective-permute-start.45
  947.5 49.4 %collective-permute-done.44.refs_2_ = bf16[8,1152,128]{2,1,0:T(8,128)(2,1)} collective-permute-done((bf16[8,1152,128]{2,1,0:T(8,128)(2,1)}, bf16[8,1152,128]{2,1,0:T(8,128)(2,1)}, u32[]{:S(2)}, u32[]{:S(2)}) %collective-permute-start.44) | collective-permute-done | bytes 2359328 | tf_op jit(solution)/shard_map/ppermute | solution.py:372
  996.9 52.5 %collective-permute-done.45.refs_4_ = bf16[8,1152,128]{2,1,0:T(8,128)(2,1)} collective-permute-done((bf16[8,1152,128]{2,1,0:T(8,128)(2,1)}, bf16[8,1152,128]{2,1,0:T(8,128)(2,1)}, u32[]{:S(2)}, u32[]{:S(2)}) %collective-permute-start.45) | collective-permute-done | bytes 2359328 | tf_op jit(solution)/shard_map/ppermute | solution.py:372
  1050.7 6.8 norm_pack.32
  1064.6 12.0 collective-permute-done.48.refs_10_
  1076.6 4.2 collective-permute-start.52
  1082.4 10.2 collective-permute-done.52.refs_14_
  1093.6 14.9 %blank.1 = (bf16[12,6144,512]{2,1,0:T(8,128)(2,1)}, bf16[12,64,6144]{2,1,0:T(8,128)(2,1)}) custom-call(s32[12]{0:T(128)} %dynamic_slice.22.len_ref), custom_call_target="tpu_custom_call" | custom-call | flops 400000000 | bytes 85000000 | tf_op jit(solution)/shard_map/blank/pallas_call | solution.py:296
  1111.3 7.7 attend.19
  1118.9 15.5 %attend.20 = (bf16[12,6144,512]{2,1,0:T(8,128)(2,1)}, bf16[12,64,6144]{2,1,0:T(8,128)(2,1)}, f32[12,128,768]{2,1,0:T(8,128)}) custom-call(s32[12]{0:T(128)} %convert_reduce_fusion.12.count_ref, s32[576]{0:T(1024)} %select_reduce_fusion.2.code_ref, bf16[4,1152,128]{2,1,0:T(8,128)(2,1)} %get-tuple-element.906.refs_0_, ...), custom_call_target="tpu_custom_call", output_to_operand_aliasing={{0}: (12, {}), {1}: (13, {})} | custom-call | flops 200000000 | bytes 4718592 | tf_op jit(solution)/shard_map/attend/pallas_call | solution.py:255
  1134.5 21.6 %attend.21 = (bf16[12,6144,512]{2,1,0:T(8,128)(2,1)}, bf16[12,64,6144]{2,1,0:T(8,128)(2,1)}, f32[12,128,768]{2,1,0:T(8,128)}) custom-call(s32[12]{0:T(128)} %convert_reduce_fusion.12.count_ref, s32[576]{0:T(1024)} %select_reduce_fusion.2.code_ref, bf16[6,1152,128]{2,1,0:T(8,128)(2,1)} %get-tuple-element.1024.refs_0_, ...), custom_call_target="tpu_custom_call", output_to_operand_aliasing={{0}: (12, {}), {1}: (13, {})} | custom-call | flops 200000000 | bytes 4718592 | tf_op jit(solution)/shard_map/attend/pallas_call | solution.py:255
  1156.1 20.3 %attend.22 = (bf16[12,6144,512]{2,1,0:T(8,128)(2,1)}, bf16[12,64,6144]{2,1,0:T(8,128)(2,1)}, f32[12,128,768]{2,1,0:T(8,128)}) custom-call(s32[12]{0:T(128)} %convert_reduce_fusion.12.count_ref, s32[576]{0:T(1024)} %select_reduce_fusion.2.code_ref, bf16[6,1152,128]{2,1,0:T(8,128)(2,1)} %get-tuple-element.1020.refs_0_, ...), custom_call_target="tpu_custom_call", output_to_operand_aliasing={{0}: (12, {}), {1}: (13, {})} | custom-call | flops 200000000 | bytes 4718592 | tf_op jit(solution)/shard_map/attend/pallas_call | solution.py:255
  1176.4 20.2 %attend.23 = (bf16[12,6144,512]{2,1,0:T(8,128)(2,1)}, bf16[12,64,6144]{2,1,0:T(8,128)(2,1)}, f32[12,128,768]{2,1,0:T(8,128)}) custom-call(s32[12]{0:T(128)} %convert_reduce_fusion.12.count_ref, s32[576]{0:T(1024)} %select_reduce_fusion.2.code_ref, bf16[6,1152,128]{2,1,0:T(8,128)(2,1)} %get-tuple-element.1016.refs_0_, ...), custom_call_target="tpu_custom_call", output_to_operand_aliasing={{0}: (12, {}), {1}: (13, {})} | custom-call | flops 200000000 | bytes 4718592 | tf_op jit(solution)/shard_map/attend/pallas_call | solution.py:255
  1196.7 13.5 %attend.24 = (bf16[12,6144,512]{2,1,0:T(8,128)(2,1)}, bf16[12,64,6144]{2,1,0:T(8,128)(2,1)}, f32[12,128,768]{2,1,0:T(8,128)}) custom-call(s32[12]{0:T(128)} %convert_reduce_fusion.12.count_ref, s32[576]{0:T(1024)} %select_reduce_fusion.2.code_ref, bf16[4,1152,128]{2,1,0:T(8,128)(2,1)} %get-tuple-element.1012.refs_0_, ...), custom_call_target="tpu_custom_call", output_to_operand_aliasing={{0}: (12, {}), {1}: (13, {})} | custom-call | flops 200000000 | bytes 4718592 | tf_op jit(solution)/shard_map/attend/pallas_call | solution.py:255
  1210.2 20.2 %attend.25 = (bf16[12,6144,512]{2,1,0:T(8,128)(2,1)}, bf16[12,64,6144]{2,1,0:T(8,128)(2,1)}, f32[12,128,768]{2,1,0:T(8,128)}) custom-call(s32[12]{0:T(128)} %convert_reduce_fusion.12.count_ref, s32[576]{0:T(1024)} %select_reduce_fusion.2.code_ref, bf16[6,1152,128]{2,1,0:T(8,128)(2,1)} %get-tuple-element.1008.refs_0_, ...), custom_call_target="tpu_custom_call", output_to_operand_aliasing={{0}: (12, {}), {1}: (13, {})} | custom-call | flops 200000000 | bytes 4718592 | tf_op jit(solution)/shard_map/attend/pallas_call | solution.py:255
  1230.4 20.3 %attend.26 = (bf16[12,6144,512]{2,1,0:T(8,128)(2,1)}, bf16[12,64,6144]{2,1,0:T(8,128)(2,1)}, f32[12,128,768]{2,1,0:T(8,128)}) custom-call(s32[12]{0:T(128)} %convert_reduce_fusion.12.count_ref, s32[576]{0:T(1024)} %select_reduce_fusion.2.code_ref, bf16[8,1152,128]{2,1,0:T(8,128)(2,1)} %get-tuple-element.1004.refs_0_, ...), custom_call_target="tpu_custom_call", output_to_operand_aliasing={{0}: (12, {}), {1}: (13, {})} | custom-call | flops 200000000 | bytes 4718592 | tf_op jit(solution)/shard_map/attend/pallas_call | solution.py:255
  1250.7 15.5 %attend.27 = (bf16[12,6144,512]{2,1,0:T(8,128)(2,1)}, bf16[12,64,6144]{2,1,0:T(8,128)(2,1)}, f32[12,128,768]{2,1,0:T(8,128)}) custom-call(s32[12]{0:T(128)} %convert_reduce_fusion.12.count_ref, s32[576]{0:T(1024)} %select_reduce_fusion.2.code_ref, bf16[8,1152,128]{2,1,0:T(8,128)(2,1)} %get-tuple-element.1000.refs_0_, ...), custom_call_target="tpu_custom_call", output_to_operand_aliasing={{0}: (12, {}), {1}: (13, {})} | custom-call | flops 200000000 | bytes 4718592 | tf_op jit(solution)/shard_map/attend/pallas_call | solution.py:255
  1266.2 14.2 %attend.28 = (bf16[12,6144,512]{2,1,0:T(8,128)(2,1)}, bf16[12,64,6144]{2,1,0:T(8,128)(2,1)}, f32[12,128,768]{2,1,0:T(8,128)}) custom-call(s32[12]{0:T(128)} %convert_reduce_fusion.12.count_ref, s32[576]{0:T(1024)} %select_reduce_fusion.2.code_ref, bf16[8,1152,128]{2,1,0:T(8,128)(2,1)} %get-tuple-element.996.refs_0_, ...), custom_call_target="tpu_custom_call", output_to_operand_aliasing={{0}: (12, {}), {1}: (13, {})} | custom-call | flops 200000000 | bytes 4718592 | tf_op jit(solution)/shard_map/attend/pallas_call | solution.py:255
  1280.4 12.7 attend.29
  1293.3 8.7 attend.30
  1302.1 6.6 copy.69
  1309.4 3.3 divide_convert_fusion
  (313 shorter events, 53.9 us)
Async XLA Ops:
  29.1 79.6 %collective-permute-start.7 = (bf16[4,1152,128]{2,1,0:T(8,128)(2,1)}, bf16[4,1152,128]{2,1,0:T(8,128)(2,1)}, u32[]{:S(2)}, u32[]{:S(2)}) collective-permute-start(bf16[4,1152,128]{2,1,0:T(8,128)(2,1)} %get-tuple-element.932), channel_id=1, source_target_pairs={{0,2},{1,3},{2,0},{3,1},{4,6},{5,7},{6,4},{7,5}} | collective-permute-start | bytes 3538952 | tf_op jit(solution)/shard_map/ppermute | solution.py:372
  29.2 96.5 %collective-permute-start.8 = (bf16[4,1152,128]{2,1,0:T(8,128)(2,1)}, bf16[4,1152,128]{2,1,0:T(8,128)(2,1)}, u32[]{:S(2)}, u32[]{:S(2)}) collective-permute-start(bf16[4,1152,128]{2,1,0:T(8,128)(2,1)} %get-tuple-element.933), channel_id=1, source_target_pairs={{0,4},{1,5},{2,6},{3,7},{4,0},{5,1},{6,2},{7,3}} | collective-permute-start | bytes 3538952 | tf_op jit(solution)/shard_map/ppermute | solution.py:372
  31.2 94.5 %collective-permute-start.9 = (bf16[4,1152,128]{2,1,0:T(8,128)(2,1)}, bf16[4,1152,128]{2,1,0:T(8,128)(2,1)}, u32[]{:S(2)}, u32[]{:S(2)}) collective-permute-start(bf16[4,1152,128]{2,1,0:T(8,128)(2,1)} %get-tuple-element.934), channel_id=1, source_target_pairs={{0,6},{1,7},{2,4},{3,5},{4,2},{5,3},{6,0},{7,1}} | collective-permute-start | bytes 3538952 | tf_op jit(solution)/shard_map/ppermute | solution.py:372
  32.6 74.8 %collective-permute-start.30 = (bf16[2,1152,128]{2,1,0:T(8,128)(2,1)}, bf16[2,1152,128]{2,1,0:T(8,128)(2,1)S(1)}, u32[]{:S(2)}, u32[]{:S(2)}) collective-permute-start(bf16[2,1152,128]{2,1,0:T(8,128)(2,1)} %get-tuple-element.971), channel_id=1, source_target_pairs={{0,4},{1,5},{2,6},{3,7},{4,0},{5,1},{6,2},{7,3}} | collective-permute-start | bytes 1769480 | tf_op jit(solution)/shard_map/ppermute | solution.py:372
  34.1 73.2 %collective-permute-start.31 = (bf16[2,1152,128]{2,1,0:T(8,128)(2,1)}, bf16[2,1152,128]{2,1,0:T(8,128)(2,1)S(1)}, u32[]{:S(2)}, u32[]{:S(2)}) collective-permute-start(bf16[2,1152,128]{2,1,0:T(8,128)(2,1)} %get-tuple-element.972), channel_id=1, source_target_pairs={{0,6},{1,7},{2,4},{3,5},{4,2},{5,3},{6,0},{7,1}} | collective-permute-start | bytes 1769480 | tf_op jit(solution)/shard_map/ppermute | solution.py:372
  129.6 41.8 %collective-permute-start.32 = (bf16[6,1152,128]{2,1,0:T(8,128)(2,1)}, bf16[6,1152,128]{2,1,0:T(8,128)(2,1)}, u32[]{:S(2)}, u32[]{:S(2)}) collective-permute-start(bf16[6,1152,128]{2,1,0:T(8,128)(2,1)} %get-tuple-element.973), channel_id=1, source_target_pairs={{0,2},{1,3},{2,0},{3,1},{4,6},{5,7},{6,4},{7,5}} | collective-permute-start | bytes 5308424 | tf_op jit(solution)/shard_map/ppermute | solution.py:372
  131.3 79.7 %collective-permute-start.33 = (bf16[6,1152,128]{2,1,0:T(8,128)(2,1)}, bf16[6,1152,128]{2,1,0:T(8,128)(2,1)}, u32[]{:S(2)}, u32[]{:S(2)}) collective-permute-start(bf16[6,1152,128]{2,1,0:T(8,128)(2,1)} %get-tuple-element.974), channel_id=1, source_target_pairs={{0,4},{1,5},{2,6},{3,7},{4,0},{5,1},{6,2},{7,3}} | collective-permute-start | bytes 5308424 | tf_op jit(solution)/shard_map/ppermute | solution.py:372
  132.2 78.9 %collective-permute-start.34 = (bf16[6,1152,128]{2,1,0:T(8,128)(2,1)}, bf16[6,1152,128]{2,1,0:T(8,128)(2,1)}, u32[]{:S(2)}, u32[]{:S(2)}) collective-permute-start(bf16[6,1152,128]{2,1,0:T(8,128)(2,1)} %get-tuple-element.975), channel_id=1, source_target_pairs={{0,6},{1,7},{2,4},{3,5},{4,2},{5,3},{6,0},{7,1}} | collective-permute-start | bytes 5308424 | tf_op jit(solution)/shard_map/ppermute | solution.py:372
  133.7 94.0 %collective-permute-start.88 = (bf16[6,1152,128]{2,1,0:T(8,128)(2,1)S(1)}, bf16[6,1152,128]{2,1,0:T(8,128)(2,1)}, u32[]{:S(2)}, u32[]{:S(2)}) collective-permute-start(bf16[6,1152,128]{2,1,0:T(8,128)(2,1)S(1)} %copy-done.9), channel_id=1, source_target_pairs={{0,1},{1,0},{2,3},{3,2},{4,5},{5,4},{6,7},{7,6}} | collective-permute-start | bytes 5308424 | tf_op jit(solution)/shard_map/ppermute | solution.py:372
  135.2 111.4 %collective-permute-start.10 = (bf16[6,1152,128]{2,1,0:T(8,128)(2,1)}, bf16[6,1152,128]{2,1,0:T(8,128)(2,1)}, u32[]{:S(2)}, u32[]{:S(2)}) collective-permute-start(bf16[6,1152,128]{2,1,0:T(8,128)(2,1)} %get-tuple-element.935), channel_id=1, source_target_pairs={{0,2},{1,3},{2,0},{3,1},{4,5},{5,4},{6,7},{7,6}} | collective-permute-start | bytes 5308424 | tf_op jit(solution)/shard_map/ppermute | solution.py:372
  171.4 77.5 %collective-permute-start.11 = (bf16[6,1152,128]{2,1,0:T(8,128)(2,1)}, bf16[6,1152,128]{2,1,0:T(8,128)(2,1)}, u32[]{:S(2)}, u32[]{:S(2)}) collective-permute-start(bf16[6,1152,128]{2,1,0:T(8,128)(2,1)} %get-tuple-element.936), channel_id=1, source_target_pairs={{0,4},{1,5},{2,6},{3,7},{4,0},{5,1},{6,2},{7,3}} | collective-permute-start | bytes 5308424 | tf_op jit(solution)/shard_map/ppermute | solution.py:372
  211.0 74.9 %collective-permute-start.12 = (bf16[6,1152,128]{2,1,0:T(8,128)(2,1)}, bf16[6,1152,128]{2,1,0:T(8,128)(2,1)}, u32[]{:S(2)}, u32[]{:S(2)}) collective-permute-start(bf16[6,1152,128]{2,1,0:T(8,128)(2,1)} %get-tuple-element.937), channel_id=1, source_target_pairs={{0,4},{1,5},{2,6},{3,7},{4,0},{5,1},{6,2},{7,3}} | collective-permute-start | bytes 5308424 | tf_op jit(solution)/shard_map/ppermute | solution.py:372
  211.0 76.0 %collective-permute-start.83 = (bf16[6,1152,128]{2,1,0:T(8,128)(2,1)}, bf16[6,1152,128]{2,1,0:T(8,128)(2,1)}, u32[]{:S(2)}, u32[]{:S(2)}) collective-permute-start(bf16[6,1152,128]{2,1,0:T(8,128)(2,1)} %get-tuple-element.1020.refs_0_), channel_id=1, source_target_pairs={{0,1},{1,0},{2,3},{3,2},{4,5},{5,4},{6,7},{7,6}} | collective-permute-start | bytes 5308424 | tf_op jit(solution)/shard_map/ppermute | solution.py:372
  227.7 61.9 %collective-permute-start.89 = (bf16[6,1152,128]{2,1,0:T(8,128)(2,1)}, bf16[6,1152,128]{2,1,0:T(8,128)(2,1)}, u32[]{:S(2)}, u32[]{:S(2)}) collective-permute-start(bf16[6,1152,128]{2,1,0:T(8,128)(2,1)} %collective-permute-done.32.refs_2_), channel_id=1, source_target_pairs={{0,1},{1,0},{2,3},{3,2},{4,5},{5,4},{6,7},{7,6}} | collective-permute-start | bytes 5308424 | tf_op jit(solution)/shard_map/ppermute | solution.py:372
  246.6 59.5 %collective-permute-start.90 = (bf16[6,1152,128]{2,1,0:T(8,128)(2,1)}, bf16[6,1152,128]{2,1,0:T(8,128)(2,1)}, u32[]{:S(2)}, u32[]{:S(2)}) collective-permute-start(bf16[6,1152,128]{2,1,0:T(8,128)(2,1)} %collective-permute-done.33.refs_4_), channel_id=1, source_target_pairs={{0,1},{1,0},{2,3},{3,2},{4,5},{5,4},{6,7},{7,6}} | collective-permute-start | bytes 5308424 | tf_op jit(solution)/shard_map/ppermute | solution.py:372
  249.0 57.2 %collective-permute-start.91 = (bf16[6,1152,128]{2,1,0:T(8,128)(2,1)}, bf16[6,1152,128]{2,1,0:T(8,128)(2,1)}, u32[]{:S(2)}, u32[]{:S(2)}) collective-permute-start(bf16[6,1152,128]{2,1,0:T(8,128)(2,1)} %collective-permute-done.34.refs_6_), channel_id=1, source_target_pairs={{0,1},{1,0},{2,3},{3,2},{4,5},{5,4},{6,7},{7,6}} | collective-permute-start | bytes 5308424 | tf_op jit(solution)/shard_map/ppermute | solution.py:372
  285.9 41.8 %collective-permute-start.35 = (bf16[6,1152,128]{2,1,0:T(8,128)(2,1)}, bf16[6,1152,128]{2,1,0:T(8,128)(2,1)}, u32[]{:S(2)}, u32[]{:S(2)}) collective-permute-start(bf16[6,1152,128]{2,1,0:T(8,128)(2,1)} %get-tuple-element.976), channel_id=1, source_target_pairs={{0,2},{1,3},{2,0},{3,1},{4,6},{5,7},{6,4},{7,5}} | collective-permute-start | bytes 5308424 | tf_op jit(solution)/shard_map/ppermute | solution.py:372
  287.1 81.6 %collective-permute-start.36 = (bf16[6,1152,128]{2,1,0:T(8,128)(2,1)}, bf16[6,1152,128]{2,1,0:T(8,128)(2,1)}, u32[]{:S(2)}, u32[]{:S(2)}) collective-permute-start(bf16[6,1152,128]{2,1,0:T(8,128)(2,1)} %get-tuple-element.977), channel_id=1, source_target_pairs={{0,4},{1,5},{4,0},{5,1},{6,2},{7,3}} | collective-permute-start | bytes 5308424 | tf_op jit(solution)/shard_map/ppermute | solution.py:372
  289.6 79.1 %collective-permute-start.37 = (bf16[6,1152,128]{2,1,0:T(8,128)(2,1)}, bf16[6,1152,128]{2,1,0:T(8,128)(2,1)}, u32[]{:S(2)}, u32[]{:S(2)}) collective-permute-start(bf16[6,1152,128]{2,1,0:T(8,128)(2,1)} %get-tuple-element.978), channel_id=1, source_target_pairs={{0,6},{1,7},{4,2},{5,3},{6,0},{7,1}} | collective-permute-start | bytes 5308424 | tf_op jit(solution)/shard_map/ppermute | solution.py:372
  306.1 82.0 %collective-permute-start.13 = (bf16[4,1152,128]{2,1,0:T(8,128)(2,1)}, bf16[4,1152,128]{2,1,0:T(8,128)(2,1)S(1)}, u32[]{:S(2)}, u32[]{:S(2)}) collective-permute-start(bf16[4,1152,128]{2,1,0:T(8,128)(2,1)} %get-tuple-element.938), channel_id=1, source_target_pairs={{0,2},{1,3},{2,0},{3,1},{4,5},{5,4},{6,7},{7,6}} | collective-permute-start | bytes 3538952 | tf_op jit(solution)/shard_map/ppermute | solution.py:372
  306.2 87.8 %collective-permute-start.14 = (bf16[4,1152,128]{2,1,0:T(8,128)(2,1)}, bf16[4,1152,128]{2,1,0:T(8,128)(2,1)}, u32[]{:S(2)}, u32[]{:S(2)}) collective-permute-start(bf16[4,1152,128]{2,1,0:T(8,128)(2,1)} %get-tuple-element.939), channel_id=1, source_target_pairs={{0,4},{1,5},{2,6},{3,7},{4,0},{5,1},{6,2},{7,3}} | collective-permute-start | bytes 3538952 | tf_op jit(solution)/shard_map/ppermute | solution.py:372
  327.7 89.7 %collective-permute-start.15 = (bf16[4,1152,128]{2,1,0:T(8,128)(2,1)}, bf16[4,1152,128]{2,1,0:T(8,128)(2,1)}, u32[]{:S(2)}, u32[]{:S(2)}) collective-permute-start(bf16[4,1152,128]{2,1,0:T(8,128)(2,1)} %get-tuple-element.940), channel_id=1, source_target_pairs={{0,4},{1,5},{2,6},{3,7},{4,0},{5,1},{6,2},{7,3}} | collective-permute-start | bytes 3538952 | tf_op jit(solution)/shard_map/ppermute | solution.py:372
  368.7 87.0 %collective-permute-start.79 = (bf16[6,1152,128]{2,1,0:T(8,128)(2,1)S(1)}, bf16[6,1152,128]{2,1,0:T(8,128)(2,1)}, u32[]{:S(2)}, u32[]{:S(2)}) collective-permute-start(bf16[6,1152,128]{2,1,0:T(8,128)(2,1)S(1)} %copy-done.10), channel_id=1, source_target_pairs={{0,1},{1,0},{2,3},{3,2},{4,5},{5,4},{6,7},{7,6}} | collective-permute-start | bytes 5308424 | tf_op jit(solution)/shard_map/ppermute | solution.py:372
  368.7 87.6 %collective-permute-start.86 = (bf16[6,1152,128]{2,1,0:T(8,128)(2,1)}, bf16[6,1152,128]{2,1,0:T(8,128)(2,1)}, u32[]{:S(2)}, u32[]{:S(2)}) collective-permute-start(bf16[6,1152,128]{2,1,0:T(8,128)(2,1)} %collective-permute-done.12), channel_id=1, source_target_pairs={{4,6},{5,7},{6,4},{7,5},{0,1},{1,0},{2,3},{3,2}} | collective-permute-start | bytes 5308424 | tf_op jit(solution)/shard_map/ppermute | solution.py:372
  388.1 68.6 %collective-permute-start.84 = (bf16[6,1152,128]{2,1,0:T(8,128)(2,1)}, bf16[6,1152,128]{2,1,0:T(8,128)(2,1)}, u32[]{:S(2)}, u32[]{:S(2)}) collective-permute-start(bf16[6,1152,128]{2,1,0:T(8,128)(2,1)} %collective-permute-done.10.refs_2_), channel_id=1, source_target_pairs={{0,1},{1,0},{2,3},{3,2},{4,5},{5,4},{6,7},{7,6}} | collective-permute-start | bytes 5308424 | tf_op jit(solution)/shard_map/ppermute | solution.py:372
  393.9 62.3 %collective-permute-start.74 = (bf16[4,1152,128]{2,1,0:T(8,128)(2,1)}, bf16[4,1152,128]{2,1,0:T(8,128)(2,1)}, u32[]{:S(2)}, u32[]{:S(2)}) collective-permute-start(bf16[4,1152,128]{2,1,0:T(8,128)(2,1)} %get-tuple-element.1012.refs_0_), channel_id=1, source_target_pairs={{0,1},{1,0},{2,3},{3,2},{4,5},{5,4},{6,7},{7,6}} | collective-permute-start | bytes 3538952 | tf_op jit(solution)/shard_map/ppermute | solution.py:372
  417.4 39.4 %collective-permute-start.85 = (bf16[6,1152,128]{2,1,0:T(8,128)(2,1)}, bf16[6,1152,128]{2,1,0:T(8,128)(2,1)}, u32[]{:S(2)}, u32[]{:S(2)}) collective-permute-start(bf16[6,1152,128]{2,1,0:T(8,128)(2,1)} %collective-permute-done.11.refs_4_), channel_id=1, source_target_pairs={{0,1},{1,0},{2,3},{3,2},{4,5},{5,4},{6,7},{7,6}} | collective-permute-start | bytes 5308424 | tf_op jit(solution)/shard_map/ppermute | solution.py:372
  463.1 41.2 %collective-permute-start.38 = (bf16[6,1152,128]{2,1,0:T(8,128)(2,1)}, bf16[6,1152,128]{2,1,0:T(8,128)(2,1)}, u32[]{:S(2)}, u32[]{:S(2)}) collective-permute-start(bf16[6,1152,128]{2,1,0:T(8,128)(2,1)} %get-tuple-element.979), channel_id=1, source_target_pairs={{0,2},{1,3},{2,0},{3,1},{4,6},{5,7},{6,4},{7,5}} | collective-permute-start | bytes 5308424 | tf_op jit(solution)/shard_map/ppermute | solution.py:372
  464.9 82.4 %collective-permute-start.39 = (bf16[6,1152,128]{2,1,0:T(8,128)(2,1)}, bf16[6,1152,128]{2,1,0:T(8,128)(2,1)}, u32[]{:S(2)}, u32[]{:S(2)}) collective-permute-start(bf16[6,1152,128]{2,1,0:T(8,128)(2,1)} %get-tuple-element.980), channel_id=1, source_target_pairs={{0,4},{1,5},{2,6},{4,0},{5,1},{6,2},{7,3}} | collective-permute-start | bytes 5308424 | tf_op jit(solution)/shard_map/ppermute | solution.py:372
  470.2 77.2 %collective-permute-start.40 = (bf16[6,1152,128]{2,1,0:T(8,128)(2,1)}, bf16[6,1152,128]{2,1,0:T(8,128)(2,1)}, u32[]{:S(2)}, u32[]{:S(2)}) collective-permute-start(bf16[6,1152,128]{2,1,0:T(8,128)(2,1)} %get-tuple-element.981), channel_id=1, source_target_pairs={{0,6},{1,7},{2,4},{4,2},{5,3},{6,0},{7,1}} | collective-permute-start | bytes 5308424 | tf_op jit(solution)/shard_map/ppermute | solution.py:372
  473.3 76.7 %collective-permute-start.70 = (bf16[6,1152,128]{2,1,0:T(8,128)(2,1)}, bf16[6,1152,128]{2,1,0:T(8,128)(2,1)}, u32[]{:S(2)}, u32[]{:S(2)}) collective-permute-start(bf16[6,1152,128]{2,1,0:T(8,128)(2,1)} %get-tuple-element.1008.refs_0_), channel_id=1, source_target_pairs={{0,1},{1,0},{2,3},{3,2},{4,5},{5,4},{6,7},{7,6}} | collective-permute-start | bytes 5308424 | tf_op jit(solution)/shard_map/ppermute | solution.py:372
  473.8 76.2 %collective-permute-start.87 = (bf16[6,1152,128]{2,1,0:T(8,128)(2,1)}, bf16[6,1152,128]{2,1,0:T(8,128)(2,1)}, u32[]{:S(2)}, u32[]{:S(2)}) collective-permute-start(bf16[6,1152,128]{2,1,0:T(8,128)(2,1)} %collective-permute-done.86.refs_6_), channel_id=1, source_target_pairs={{0,1},{1,0},{2,3},{3,2},{4,5},{5,4},{6,7},{7,6}} | collective-permute-start | bytes 5308424 | tf_op jit(solution)/shard_map/ppermute | solution.py:372
  504.3 87.1 %collective-permute-start.16 = (bf16[8,1152,128]{2,1,0:T(8,128)(2,1)}, bf16[8,1152,128]{2,1,0:T(8,128)(2,1)}, u32[]{:S(2)}, u32[]{:S(2)}) collective-permute-start(bf16[8,1152,128]{2,1,0:T(8,128)(2,1)} %get-tuple-element.941), channel_id=1, source_target_pairs={{0,2},{1,3},{2,0},{3,1},{4,6},{5,7},{6,4},{7,5}} | collective-permute-start | bytes 7077896 | tf_op jit(solution)/shard_map/ppermute | solution.py:372
  547.4 103.4 %collective-permute-start.17 = (bf16[8,1152,128]{2,1,0:T(8,128)(2,1)}, bf16[8,1152,128]{2,1,0:T(8,128)(2,1)}, u32[]{:S(2)}, u32[]{:S(2)}) collective-permute-start(bf16[8,1152,128]{2,1,0:T(8,128)(2,1)} %get-tuple-element.942), channel_id=1, source_target_pairs={{0,4},{1,5},{2,6},{3,7},{4,0},{5,1},{6,2},{7,3}} | collective-permute-start | bytes 7077896 | tf_op jit(solution)/shard_map/ppermute | solution.py:372
  547.4 103.4 %collective-permute-start.18 = (bf16[8,1152,128]{2,1,0:T(8,128)(2,1)}, bf16[8,1152,128]{2,1,0:T(8,128)(2,1)}, u32[]{:S(2)}, u32[]{:S(2)}) collective-permute-start(bf16[8,1152,128]{2,1,0:T(8,128)(2,1)} %get-tuple-element.943), channel_id=1, source_target_pairs={{0,6},{1,7},{2,4},{3,5},{4,2},{5,3},{6,0},{7,1}} | collective-permute-start | bytes 7077896 | tf_op jit(solution)/shard_map/ppermute | solution.py:372
  549.9 101.5 %collective-permute-start.66 = (bf16[8,1152,128]{2,1,0:T(8,128)(2,1)}, bf16[8,1152,128]{2,1,0:T(8,128)(2,1)}, u32[]{:S(2)}, u32[]{:S(2)}) collective-permute-start(bf16[8,1152,128]{2,1,0:T(8,128)(2,1)} %get-tuple-element.1004.refs_0_), channel_id=1, source_target_pairs={{0,1},{1,0},{2,3},{3,2},{4,5},{5,4},{6,7},{7,6}} | collective-permute-start | bytes 7077896 | tf_op jit(solution)/shard_map/ppermute | solution.py:372
  572.1 101.2 %collective-permute-start.71 = (bf16[6,1152,128]{2,1,0:T(8,128)(2,1)}, bf16[6,1152,128]{2,1,0:T(8,128)(2,1)}, u32[]{:S(2)}, u32[]{:S(2)}) collective-permute-start(bf16[6,1152,128]{2,1,0:T(8,128)(2,1)} %collective-permute-done.38.refs_2_), channel_id=1, source_target_pairs={{0,1},{1,0},{2,3},{3,2},{4,5},{5,4},{6,7},{7,6}} | collective-permute-start | bytes 5308424 | tf_op jit(solution)/shard_map/ppermute | solution.py:372
  591.4 81.9 %collective-permute-start.72 = (bf16[6,1152,128]{2,1,0:T(8,128)(2,1)}, bf16[6,1152,128]{2,1,0:T(8,128)(2,1)}, u32[]{:S(2)}, u32[]{:S(2)}) collective-permute-start(bf16[6,1152,128]{2,1,0:T(8,128)(2,1)} %collective-permute-done.39.refs_4_), channel_id=1, source_target_pairs={{0,1},{1,0},{2,3},{3,2},{4,5},{5,4},{6,7},{7,6}} | collective-permute-start | bytes 5308424 | tf_op jit(solution)/shard_map/ppermute | solution.py:372
  650.8 54.4 %collective-permute-start.41 = (bf16[8,1152,128]{2,1,0:T(8,128)(2,1)}, bf16[8,1152,128]{2,1,0:T(8,128)(2,1)}, u32[]{:S(2)}, u32[]{:S(2)}) collective-permute-start(bf16[8,1152,128]{2,1,0:T(8,128)(2,1)} %get-tuple-element.982), channel_id=1, source_target_pairs={{0,2},{1,3},{2,0},{3,1},{4,6},{5,7},{6,4},{7,5}} | collective-permute-start | bytes 7077896 | tf_op jit(solution)/shard_map/ppermute | solution.py:372
  651.4 105.0 %collective-permute-start.42 = (bf16[8,1152,128]{2,1,0:T(8,128)(2,1)}, bf16[8,1152,128]{2,1,0:T(8,128)(2,1)}, u32[]{:S(2)}, u32[]{:S(2)}) collective-permute-start(bf16[8,1152,128]{2,1,0:T(8,128)(2,1)} %get-tuple-element.983), channel_id=1, source_target_pairs={{0,4},{1,5},{2,6},{3,7},{4,0},{5,1},{6,2},{7,3}} | collective-permute-start | bytes 7077896 | tf_op jit(solution)/shard_map/ppermute | solution.py:372
  673.3 83.1 %collective-permute-start.43 = (bf16[8,1152,128]{2,1,0:T(8,128)(2,1)}, bf16[8,1152,128]{2,1,0:T(8,128)(2,1)}, u32[]{:S(2)}, u32[]{:S(2)}) collective-permute-start(bf16[8,1152,128]{2,1,0:T(8,128)(2,1)} %get-tuple-element.984), channel_id=1, source_target_pairs={{0,6},{1,7},{2,4},{3,5},{4,2},{5,3},{6,0},{7,1}} | collective-permute-start | bytes 7077896 | tf_op jit(solution)/shard_map/ppermute | solution.py:372
  673.3 133.0 %collective-permute-start.19 = (bf16[8,1152,128]{2,1,0:T(8,128)(2,1)}, bf16[8,1152,128]{2,1,0:T(8,128)(2,1)}, u32[]{:S(2)}, u32[]{:S(2)}) collective-permute-start(bf16[8,1152,128]{2,1,0:T(8,128)(2,1)} %get-tuple-element.944), channel_id=1, source_target_pairs={{0,2},{1,3},{2,0},{3,1},{4,6},{5,7},{6,4},{7,5}} | collective-permute-start | bytes 7077896 | tf_op jit(solution)/shard_map/ppermute | solution.py:372
  674.7 182.1 %collective-permute-start.20 = (bf16[8,1152,128]{2,1,0:T(8,128)(2,1)}, bf16[8,1152,128]{2,1,0:T(8,128)(2,1)}, u32[]{:S(2)}, u32[]{:S(2)}) collective-permute-start(bf16[8,1152,128]{2,1,0:T(8,128)(2,1)} %get-tuple-element.945), channel_id=1, source_target_pairs={{0,4},{1,5},{2,6},{3,7},{4,0},{5,1},{6,2},{7,3}} | collective-permute-start | bytes 7077896 | tf_op jit(solution)/shard_map/ppermute | solution.py:372
  705.2 151.6 %collective-permute-start.21 = (bf16[8,1152,128]{2,1,0:T(8,128)(2,1)}, bf16[8,1152,128]{2,1,0:T(8,128)(2,1)}, u32[]{:S(2)}, u32[]{:S(2)}) collective-permute-start(bf16[8,1152,128]{2,1,0:T(8,128)(2,1)} %get-tuple-element.946), channel_id=1, source_target_pairs={{0,6},{1,7},{2,4},{3,5},{4,2},{5,3},{6,0},{7,1}} | collective-permute-start | bytes 7077896 | tf_op jit(solution)/shard_map/ppermute | solution.py:372
  756.4 134.1 %collective-permute-start.62 = (bf16[8,1152,128]{2,1,0:T(8,128)(2,1)S(1)}, bf16[8,1152,128]{2,1,0:T(8,128)(2,1)}, u32[]{:S(2)}, u32[]{:S(2)}) collective-permute-start(bf16[8,1152,128]{2,1,0:T(8,128)(2,1)S(1)} %copy-done.8), channel_id=1, source_target_pairs={{0,1},{1,0},{2,3},{3,2},{4,5},{5,4},{6,7},{7,6}} | collective-permute-start | bytes 7077896 | tf_op jit(solution)/shard_map/ppermute | solution.py:372
  756.4 134.2 %collective-permute-start.67 = (bf16[8,1152,128]{2,1,0:T(8,128)(2,1)}, bf16[8,1152,128]{2,1,0:T(8,128)(2,1)}, u32[]{:S(2)}, u32[]{:S(2)}) collective-permute-start(bf16[8,1152,128]{2,1,0:T(8,128)(2,1)} %collective-permute-done.16.refs_2_), channel_id=1, source_target_pairs={{0,1},{1,0},{2,3},{3,2},{4,5},{5,4},{6,7},{7,6}} | collective-permute-start | bytes 7077896 | tf_op jit(solution)/shard_map/ppermute | solution.py:372
  806.4 84.2 %collective-permute-start.68 = (bf16[8,1152,128]{2,1,0:T(8,128)(2,1)}, bf16[8,1152,128]{2,1,0:T(8,128)(2,1)}, u32[]{:S(2)}, u32[]{:S(2)}) collective-permute-start(bf16[8,1152,128]{2,1,0:T(8,128)(2,1)} %collective-permute-done.17.refs_4_), channel_id=1, source_target_pairs={{0,1},{1,0},{2,3},{3,2},{4,5},{5,4},{6,7},{7,6}} | collective-permute-start | bytes 7077896 | tf_op jit(solution)/shard_map/ppermute | solution.py:372
  890.6 56.3 %collective-permute-start.63 = (bf16[8,1152,128]{2,1,0:T(8,128)(2,1)}, bf16[8,1152,128]{2,1,0:T(8,128)(2,1)}, u32[]{:S(2)}, u32[]{:S(2)}) collective-permute-start(bf16[8,1152,128]{2,1,0:T(8,128)(2,1)} %collective-permute-done.41.refs_2_), channel_id=1, source_target_pairs={{0,1},{1,0},{2,3},{3,2},{4,5},{5,4},{6,7},{7,6}} | collective-permute-start | bytes 7077896 | tf_op jit(solution)/shard_map/ppermute | solution.py:372
  890.6 56.3 %collective-permute-start.64 = (bf16[8,1152,128]{2,1,0:T(8,128)(2,1)}, bf16[8,1152,128]{2,1,0:T(8,128)(2,1)}, u32[]{:S(2)}, u32[]{:S(2)}) collective-permute-start(bf16[8,1152,128]{2,1,0:T(8,128)(2,1)} %collective-permute-done.42.refs_4_), channel_id=1, source_target_pairs={{0,1},{1,0},{2,3},{3,2},{4,5},{5,4},{6,7},{7,6}} | collective-permute-start | bytes 7077896 | tf_op jit(solution)/shard_map/ppermute | solution.py:372
  891.1 51.3 %collective-permute-start.25 = (bf16[4,1152,128]{2,1,0:T(8,128)(2,1)}, bf16[4,1152,128]{2,1,0:T(8,128)(2,1)}, u32[]{:S(2)}, u32[]{:S(2)}) collective-permute-start(bf16[4,1152,128]{2,1,0:T(8,128)(2,1)} %get-tuple-element.949), channel_id=1, source_target_pairs={{0,4},{1,5},{2,6},{3,7},{4,0},{5,1},{6,2},{7,3}} | collective-permute-start | bytes 3538952 | tf_op jit(solution)/shard_map/ppermute | solution.py:372
  891.1 51.3 %collective-permute-start.27 = (bf16[4,1152,128]{2,1,0:T(8,128)(2,1)}, bf16[4,1152,128]{2,1,0:T(8,128)(2,1)S(1)}, u32[]{:S(2)}, u32[]{:S(2)}) collective-permute-start(bf16[4,1152,128]{2,1,0:T(8,128)(2,1)} %get-tuple-element.950), channel_id=1, source_target_pairs={{0,6},{1,7},{2,4},{3,5}} | collective-permute-start | bytes 3538952 | tf_op jit(solution)/shard_map/ppermute | solution.py:372
  942.4 54.5 %collective-permute-start.44 = (bf16[8,1152,128]{2,1,0:T(8,128)(2,1)}, bf16[8,1152,128]{2,1,0:T(8,128)(2,1)}, u32[]{:S(2)}, u32[]{:S(2)}) collective-permute-start(bf16[8,1152,128]{2,1,0:T(8,128)(2,1)} %get-tuple-element.985), channel_id=1, source_target_pairs={{0,2},{1,3},{2,0},{3,1},{4,6},{5,7},{6,4},{7,5}} | collective-permute-start | bytes 7077896 | tf_op jit(solution)/shard_map/ppermute | solution.py:372
  944.4 105.0 %collective-permute-start.45 = (bf16[8,1152,128]{2,1,0:T(8,128)(2,1)}, bf16[8,1152,128]{2,1,0:T(8,128)(2,1)}, u32[]{:S(2)}, u32[]{:S(2)}) collective-permute-start(bf16[8,1152,128]{2,1,0:T(8,128)(2,1)} %get-tuple-element.986), channel_id=1, source_target_pairs={{0,4},{1,5},{2,6},{3,7},{4,0},{5,1},{6,2},{7,3}} | collective-permute-start | bytes 7077896 | tf_op jit(solution)/shard_map/ppermute | solution.py:372
  946.9 102.5 %collective-permute-start.46 = (bf16[8,1152,128]{2,1,0:T(8,128)(2,1)}, bf16[8,1152,128]{2,1,0:T(8,128)(2,1)}, u32[]{:S(2)}, u32[]{:S(2)}) collective-permute-start(bf16[8,1152,128]{2,1,0:T(8,128)(2,1)} %get-tuple-element.987), channel_id=1, source_target_pairs={{0,6},{1,7},{2,4},{3,5},{4,2},{5,3},{6,0},{7,1}} | collective-permute-start | bytes 7077896 | tf_op jit(solution)/shard_map/ppermute | solution.py:372
  946.9 103.0 %collective-permute-start.54 = (bf16[8,1152,128]{2,1,0:T(8,128)(2,1)}, bf16[8,1152,128]{2,1,0:T(8,128)(2,1)}, u32[]{:S(2)}, u32[]{:S(2)}) collective-permute-start(bf16[8,1152,128]{2,1,0:T(8,128)(2,1)} %get-tuple-element.992.refs_0_), channel_id=1, source_target_pairs={{0,1},{1,0},{2,3},{3,2},{4,5},{5,4},{6,7},{7,6}} | collective-permute-start | bytes 7077896 | tf_op jit(solution)/shard_map/ppermute | solution.py:372
  947.3 110.8 %collective-permute-start.59 = (bf16[8,1152,128]{2,1,0:T(8,128)(2,1)}, bf16[8,1152,128]{2,1,0:T(8,128)(2,1)}, u32[]{:S(2)}, u32[]{:S(2)}) collective-permute-start(bf16[8,1152,128]{2,1,0:T(8,128)(2,1)} %collective-permute-done.19.refs_2_), channel_id=1, source_target_pairs={{0,1},{1,0},{2,3},{3,2},{4,5},{5,4},{6,7},{7,6}} | collective-permute-start | bytes 7077896 | tf_op jit(solution)/shard_map/ppermute | solution.py:372
  996.9 63.7 %collective-permute-start.60 = (bf16[8,1152,128]{2,1,0:T(8,128)(2,1)}, bf16[8,1152,128]{2,1,0:T(8,128)(2,1)}, u32[]{:S(2)}, u32[]{:S(2)}) collective-permute-start(bf16[8,1152,128]{2,1,0:T(8,128)(2,1)} %collective-permute-done.20.refs_4_), channel_id=1, source_target_pairs={{0,1},{1,0},{2,3},{3,2},{4,5},{5,4},{6,7},{7,6}} | collective-permute-start | bytes 7077896 | tf_op jit(solution)/shard_map/ppermute | solution.py:372
  1057.6 35.5 %collective-permute-start.56 = (bf16[8,1152,128]{2,1,0:T(8,128)(2,1)}, bf16[8,1152,128]{2,1,0:T(8,128)(2,1)}, u32[]{:S(2)}, u32[]{:S(2)}) collective-permute-start(bf16[8,1152,128]{2,1,0:T(8,128)(2,1)} %collective-permute-done.45.refs_4_), channel_id=1, source_target_pairs={{0,1},{1,0},{2,3},{3,2},{4,5},{5,4},{6,7},{7,6}} | collective-permute-start | bytes 7077896 | tf_op jit(solution)/shard_map/ppermute | solution.py:372
  1058.1 35.1 %collective-permute-start.57 = (bf16[8,1152,128]{2,1,0:T(8,128)(2,1)}, bf16[8,1152,128]{2,1,0:T(8,128)(2,1)}, u32[]{:S(2)}, u32[]{:S(2)}) collective-permute-start(bf16[8,1152,128]{2,1,0:T(8,128)(2,1)} %collective-permute-done.46.refs_6_), channel_id=1, source_target_pairs={{0,1},{1,0},{2,3},{3,2},{4,5},{5,4},{6,7},{7,6}} | collective-permute-start | bytes 7077896 | tf_op jit(solution)/shard_map/ppermute | solution.py:372
  1076.5 216.6 %collective-permute-start.28 = (bf16[4,1152,128]{2,1,0:T(8,128)(2,1)}, bf16[4,1152,128]{2,1,0:T(8,128)(2,1)}, u32[]{:S(2)}, u32[]{:S(2)}) collective-permute-start(bf16[4,1152,128]{2,1,0:T(8,128)(2,1)} %copy-done.18), channel_id=1, source_target_pairs={{0,1},{1,0},{2,3},{3,2},{4,5},{5,4},{6,7},{7,6}} | collective-permute-start | bytes 3538952 | tf_op jit(solution)/shard_map/ppermute | solution.py:372
  1092.6 200.5 %collective-permute-start.47 = (bf16[2,1152,128]{2,1,0:T(8,128)(2,1)}, bf16[2,1152,128]{2,1,0:T(8,128)(2,1)}, u32[]{:S(2)}, u32[]{:S(2)}) collective-permute-start(bf16[2,1152,128]{2,1,0:T(8,128)(2,1)} %get-tuple-element.988.refs_8_), channel_id=1, source_target_pairs={{0,1},{1,0},{2,3},{3,2},{4,5},{5,4},{6,7},{7,6}} | collective-permute-start | bytes 1769480 | tf_op jit(solution)/shard_map/ppermute | solution.py:372
  1092.6 200.6 %collective-permute-start.49 = (bf16[2,1152,128]{2,1,0:T(8,128)(2,1)}, bf16[2,1152,128]{2,1,0:T(8,128)(2,1)}, u32[]{:S(2)}, u32[]{:S(2)}) collective-permute-start(bf16[2,1152,128]{2,1,0:T(8,128)(2,1)} %collective-permute-done.48.refs_10_), channel_id=1, source_target_pairs={{0,1},{1,0},{2,3},{3,2},{4,5},{5,4},{6,7},{7,6}} | collective-permute-start | bytes 1769480 | tf_op jit(solution)/shard_map/ppermute | solution.py:372
  1093.1 200.1 %collective-permute-start.51 = (bf16[2,1152,128]{2,1,0:T(8,128)(2,1)}, bf16[2,1152,128]{2,1,0:T(8,128)(2,1)}, u32[]{:S(2)}, u32[]{:S(2)}) collective-permute-start(bf16[2,1152,128]{2,1,0:T(8,128)(2,1)} %collective-permute-done.50.refs_12_), channel_id=1, source_target_pairs={{0,1},{1,0},{2,3},{3,2},{4,5},{5,4},{6,7},{7,6}} | collective-permute-start | bytes 1769480 | tf_op jit(solution)/shard_map/ppermute | solution.py:372
  1093.2 200.0 %collective-permute-start.53 = (bf16[2,1152,128]{2,1,0:T(8,128)(2,1)}, bf16[2,1152,128]{2,1,0:T(8,128)(2,1)}, u32[]{:S(2)}, u32[]{:S(2)}) collective-permute-start(bf16[2,1152,128]{2,1,0:T(8,128)(2,1)} %collective-permute-done.52.refs_14_), channel_id=1, source_target_pairs={{0,1},{1,0},{2,3},{3,2},{4,5},{5,4},{6,7},{7,6}} | collective-permute-start | bytes 1769480 | tf_op jit(solution)/shard_map/ppermute | solution.py:372
  (77 other events, 3079.1 us)

commit v2 on v1

--- a/solution.py
+++ b/solution.py
@@ -71,7 +71,9 @@
 
 
 PLAN = Plan(
-    [direct(2), direct(4), direct(6), relay(6), no_chip1(6), relay(4), no_3(6)] + [direct(8)] * 4 + [end(4), end(2)]
+    [direct(2), direct(4), direct(6), relay(6), no_chip1(6), relay(4), no_3(6)]
+    + [direct(8)] * 3
+    + [direct(6), end(4), end(2), end(2)]
 )
 EXTRA = 4
 
@@ -148,7 +150,7 @@
     )(*tabs, c_raw, k_t, gain, cos_t, sin_t, *after)
 
 
-def attend(chunk, start, first, counts, codes, parts, q_lat, q_rope_t, caches, state):
+def attend(chunk, start, first, last, counts, codes, parts, q_lat, q_rope_t, caches, state):
     total = len(parts)
 
     def kernel(count_ref, code_ref, *refs):
@@ -241,6 +243,15 @@
         def _():
             drain((steps + 1) % 2)
 
+        if last:
+            o_ref = outs[3]
+
+            def finish(r, _):
+                o_ref[r] = (st_ref[r, :, :RANK] / st_ref[r, :, RANK : RANK + 1]).astype(jnp.bfloat16)
+                return 0
+
+            lax.fori_loop(0, REQ, finish, 0)
+
     smem, vmem, anywhere = (pl.BlockSpec(memory_space=m) for m in (pltpu.SMEM, pltpu.VMEM, pl.ANY))
     state_shape = (REQ, HEADS, RANK + 256)
     in_specs = [smem] * 2 + [anywhere] * total + [vmem] * 2 + [anywhere] * 2
@@ -252,6 +263,9 @@
         operands.append(state)
     out_specs = [anywhere, anywhere, vmem]
     out_shape = [jax.ShapeDtypeStruct(c.shape, c.dtype) for c in caches] + [jax.ShapeDtypeStruct(state_shape, jnp.float32)]
+    if last:
+        out_specs.append(vmem)
+        out_shape.append(jax.ShapeDtypeStruct((REQ, HEADS, RANK), jnp.bfloat16))
     return pl.pallas_call(
         kernel,
         in_specs=in_specs,
@@ -406,11 +420,13 @@
             near, over, far = landed[c]
             if plan.chunks[c][1] == "relay":
                 far = send(far, pairs(LOW, 2) + pairs(UP, 1))
+                far, landed[c + 1] = lax.optimization_barrier((far, landed[c + 1]))
             parts += [owns[c], twins[c]]
             for x in (near, over, far):
                 parts += [x, send(x, pairs(ALL, 1))]
-        *caches, state = attend(number, int(first[number]), number == 0, counts, codes, parts, q_lat, q_rope_t, caches, state)
-    return caches[0], caches[1], state
+        got = attend(number, int(first[number]), number == 0, number == len(runs) - 1, counts, codes, parts, q_lat, q_rope_t, caches, state)
+        caches, state = got[:2], got[2]
+    return got
 
 
 def run_extra(step, me, left, weights, q_lat, q_rope_t, caches, state):
@@ -425,7 +441,7 @@
     for q, x in enumerate(staged):
         x = lax.ppermute(x, "x", pairs(ALL, 2 * q)) if q else x
         parts += [x, lax.ppermute(x, "x", pairs(ALL, 1))]
-    return attend(0, 0, False, counts, codes, parts, q_lat, q_rope_t, caches, state)
+    return attend(0, 0, False, True, counts, codes, parts, q_lat, q_rope_t, caches, state)
 
 
 def local_step(c_raw, k_raw, norm_gain, rope_cos, rope_sin, seq_lens, q_lat, q_rope):
@@ -434,17 +450,16 @@
     own_lens = lax.dynamic_slice_in_dim(seq_lens, me * REQ, REQ)
     weights = (c_raw, jnp.swapaxes(k_raw, 1, 2), norm_gain[None, :], rope_cos.T, rope_sin.T)
     q_rope_t = jnp.swapaxes(q_rope, 1, 2)
-    c_cache, k_cache_t, state = run_plan(me, left, own_lens, weights, q_lat, q_rope_t)
+    done = run_plan(me, left, own_lens, weights, q_lat, q_rope_t)
     need = jnp.sum((left > 0).astype(jnp.int32), axis=-1)
     cap = np.stack([[PLAN.cap[s, (s // 2) ^ chip] for chip in range(CHIPS)] for s in range(N)])
     steps = (jnp.maximum(jnp.max(need - jnp.asarray(cap)), 0) + EXTRA - 1) // EXTRA
 
     def body(carry):
-        step, *caches, state = carry
-        return step + 1, *run_extra(step, me, left, weights, q_lat, q_rope_t, caches, state)
-
-    _, c_cache, k_cache_t, state = lax.while_loop(lambda carry: carry[0] < steps, body, (jnp.int32(0), c_cache, k_cache_t, state))
-    o_lat = (state[:, :, :RANK] / state[:, :, RANK : RANK + 1]).astype(jnp.bfloat16)
+        step, c_cache, k_cache_t, state, _ = carry
+        return step + 1, *run_extra(step, me, left, weights, q_lat, q_rope_t, (c_cache, k_cache_t), state)
+
+    _, c_cache, k_cache_t, _, o_lat = lax.while_loop(lambda carry: carry[0] < steps, body, (jnp.int32(0), *done))
     return c_cache, jnp.swapaxes(k_cache_t, 1, 2), o_lat
 
 

time: 1330 us -> 1300 us (0.977)
  waiting for transfers between devices: 811 us -> 708 us
  starting transfers between devices: 64.5 us -> 109 us
  local copies, waits for them, and re-layouts: 19.7 us -> 37 us
    ppermute x93 -> x100, waiting for transfers between devices: 811 us -> 708 us  [send(): return lax.ppermute(x, 'x', pairs)]
    ppermute x93 -> x100, starting transfers between devices: 64.5 us -> 109 us  [send(): return lax.ppermute(x, 'x', pairs)]
    concatenate x14 -> x15, local copies, waits for them, and re-layouts: 1.13 us -> 17.4 us  [attend_tables(): jnp.concatenate([code[:, s:s + w].reshape(-1) for w, s in zip(widths, sta...]
    pallas_call x12 -> x13, Pallas kernels: 190 us -> 198 us  [attend(): pl.pallas_call(kernel, in_specs=in_specs, out_specs=out_specs, out_shape=...]
    pallas_call x13 -> x14, Pallas kernels: 202 us -> 203 us  [norm_pack(): pl.pallas_call(kernel, grid_spec=grid_spec, out_shape=[jax.ShapeDtypeStru...]
  transfers between devices with their start and end apart: 93 -> 100, of which waited for: 33 -> 35; matrix products, arithmetic and copies ran while one was open for 1% -> 3% of each run, Pallas kernels for 30% -> 31%
where the time goes in v2:
time: 1300 us; the launch traced here: 1280 us
  waiting for transfers between devices  708 us (54%)
  Pallas kernels  416 us (32%)
  starting transfers between devices  109 us (8%)
  local copies, waits for them, and re-layouts  37 us (3%)
    ppermute x100, waiting for transfers between devices, send(): return lax.ppermute(x, 'x', pairs)  708 us
    pallas_call x14, Pallas kernels, norm_pack(): pl.pallas_call(kernel, grid_spec=grid_spec, out_shape=[jax.ShapeDtypeStru...  203 us
    pallas_call x13, Pallas kernels, attend(): pl.pallas_call(kernel, in_specs=in_specs, out_specs=out_specs, out_shape=...  198 us
    ppermute x100, starting transfers between devices, send(): return lax.ppermute(x, 'x', pairs)  109 us
  transfers between devices with their start and end apart: 100, of which 35 were waited for; matrix products, arithmetic and copies ran while one was open for 3% of the time, Pallas kernels for 31%

profile of v2, /device:TPU:0, one launch (start us, length us, event | category | flops | bytes accessed | tf_op | source)
XLA Modules:
  0.0 1282.3 jit_solution(7775553236989141133)
XLA Ops:
  6.8 6.8 norm_pack.21
  13.6 3.3 collective-permute-start.7
  17.0 11.7 norm_pack.22
  34.7 16.7 %norm_pack.23 = (bf16[6,1152,128]{2,1,0:T(8,128)(2,1)}, bf16[6,1152,128]{2,1,0:T(8,128)(2,1)}, bf16[6,1152,128]{2,1,0:T(8,128)(2,1)}, bf16[6,1152,128]{2,1,0:T(8,128)(2,1)}) custom-call(s32[288]{0:T(512)} %get-tuple-element.1398.req_ref, s32[288]{0:T(512)} %get-tuple-element.1397.unit_ref, s32[288]{0:T(512)} %reshape.794.ok_ref, ...), custom_call_target="tpu_custom_call" | custom-call | flops 600000000 | bytes 14155776 | tf_op jit(solution)/shard_map/norm_pack/pallas_call | solution.py:144
  51.4 55.6 %collective-permute-done.8.refs_4_ = bf16[2,1152,128]{2,1,0:T(8,128)(2,1)S(1)} collective-permute-done((bf16[2,1152,128]{2,1,0:T(8,128)(2,1)}, bf16[2,1152,128]{2,1,0:T(8,128)(2,1)S(1)}, u32[]{:S(2)}, u32[]{:S(2)}) %collective-permute-start.8) | collective-permute-done | bytes 589856 | tf_op jit(solution)/shard_map/ppermute | solution.py:386
  108.9 16.6 %norm_pack.24 = (bf16[6,1152,128]{2,1,0:T(8,128)(2,1)}, bf16[6,1152,128]{2,1,0:T(8,128)(2,1)}, bf16[6,1152,128]{2,1,0:T(8,128)(2,1)}, bf16[6,1152,128]{2,1,0:T(8,128)(2,1)}) custom-call(s32[288]{0:T(512)} %get-tuple-element.1398.req_ref, s32[288]{0:T(512)} %get-tuple-element.1397.unit_ref, s32[288]{0:T(512)} %reshape.794.ok_ref, ...), custom_call_target="tpu_custom_call" | custom-call | flops 600000000 | bytes 14155776 | tf_op jit(solution)/shard_map/norm_pack/pallas_call | solution.py:144
  133.7 34.4 %collective-permute-done.10.refs_2_ = bf16[6,1152,128]{2,1,0:T(8,128)(2,1)} collective-permute-done((bf16[6,1152,128]{2,1,0:T(8,128)(2,1)}, bf16[6,1152,128]{2,1,0:T(8,128)(2,1)}, u32[]{:S(2)}, u32[]{:S(2)}) %collective-permute-start.10) | collective-permute-done | bytes 1769504 | tf_op jit(solution)/shard_map/ppermute | solution.py:386
  168.1 39.6 %collective-permute-done.11.refs_4_ = bf16[6,1152,128]{2,1,0:T(8,128)(2,1)} collective-permute-done((bf16[6,1152,128]{2,1,0:T(8,128)(2,1)}, bf16[6,1152,128]{2,1,0:T(8,128)(2,1)}, u32[]{:S(2)}, u32[]{:S(2)}) %collective-permute-start.11) | collective-permute-done | bytes 1769504 | tf_op jit(solution)/shard_map/ppermute | solution.py:386
  207.7 16.6 %norm_pack.25 = (bf16[6,1152,128]{2,1,0:T(8,128)(2,1)}, bf16[6,1152,128]{2,1,0:T(8,128)(2,1)}, bf16[6,1152,128]{2,1,0:T(8,128)(2,1)}, bf16[6,1152,128]{2,1,0:T(8,128)(2,1)}) custom-call(s32[288]{0:T(512)} %get-tuple-element.1398.req_ref, s32[288]{0:T(512)} %get-tuple-element.1397.unit_ref, s32[288]{0:T(512)} %reshape.794.ok_ref, ...), custom_call_target="tpu_custom_call" | custom-call | flops 600000000 | bytes 14155776 | tf_op jit(solution)/shard_map/norm_pack/pallas_call | solution.py:144
  224.9 18.4 %collective-permute-done.35.refs_2_ = bf16[6,1152,128]{2,1,0:T(8,128)(2,1)} collective-permute-done((bf16[6,1152,128]{2,1,0:T(8,128)(2,1)}, bf16[6,1152,128]{2,1,0:T(8,128)(2,1)}, u32[]{:S(2)}, u32[]{:S(2)}) %collective-permute-start.35) | collective-permute-done | bytes 1769504 | tf_op jit(solution)/shard_map/ppermute | solution.py:386
  245.6 37.0 %collective-permute-done.37 = bf16[6,1152,128]{2,1,0:T(8,128)(2,1)} collective-permute-done((bf16[6,1152,128]{2,1,0:T(8,128)(2,1)}, bf16[6,1152,128]{2,1,0:T(8,128)(2,1)}, u32[]{:S(2)}, u32[]{:S(2)}) %collective-permute-start.37) | collective-permute-done | bytes 1769504 | tf_op jit(solution)/shard_map/ppermute | solution.py:386
  282.9 3.3 collective-permute-start.14
  286.3 5.0 collective-permute-start.15
  291.3 11.6 norm_pack.26
  303.0 21.3 %collective-permute-done.13.refs_2_ = bf16[6,1152,128]{2,1,0:T(8,128)(2,1)S(1)} collective-permute-done((bf16[6,1152,128]{2,1,0:T(8,128)(2,1)}, bf16[6,1152,128]{2,1,0:T(8,128)(2,1)S(1)}, u32[]{:S(2)}, u32[]{:S(2)}) %collective-permute-start.13) | collective-permute-done | bytes 1769504 | tf_op jit(solution)/shard_map/ppermute | solution.py:386
  324.6 40.0 %collective-permute-done.14.refs_4_ = bf16[6,1152,128]{2,1,0:T(8,128)(2,1)} collective-permute-done((bf16[6,1152,128]{2,1,0:T(8,128)(2,1)}, bf16[6,1152,128]{2,1,0:T(8,128)(2,1)}, u32[]{:S(2)}, u32[]{:S(2)}) %collective-permute-start.14) | collective-permute-done | bytes 1769504 | tf_op jit(solution)/shard_map/ppermute | solution.py:386
  365.1 18.6 %collective-permute-done.38.refs_2_ = bf16[4,1152,128]{2,1,0:T(8,128)(2,1)S(1)} collective-permute-done((bf16[4,1152,128]{2,1,0:T(8,128)(2,1)}, bf16[4,1152,128]{2,1,0:T(8,128)(2,1)S(1)}, u32[]{:S(2)}, u32[]{:S(2)}) %collective-permute-start.38) | collective-permute-done | bytes 1179680 | tf_op jit(solution)/shard_map/ppermute | solution.py:386
  383.7 6.1 collective-permute-done.39.refs_4_
  389.8 16.6 %norm_pack.27 = (bf16[6,1152,128]{2,1,0:T(8,128)(2,1)}, bf16[6,1152,128]{2,1,0:T(8,128)(2,1)}, bf16[6,1152,128]{2,1,0:T(8,128)(2,1)}, bf16[6,1152,128]{2,1,0:T(8,128)(2,1)}) custom-call(s32[288]{0:T(512)} %get-tuple-element.1398.req_ref, s32[288]{0:T(512)} %get-tuple-element.1397.unit_ref, s32[288]{0:T(512)} %reshape.794.ok_ref, ...), custom_call_target="tpu_custom_call" | custom-call | flops 600000000 | bytes 14155776 | tf_op jit(solution)/shard_map/norm_pack/pallas_call | solution.py:144
  406.4 7.1 collective-permute-done.40
  414.7 21.6 %norm_pack.28 = (bf16[8,1152,128]{2,1,0:T(8,128)(2,1)}, bf16[8,1152,128]{2,1,0:T(8,128)(2,1)}, bf16[8,1152,128]{2,1,0:T(8,128)(2,1)}, bf16[8,1152,128]{2,1,0:T(8,128)(2,1)}) custom-call(s32[288]{0:T(512)} %get-tuple-element.1398.req_ref, s32[288]{0:T(512)} %get-tuple-element.1397.unit_ref, s32[288]{0:T(512)} %reshape.794.ok_ref, ...), custom_call_target="tpu_custom_call" | custom-call | flops 800000000 | bytes 18874368 | tf_op jit(solution)/shard_map/norm_pack/pallas_call | solution.py:144
  439.6 40.5 %collective-permute-start.18 = (bf16[6,1152,128]{2,1,0:T(8,128)(2,1)}, bf16[6,1152,128]{2,1,0:T(8,128)(2,1)S(1)}, u32[]{:S(2)}, u32[]{:S(2)}) collective-permute-start(bf16[6,1152,128]{2,1,0:T(8,128)(2,1)} %get-tuple-element.989), channel_id=1, source_target_pairs={{0,6},{1,7},{2,4},{4,2},{5,3},{6,0},{7,1}} | collective-permute-start | bytes 5308424 | tf_op jit(solution)/shard_map/ppermute | solution.py:386
  480.7 36.7 %collective-permute-done.17.refs_4_ = bf16[6,1152,128]{2,1,0:T(8,128)(2,1)S(1)} collective-permute-done((bf16[6,1152,128]{2,1,0:T(8,128)(2,1)}, bf16[6,1152,128]{2,1,0:T(8,128)(2,1)S(1)}, u32[]{:S(2)}, u32[]{:S(2)}) %collective-permute-start.17) | collective-permute-done | bytes 1769504 | tf_op jit(solution)/shard_map/ppermute | solution.py:386
  521.6 21.6 %norm_pack.29 = (bf16[8,1152,128]{2,1,0:T(8,128)(2,1)}, bf16[8,1152,128]{2,1,0:T(8,128)(2,1)}, bf16[8,1152,128]{2,1,0:T(8,128)(2,1)}, bf16[8,1152,128]{2,1,0:T(8,128)(2,1)}) custom-call(s32[288]{0:T(512)} %get-tuple-element.1398.req_ref, s32[288]{0:T(512)} %get-tuple-element.1397.unit_ref, s32[288]{0:T(512)} %reshape.794.ok_ref, ...), custom_call_target="tpu_custom_call" | custom-call | flops 800000000 | bytes 18874368 | tf_op jit(solution)/shard_map/norm_pack/pallas_call | solution.py:144
  543.6 28.3 %collective-permute-done.41.refs_2_ = bf16[8,1152,128]{2,1,0:T(8,128)(2,1)} collective-permute-done((bf16[8,1152,128]{2,1,0:T(8,128)(2,1)}, bf16[8,1152,128]{2,1,0:T(8,128)(2,1)}, u32[]{:S(2)}, u32[]{:S(2)}) %collective-permute-start.41) | collective-permute-done | bytes 2359328 | tf_op jit(solution)/shard_map/ppermute | solution.py:386
  571.9 50.6 %collective-permute-done.42.refs_4_ = bf16[8,1152,128]{2,1,0:T(8,128)(2,1)} collective-permute-done((bf16[8,1152,128]{2,1,0:T(8,128)(2,1)}, bf16[8,1152,128]{2,1,0:T(8,128)(2,1)}, u32[]{:S(2)}, u32[]{:S(2)}) %collective-permute-start.42) | collective-permute-done | bytes 2359328 | tf_op jit(solution)/shard_map/ppermute | solution.py:386
  624.3 2.5 collective-permute-done.85.refs_7_
  630.3 21.6 %norm_pack.30 = (bf16[8,1152,128]{2,1,0:T(8,128)(2,1)}, bf16[8,1152,128]{2,1,0:T(8,128)(2,1)}, bf16[8,1152,128]{2,1,0:T(8,128)(2,1)}, bf16[8,1152,128]{2,1,0:T(8,128)(2,1)}) custom-call(s32[288]{0:T(512)} %get-tuple-element.1398.req_ref, s32[288]{0:T(512)} %get-tuple-element.1397.unit_ref, s32[288]{0:T(512)} %reshape.794.ok_ref, ...), custom_call_target="tpu_custom_call" | custom-call | flops 800000000 | bytes 18874368 | tf_op jit(solution)/shard_map/norm_pack/pallas_call | solution.py:144
  652.5 24.5 %collective-permute-done.19.refs_2_ = bf16[8,1152,128]{2,1,0:T(8,128)(2,1)} collective-permute-done((bf16[8,1152,128]{2,1,0:T(8,128)(2,1)}, bf16[8,1152,128]{2,1,0:T(8,128)(2,1)}, u32[]{:S(2)}, u32[]{:S(2)}) %collective-permute-start.19) | collective-permute-done | bytes 2359328 | tf_op jit(solution)/shard_map/ppermute | solution.py:386
  677.0 54.0 %collective-permute-done.20.refs_4_ = bf16[8,1152,128]{2,1,0:T(8,128)(2,1)} collective-permute-done((bf16[8,1152,128]{2,1,0:T(8,128)(2,1)}, bf16[8,1152,128]{2,1,0:T(8,128)(2,1)}, u32[]{:S(2)}, u32[]{:S(2)}) %collective-permute-start.20) | collective-permute-done | bytes 2359328 | tf_op jit(solution)/shard_map/ppermute | solution.py:386
  735.0 16.6 %norm_pack.31 = (bf16[6,1152,128]{2,1,0:T(8,128)(2,1)}, bf16[6,1152,128]{2,1,0:T(8,128)(2,1)}, bf16[6,1152,128]{2,1,0:T(8,128)(2,1)}, bf16[6,1152,128]{2,1,0:T(8,128)(2,1)}) custom-call(s32[288]{0:T(512)} %get-tuple-element.1398.req_ref, s32[288]{0:T(512)} %get-tuple-element.1397.unit_ref, s32[288]{0:T(512)} %reshape.794.ok_ref, ...), custom_call_target="tpu_custom_call" | custom-call | flops 600000000 | bytes 14155776 | tf_op jit(solution)/shard_map/norm_pack/pallas_call | solution.py:144
  751.6 33.8 %collective-permute-done.44.refs_2_ = bf16[8,1152,128]{2,1,0:T(8,128)(2,1)} collective-permute-done((bf16[8,1152,128]{2,1,0:T(8,128)(2,1)}, bf16[8,1152,128]{2,1,0:T(8,128)(2,1)}, u32[]{:S(2)}, u32[]{:S(2)}) %collective-permute-start.44) | collective-permute-done | bytes 2359328 | tf_op jit(solution)/shard_map/ppermute | solution.py:386
  786.2 48.6 %collective-permute-done.45.refs_4_ = bf16[8,1152,128]{2,1,0:T(8,128)(2,1)} collective-permute-done((bf16[8,1152,128]{2,1,0:T(8,128)(2,1)}, bf16[8,1152,128]{2,1,0:T(8,128)(2,1)}, u32[]{:S(2)}, u32[]{:S(2)}) %collective-permute-start.45) | collective-permute-done | bytes 2359328 | tf_op jit(solution)/shard_map/ppermute | solution.py:386
  835.7 2.6 collective-permute-start.24
  838.3 11.6 norm_pack.32
  850.0 23.9 %collective-permute-done.22.refs_2_ = bf16[6,1152,128]{2,1,0:T(8,128)(2,1)} collective-permute-done((bf16[6,1152,128]{2,1,0:T(8,128)(2,1)}, bf16[6,1152,128]{2,1,0:T(8,128)(2,1)}, u32[]{:S(2)}, u32[]{:S(2)}) %collective-permute-start.22) | collective-permute-done | bytes 1769504 | tf_op jit(solution)/shard_map/ppermute | solution.py:386
  873.9 2.5 collective-permute-start.49
  876.4 38.1 %collective-permute-done.23.refs_4_ = bf16[6,1152,128]{2,1,0:T(8,128)(2,1)} collective-permute-done((bf16[6,1152,128]{2,1,0:T(8,128)(2,1)}, bf16[6,1152,128]{2,1,0:T(8,128)(2,1)}, u32[]{:S(2)}, u32[]{:S(2)}) %collective-permute-start.23) | collective-permute-done | bytes 1769504 | tf_op jit(solution)/shard_map/ppermute | solution.py:386
  915.0 22.1 %collective-permute-done.47.refs_2_ = bf16[4,1152,128]{2,1,0:T(8,128)(2,1)S(1)} collective-permute-done((bf16[4,1152,128]{2,1,0:T(8,128)(2,1)}, bf16[4,1152,128]{2,1,0:T(8,128)(2,1)S(1)}, u32[]{:S(2)}, u32[]{:S(2)}) %collective-permute-start.47) | collective-permute-done | bytes 1179680 | tf_op jit(solution)/shard_map/ppermute | solution.py:386
  938.2 21.0 %collective-permute-done.49.refs_6_ = bf16[4,1152,128]{2,1,0:T(8,128)(2,1)S(1)} collective-permute-done((bf16[4,1152,128]{2,1,0:T(8,128)(2,1)}, bf16[4,1152,128]{2,1,0:T(8,128)(2,1)S(1)}, u32[]{:S(2)}, u32[]{:S(2)}) %collective-permute-start.49) | collective-permute-done | bytes 1179680 | tf_op jit(solution)/shard_map/ppermute | solution.py:386
  960.1 6.6 norm_pack.33
  966.8 6.6 norm_pack.34
  973.6 6.2 collective-permute-start.55
  979.8 10.1 collective-permute-done.51.refs_10_
  990.7 4.9 collective-permute-done.53.refs_12_
  996.5 3.7 collective-permute-done.55.refs_14_
  1000.2 3.9 collective-permute-start.28
  1006.5 8.9 collective-permute-done.26.refs_2_
  1015.4 10.7 collective-permute-done.28.refs_4_
  1059.0 14.9 %blank.1 = (bf16[12,6144,512]{2,1,0:T(8,128)(2,1)}, bf16[12,64,6144]{2,1,0:T(8,128)(2,1)}) custom-call(s32[12]{0:T(128)} %dynamic_slice.22.len_ref), custom_call_target="tpu_custom_call" | custom-call | flops 400000000 | bytes 85000000 | tf_op jit(solution)/shard_map/blank/pallas_call | solution.py:310
  1073.9 3.6 collective-permute-start.52
  1083.3 7.7 attend.20
  1091.1 15.5 %attend.21 = (bf16[12,6144,512]{2,1,0:T(8,128)(2,1)}, bf16[12,64,6144]{2,1,0:T(8,128)(2,1)}, f32[12,128,768]{2,1,0:T(8,128)}) custom-call(s32[13]{0:T(128)} %convert_reduce_fusion.12.count_ref, s32[576]{0:T(1024)} %select_reduce_fusion.2.code_ref, bf16[4,1152,128]{2,1,0:T(8,128)(2,1)} %get-tuple-element.948.refs_0_, ...), custom_call_target="tpu_custom_call", output_to_operand_aliasing={{0}: (12, {}), {1}: (13, {})} | custom-call | flops 200000000 | bytes 4718592 | tf_op jit(solution)/shard_map/attend/pallas_call | solution.py:269
  1106.6 21.7 %attend.22 = (bf16[12,6144,512]{2,1,0:T(8,128)(2,1)}, bf16[12,64,6144]{2,1,0:T(8,128)(2,1)}, f32[12,128,768]{2,1,0:T(8,128)}) custom-call(s32[13]{0:T(128)} %convert_reduce_fusion.12.count_ref, s32[576]{0:T(1024)} %select_reduce_fusion.2.code_ref, bf16[6,1152,128]{2,1,0:T(8,128)(2,1)} %get-tuple-element.1085.refs_0_, ...), custom_call_target="tpu_custom_call", output_to_operand_aliasing={{0}: (12, {}), {1}: (13, {})} | custom-call | flops 200000000 | bytes 4718592 | tf_op jit(solution)/shard_map/attend/pallas_call | solution.py:269
  1128.3 20.3 %attend.23 = (bf16[12,6144,512]{2,1,0:T(8,128)(2,1)}, bf16[12,64,6144]{2,1,0:T(8,128)(2,1)}, f32[12,128,768]{2,1,0:T(8,128)}) custom-call(s32[13]{0:T(128)} %convert_reduce_fusion.12.count_ref, s32[576]{0:T(1024)} %select_reduce_fusion.2.code_ref, bf16[6,1152,128]{2,1,0:T(8,128)(2,1)} %get-tuple-element.1081.refs_0_, ...), custom_call_target="tpu_custom_call", output_to_operand_aliasing={{0}: (12, {}), {1}: (13, {})} | custom-call | flops 200000000 | bytes 4718592 | tf_op jit(solution)/shard_map/attend/pallas_call | solution.py:269
  1148.6 20.3 %attend.24 = (bf16[12,6144,512]{2,1,0:T(8,128)(2,1)}, bf16[12,64,6144]{2,1,0:T(8,128)(2,1)}, f32[12,128,768]{2,1,0:T(8,128)}) custom-call(s32[13]{0:T(128)} %convert_reduce_fusion.12.count_ref, s32[576]{0:T(1024)} %select_reduce_fusion.2.code_ref, bf16[6,1152,128]{2,1,0:T(8,128)(2,1)} %get-tuple-element.1073.refs_0_, ...), custom_call_target="tpu_custom_call", output_to_operand_aliasing={{0}: (12, {}), {1}: (13, {})} | custom-call | flops 200000000 | bytes 4718592 | tf_op jit(solution)/shard_map/attend/pallas_call | solution.py:269
  1168.9 13.5 %attend.25 = (bf16[12,6144,512]{2,1,0:T(8,128)(2,1)}, bf16[12,64,6144]{2,1,0:T(8,128)(2,1)}, f32[12,128,768]{2,1,0:T(8,128)}) custom-call(s32[13]{0:T(128)} %convert_reduce_fusion.12.count_ref, s32[576]{0:T(1024)} %select_reduce_fusion.2.code_ref, bf16[4,1152,128]{2,1,0:T(8,128)(2,1)} %get-tuple-element.1069.refs_0_, ...), custom_call_target="tpu_custom_call", output_to_operand_aliasing={{0}: (12, {}), {1}: (13, {})} | custom-call | flops 200000000 | bytes 4718592 | tf_op jit(solution)/shard_map/attend/pallas_call | solution.py:269
  1182.4 20.3 %attend.26 = (bf16[12,6144,512]{2,1,0:T(8,128)(2,1)}, bf16[12,64,6144]{2,1,0:T(8,128)(2,1)}, f32[12,128,768]{2,1,0:T(8,128)}) custom-call(s32[13]{0:T(128)} %convert_reduce_fusion.12.count_ref, s32[576]{0:T(1024)} %select_reduce_fusion.2.code_ref, bf16[6,1152,128]{2,1,0:T(8,128)(2,1)} %get-tuple-element.1061.refs_0_, ...), custom_call_target="tpu_custom_call", output_to_operand_aliasing={{0}: (12, {}), {1}: (13, {})} | custom-call | flops 200000000 | bytes 4718592 | tf_op jit(solution)/shard_map/attend/pallas_call | solution.py:269
  1202.7 20.3 %attend.27 = (bf16[12,6144,512]{2,1,0:T(8,128)(2,1)}, bf16[12,64,6144]{2,1,0:T(8,128)(2,1)}, f32[12,128,768]{2,1,0:T(8,128)}) custom-call(s32[13]{0:T(128)} %convert_reduce_fusion.12.count_ref, s32[576]{0:T(1024)} %select_reduce_fusion.2.code_ref, bf16[8,1152,128]{2,1,0:T(8,128)(2,1)} %get-tuple-element.1057.refs_0_, ...), custom_call_target="tpu_custom_call", output_to_operand_aliasing={{0}: (12, {}), {1}: (13, {})} | custom-call | flops 200000000 | bytes 4718592 | tf_op jit(solution)/shard_map/attend/pallas_call | solution.py:269
  1223.0 15.5 %attend.28 = (bf16[12,6144,512]{2,1,0:T(8,128)(2,1)}, bf16[12,64,6144]{2,1,0:T(8,128)(2,1)}, f32[12,128,768]{2,1,0:T(8,128)}) custom-call(s32[13]{0:T(128)} %convert_reduce_fusion.12.count_ref, s32[576]{0:T(1024)} %select_reduce_fusion.2.code_ref, bf16[8,1152,128]{2,1,0:T(8,128)(2,1)} %get-tuple-element.1053.refs_0_, ...), custom_call_target="tpu_custom_call", output_to_operand_aliasing={{0}: (12, {}), {1}: (13, {})} | custom-call | flops 200000000 | bytes 4718592 | tf_op jit(solution)/shard_map/attend/pallas_call | solution.py:269
  1238.5 14.2 %attend.29 = (bf16[12,6144,512]{2,1,0:T(8,128)(2,1)}, bf16[12,64,6144]{2,1,0:T(8,128)(2,1)}, f32[12,128,768]{2,1,0:T(8,128)}) custom-call(s32[13]{0:T(128)} %convert_reduce_fusion.12.count_ref, s32[576]{0:T(1024)} %select_reduce_fusion.2.code_ref, bf16[8,1152,128]{2,1,0:T(8,128)(2,1)} %get-tuple-element.1049.refs_0_, ...), custom_call_target="tpu_custom_call", output_to_operand_aliasing={{0}: (12, {}), {1}: (13, {})} | custom-call | flops 200000000 | bytes 4718592 | tf_op jit(solution)/shard_map/attend/pallas_call | solution.py:269
  1252.7 11.3 attend.30
  1264.0 8.7 attend.31
  1272.9 8.9 attend.32
  (337 shorter events, 91.9 us)
Async XLA Ops:
  28.7 79.3 %collective-permute-start.32 = (bf16[4,1152,128]{2,1,0:T(8,128)(2,1)}, bf16[4,1152,128]{2,1,0:T(8,128)(2,1)}, u32[]{:S(2)}, u32[]{:S(2)}) collective-permute-start(bf16[4,1152,128]{2,1,0:T(8,128)(2,1)} %get-tuple-element.1019), channel_id=1, source_target_pairs={{0,2},{1,3},{2,0},{3,1},{4,6},{5,7},{6,4},{7,5}} | collective-permute-start | bytes 3538952 | tf_op jit(solution)/shard_map/ppermute | solution.py:386
  28.8 79.6 %collective-permute-start.33 = (bf16[4,1152,128]{2,1,0:T(8,128)(2,1)}, bf16[4,1152,128]{2,1,0:T(8,128)(2,1)}, u32[]{:S(2)}, u32[]{:S(2)}) collective-permute-start(bf16[4,1152,128]{2,1,0:T(8,128)(2,1)} %get-tuple-element.1020), channel_id=1, source_target_pairs={{0,4},{1,5},{2,6},{3,7},{4,0},{5,1},{6,2},{7,3}} | collective-permute-start | bytes 3538952 | tf_op jit(solution)/shard_map/ppermute | solution.py:386
  30.8 77.7 %collective-permute-start.34 = (bf16[4,1152,128]{2,1,0:T(8,128)(2,1)}, bf16[4,1152,128]{2,1,0:T(8,128)(2,1)}, u32[]{:S(2)}, u32[]{:S(2)}) collective-permute-start(bf16[4,1152,128]{2,1,0:T(8,128)(2,1)} %get-tuple-element.1021), channel_id=1, source_target_pairs={{0,6},{1,7},{2,4},{3,5},{4,2},{5,3},{6,0},{7,1}} | collective-permute-start | bytes 3538952 | tf_op jit(solution)/shard_map/ppermute | solution.py:386
  32.2 74.8 %collective-permute-start.8 = (bf16[2,1152,128]{2,1,0:T(8,128)(2,1)}, bf16[2,1152,128]{2,1,0:T(8,128)(2,1)S(1)}, u32[]{:S(2)}, u32[]{:S(2)}) collective-permute-start(bf16[2,1152,128]{2,1,0:T(8,128)(2,1)} %get-tuple-element.979), channel_id=1, source_target_pairs={{0,4},{1,5},{2,6},{3,7},{4,0},{5,1},{6,2},{7,3}} | collective-permute-start | bytes 1769480 | tf_op jit(solution)/shard_map/ppermute | solution.py:386
  33.8 73.2 %collective-permute-start.9 = (bf16[2,1152,128]{2,1,0:T(8,128)(2,1)S(1)}, bf16[2,1152,128]{2,1,0:T(8,128)(2,1)S(1)}, u32[]{:S(2)}, u32[]{:S(2)}) collective-permute-start(bf16[2,1152,128]{2,1,0:T(8,128)(2,1)S(1)} %copy-done.53), channel_id=1, source_target_pairs={{0,6},{1,7},{2,4},{3,5},{4,2},{5,3},{6,0},{7,1}} | collective-permute-start | bytes 1769480 | tf_op jit(solution)/shard_map/ppermute | solution.py:386
  128.0 79.7 %collective-permute-start.11 = (bf16[6,1152,128]{2,1,0:T(8,128)(2,1)}, bf16[6,1152,128]{2,1,0:T(8,128)(2,1)}, u32[]{:S(2)}, u32[]{:S(2)}) collective-permute-start(bf16[6,1152,128]{2,1,0:T(8,128)(2,1)} %get-tuple-element.982), channel_id=1, source_target_pairs={{0,4},{1,5},{2,6},{3,7},{4,0},{5,1},{6,2},{7,3}} | collective-permute-start | bytes 5308424 | tf_op jit(solution)/shard_map/ppermute | solution.py:386
  128.6 95.7 %collective-permute-start.12 = (bf16[6,1152,128]{2,1,0:T(8,128)(2,1)}, bf16[6,1152,128]{2,1,0:T(8,128)(2,1)}, u32[]{:S(2)}, u32[]{:S(2)}) collective-permute-start(bf16[6,1152,128]{2,1,0:T(8,128)(2,1)} %get-tuple-element.983), channel_id=1, source_target_pairs={{0,6},{1,7},{2,4},{3,5},{4,2},{5,3},{6,0},{7,1}} | collective-permute-start | bytes 5308424 | tf_op jit(solution)/shard_map/ppermute | solution.py:386
  130.3 94.1 %collective-permute-start.95 = (bf16[6,1152,128]{2,1,0:T(8,128)(2,1)S(1)}, bf16[6,1152,128]{2,1,0:T(8,128)(2,1)}, u32[]{:S(2)}, u32[]{:S(2)}) collective-permute-start(bf16[6,1152,128]{2,1,0:T(8,128)(2,1)S(1)} %copy-done.8), channel_id=1, source_target_pairs={{0,1},{1,0},{2,3},{3,2},{4,5},{5,4},{6,7},{7,6}} | collective-permute-start | bytes 5308424 | tf_op jit(solution)/shard_map/ppermute | solution.py:386
  132.0 111.3 %collective-permute-start.35 = (bf16[6,1152,128]{2,1,0:T(8,128)(2,1)}, bf16[6,1152,128]{2,1,0:T(8,128)(2,1)}, u32[]{:S(2)}, u32[]{:S(2)}) collective-permute-start(bf16[6,1152,128]{2,1,0:T(8,128)(2,1)} %get-tuple-element.1022), channel_id=1, source_target_pairs={{0,2},{1,3},{2,0},{3,1},{4,5},{5,4},{6,7},{7,6}} | collective-permute-start | bytes 5308424 | tf_op jit(solution)/shard_map/ppermute | solution.py:386
  168.1 77.5 %collective-permute-start.36 = (bf16[6,1152,128]{2,1,0:T(8,128)(2,1)}, bf16[6,1152,128]{2,1,0:T(8,128)(2,1)}, u32[]{:S(2)}, u32[]{:S(2)}) collective-permute-start(bf16[6,1152,128]{2,1,0:T(8,128)(2,1)} %get-tuple-element.1023), channel_id=1, source_target_pairs={{0,4},{1,5},{2,6},{3,7},{4,0},{5,1},{6,2},{7,3}} | collective-permute-start | bytes 5308424 | tf_op jit(solution)/shard_map/ppermute | solution.py:386
  207.7 74.9 %collective-permute-start.37 = (bf16[6,1152,128]{2,1,0:T(8,128)(2,1)}, bf16[6,1152,128]{2,1,0:T(8,128)(2,1)}, u32[]{:S(2)}, u32[]{:S(2)}) collective-permute-start(bf16[6,1152,128]{2,1,0:T(8,128)(2,1)} %get-tuple-element.1024), channel_id=1, source_target_pairs={{0,4},{1,5},{2,6},{3,7},{4,0},{5,1},{6,2},{7,3}} | collective-permute-start | bytes 5308424 | tf_op jit(solution)/shard_map/ppermute | solution.py:386
  224.3 58.6 %collective-permute-start.91 = (bf16[6,1152,128]{2,1,0:T(8,128)(2,1)}, bf16[6,1152,128]{2,1,0:T(8,128)(2,1)}, u32[]{:S(2)}, u32[]{:S(2)}) collective-permute-start(bf16[6,1152,128]{2,1,0:T(8,128)(2,1)} %get-tuple-element.1081.refs_0_), channel_id=1, source_target_pairs={{0,1},{1,0},{2,3},{3,2},{4,5},{5,4},{6,7},{7,6}} | collective-permute-start | bytes 5308424 | tf_op jit(solution)/shard_map/ppermute | solution.py:386
  224.4 61.9 %collective-permute-start.96 = (bf16[6,1152,128]{2,1,0:T(8,128)(2,1)}, bf16[6,1152,128]{2,1,0:T(8,128)(2,1)}, u32[]{:S(2)}, u32[]{:S(2)}) collective-permute-start(bf16[6,1152,128]{2,1,0:T(8,128)(2,1)} %collective-permute-done.10.refs_2_), channel_id=1, source_target_pairs={{0,1},{1,0},{2,3},{3,2},{4,5},{5,4},{6,7},{7,6}} | collective-permute-start | bytes 5308424 | tf_op jit(solution)/shard_map/ppermute | solution.py:386
  243.3 48.0 %collective-permute-start.97 = (bf16[6,1152,128]{2,1,0:T(8,128)(2,1)}, bf16[6,1152,128]{2,1,0:T(8,128)(2,1)}, u32[]{:S(2)}, u32[]{:S(2)}) collective-permute-start(bf16[6,1152,128]{2,1,0:T(8,128)(2,1)} %collective-permute-done.11.refs_4_), channel_id=1, source_target_pairs={{0,1},{1,0},{2,3},{3,2},{4,5},{5,4},{6,7},{7,6}} | collective-permute-start | bytes 5308424 | tf_op jit(solution)/shard_map/ppermute | solution.py:386
  245.6 57.3 %collective-permute-start.98 = (bf16[6,1152,128]{2,1,0:T(8,128)(2,1)}, bf16[6,1152,128]{2,1,0:T(8,128)(2,1)}, u32[]{:S(2)}, u32[]{:S(2)}) collective-permute-start(bf16[6,1152,128]{2,1,0:T(8,128)(2,1)} %collective-permute-done.12.refs_6_), channel_id=1, source_target_pairs={{0,1},{1,0},{2,3},{3,2},{4,5},{5,4},{6,7},{7,6}} | collective-permute-start | bytes 5308424 | tf_op jit(solution)/shard_map/ppermute | solution.py:386
  282.9 81.6 %collective-permute-start.14 = (bf16[6,1152,128]{2,1,0:T(8,128)(2,1)}, bf16[6,1152,128]{2,1,0:T(8,128)(2,1)}, u32[]{:S(2)}, u32[]{:S(2)}) collective-permute-start(bf16[6,1152,128]{2,1,0:T(8,128)(2,1)} %get-tuple-element.985), channel_id=1, source_target_pairs={{0,4},{1,5},{4,0},{5,1},{6,2},{7,3}} | collective-permute-start | bytes 5308424 | tf_op jit(solution)/shard_map/ppermute | solution.py:386
  286.3 78.3 %collective-permute-start.15 = (bf16[6,1152,128]{2,1,0:T(8,128)(2,1)}, bf16[6,1152,128]{2,1,0:T(8,128)(2,1)}, u32[]{:S(2)}, u32[]{:S(2)}) collective-permute-start(bf16[6,1152,128]{2,1,0:T(8,128)(2,1)} %get-tuple-element.986), channel_id=1, source_target_pairs={{0,6},{1,7},{4,2},{5,3},{6,0},{7,1}} | collective-permute-start | bytes 5308424 | tf_op jit(solution)/shard_map/ppermute | solution.py:386
  291.3 73.8 %collective-permute-start.86 = (bf16[6,1152,128]{2,1,0:T(8,128)(2,1)}, bf16[6,1152,128]{2,1,0:T(8,128)(2,1)}, u32[]{:S(2)}, u32[]{:S(2)}) collective-permute-start(bf16[6,1152,128]{2,1,0:T(8,128)(2,1)} %get-tuple-element.1073.refs_0_), channel_id=1, source_target_pairs={{0,1},{1,0},{2,3},{3,2},{4,5},{5,4},{6,7},{7,6}} | collective-permute-start | bytes 5308424 | tf_op jit(solution)/shard_map/ppermute | solution.py:386
  302.9 80.8 %collective-permute-start.38 = (bf16[4,1152,128]{2,1,0:T(8,128)(2,1)}, bf16[4,1152,128]{2,1,0:T(8,128)(2,1)S(1)}, u32[]{:S(2)}, u32[]{:S(2)}) collective-permute-start(bf16[4,1152,128]{2,1,0:T(8,128)(2,1)} %get-tuple-element.1025), channel_id=1, source_target_pairs={{0,2},{1,3},{2,0},{3,1},{4,5},{5,4},{6,7},{7,6}} | collective-permute-start | bytes 3538952 | tf_op jit(solution)/shard_map/ppermute | solution.py:386
  324.3 65.5 %collective-permute-start.39 = (bf16[4,1152,128]{2,1,0:T(8,128)(2,1)}, bf16[4,1152,128]{2,1,0:T(8,128)(2,1)}, u32[]{:S(2)}, u32[]{:S(2)}) collective-permute-start(bf16[4,1152,128]{2,1,0:T(8,128)(2,1)} %get-tuple-element.1026), channel_id=1, source_target_pairs={{0,4},{1,5},{2,6},{3,7},{4,0},{5,1},{6,2},{7,3}} | collective-permute-start | bytes 3538952 | tf_op jit(solution)/shard_map/ppermute | solution.py:386
  364.5 71.9 %collective-permute-start.87 = (bf16[6,1152,128]{2,1,0:T(8,128)(2,1)}, bf16[6,1152,128]{2,1,0:T(8,128)(2,1)}, u32[]{:S(2)}, u32[]{:S(2)}) collective-permute-start(bf16[6,1152,128]{2,1,0:T(8,128)(2,1)} %collective-permute-done.37), channel_id=1, source_target_pairs={{4,6},{5,7},{6,4},{7,5},{0,1},{1,0},{2,3},{3,2}} | collective-permute-start | bytes 5308424 | tf_op jit(solution)/shard_map/ppermute | solution.py:386
  364.5 73.8 %collective-permute-start.92 = (bf16[6,1152,128]{2,1,0:T(8,128)(2,1)}, bf16[6,1152,128]{2,1,0:T(8,128)(2,1)}, u32[]{:S(2)}, u32[]{:S(2)}) collective-permute-start(bf16[6,1152,128]{2,1,0:T(8,128)(2,1)} %collective-permute-done.35.refs_2_), channel_id=1, source_target_pairs={{0,1},{1,0},{2,3},{3,2},{4,5},{5,4},{6,7},{7,6}} | collective-permute-start | bytes 5308424 | tf_op jit(solution)/shard_map/ppermute | solution.py:386
  365.0 73.8 %collective-permute-start.93 = (bf16[6,1152,128]{2,1,0:T(8,128)(2,1)}, bf16[6,1152,128]{2,1,0:T(8,128)(2,1)}, u32[]{:S(2)}, u32[]{:S(2)}) collective-permute-start(bf16[6,1152,128]{2,1,0:T(8,128)(2,1)} %collective-permute-done.36.refs_4_), channel_id=1, source_target_pairs={{0,1},{1,0},{2,3},{3,2},{4,5},{5,4},{6,7},{7,6}} | collective-permute-start | bytes 5308424 | tf_op jit(solution)/shard_map/ppermute | solution.py:386
  389.8 46.6 %collective-permute-start.82 = (bf16[4,1152,128]{2,1,0:T(8,128)(2,1)}, bf16[4,1152,128]{2,1,0:T(8,128)(2,1)}, u32[]{:S(2)}, u32[]{:S(2)}) collective-permute-start(bf16[4,1152,128]{2,1,0:T(8,128)(2,1)} %get-tuple-element.1069.refs_0_), channel_id=1, source_target_pairs={{0,1},{1,0},{2,3},{3,2},{4,5},{5,4},{6,7},{7,6}} | collective-permute-start | bytes 3538952 | tf_op jit(solution)/shard_map/ppermute | solution.py:386
  413.5 67.1 %collective-permute-start.16 = (bf16[6,1152,128]{2,1,0:T(8,128)(2,1)}, bf16[6,1152,128]{2,1,0:T(8,128)(2,1)}, u32[]{:S(2)}, u32[]{:S(2)}) collective-permute-start(bf16[6,1152,128]{2,1,0:T(8,128)(2,1)} %get-tuple-element.987), channel_id=1, source_target_pairs={{0,2},{1,3},{2,0},{3,1},{4,6},{5,7},{6,4},{7,5}} | collective-permute-start | bytes 5308424 | tf_op jit(solution)/shard_map/ppermute | solution.py:386
  436.4 81.0 %collective-permute-start.17 = (bf16[6,1152,128]{2,1,0:T(8,128)(2,1)}, bf16[6,1152,128]{2,1,0:T(8,128)(2,1)S(1)}, u32[]{:S(2)}, u32[]{:S(2)}) collective-permute-start(bf16[6,1152,128]{2,1,0:T(8,128)(2,1)} %get-tuple-element.988), channel_id=1, source_target_pairs={{0,4},{1,5},{2,6},{4,0},{5,1},{6,2},{7,3}} | collective-permute-start | bytes 5308424 | tf_op jit(solution)/shard_map/ppermute | solution.py:386
  439.6 77.9 %collective-permute-start.18 = (bf16[6,1152,128]{2,1,0:T(8,128)(2,1)}, bf16[6,1152,128]{2,1,0:T(8,128)(2,1)S(1)}, u32[]{:S(2)}, u32[]{:S(2)}) collective-permute-start(bf16[6,1152,128]{2,1,0:T(8,128)(2,1)} %get-tuple-element.989), channel_id=1, source_target_pairs={{0,6},{1,7},{2,4},{4,2},{5,3},{6,0},{7,1}} | collective-permute-start | bytes 5308424 | tf_op jit(solution)/shard_map/ppermute | solution.py:386
  517.5 54.5 %collective-permute-start.41 = (bf16[8,1152,128]{2,1,0:T(8,128)(2,1)}, bf16[8,1152,128]{2,1,0:T(8,128)(2,1)}, u32[]{:S(2)}, u32[]{:S(2)}) collective-permute-start(bf16[8,1152,128]{2,1,0:T(8,128)(2,1)} %get-tuple-element.1028), channel_id=1, source_target_pairs={{0,2},{1,3},{2,0},{3,1},{4,6},{5,7},{6,4},{7,5}} | collective-permute-start | bytes 7077896 | tf_op jit(solution)/shard_map/ppermute | solution.py:386
  518.7 103.9 %collective-permute-start.42 = (bf16[8,1152,128]{2,1,0:T(8,128)(2,1)}, bf16[8,1152,128]{2,1,0:T(8,128)(2,1)}, u32[]{:S(2)}, u32[]{:S(2)}) collective-permute-start(bf16[8,1152,128]{2,1,0:T(8,128)(2,1)} %get-tuple-element.1029), channel_id=1, source_target_pairs={{0,4},{1,5},{2,6},{3,7},{4,0},{5,1},{6,2},{7,3}} | collective-permute-start | bytes 7077896 | tf_op jit(solution)/shard_map/ppermute | solution.py:386
  519.9 103.9 %collective-permute-start.43 = (bf16[8,1152,128]{2,1,0:T(8,128)(2,1)}, bf16[8,1152,128]{2,1,0:T(8,128)(2,1)}, u32[]{:S(2)}, u32[]{:S(2)}) collective-permute-start(bf16[8,1152,128]{2,1,0:T(8,128)(2,1)} %get-tuple-element.1030), channel_id=1, source_target_pairs={{0,6},{1,7},{2,4},{3,5},{4,2},{5,3},{6,0},{7,1}} | collective-permute-start | bytes 7077896 | tf_op jit(solution)/shard_map/ppermute | solution.py:386
  521.5 102.3 %collective-permute-start.73 = (bf16[8,1152,128]{2,1,0:T(8,128)(2,1)}, bf16[8,1152,128]{2,1,0:T(8,128)(2,1)}, u32[]{:S(2)}, u32[]{:S(2)}) collective-permute-start(bf16[8,1152,128]{2,1,0:T(8,128)(2,1)} %get-tuple-element.1057.refs_0_), channel_id=1, source_target_pairs={{0,1},{1,0},{2,3},{3,2},{4,5},{5,4},{6,7},{7,6}} | collective-permute-start | bytes 7077896 | tf_op jit(solution)/shard_map/ppermute | solution.py:386
  543.2 83.6 %collective-permute-start.79 = (bf16[6,1152,128]{2,1,0:T(8,128)(2,1)}, bf16[6,1152,128]{2,1,0:T(8,128)(2,1)S(1)}, u32[]{:S(2)}, u32[]{:S(2)}) collective-permute-start(bf16[6,1152,128]{2,1,0:T(8,128)(2,1)} %collective-permute-done.16.refs_2_), channel_id=1, source_target_pairs={{0,1},{1,0},{2,3},{3,2},{4,5},{5,4},{6,7},{7,6}} | collective-permute-start | bytes 5308424 | tf_op jit(solution)/shard_map/ppermute | solution.py:386
  571.9 57.2 %collective-permute-start.80 = (bf16[6,1152,128]{2,1,0:T(8,128)(2,1)S(1)}, bf16[6,1152,128]{2,1,0:T(8,128)(2,1)S(1)}, u32[]{:S(2)}, u32[]{:S(2)}) collective-permute-start(bf16[6,1152,128]{2,1,0:T(8,128)(2,1)S(1)} %copy-done.14), channel_id=1, source_target_pairs={{0,1},{1,0},{2,3},{3,2},{4,5},{5,4},{6,7},{7,6}} | collective-permute-start | bytes 5308424 | tf_op jit(solution)/shard_map/ppermute | solution.py:386
  622.5 54.4 %collective-permute-start.19 = (bf16[8,1152,128]{2,1,0:T(8,128)(2,1)}, bf16[8,1152,128]{2,1,0:T(8,128)(2,1)}, u32[]{:S(2)}, u32[]{:S(2)}) collective-permute-start(bf16[8,1152,128]{2,1,0:T(8,128)(2,1)} %get-tuple-element.990), channel_id=1, source_target_pairs={{0,2},{1,3},{2,0},{3,1},{4,6},{5,7},{6,4},{7,5}} | collective-permute-start | bytes 7077896 | tf_op jit(solution)/shard_map/ppermute | solution.py:386
  626.8 104.2 %collective-permute-start.20 = (bf16[8,1152,128]{2,1,0:T(8,128)(2,1)}, bf16[8,1152,128]{2,1,0:T(8,128)(2,1)}, u32[]{:S(2)}, u32[]{:S(2)}) collective-permute-start(bf16[8,1152,128]{2,1,0:T(8,128)(2,1)} %get-tuple-element.991), channel_id=1, source_target_pairs={{0,4},{1,5},{2,6},{3,7},{4,0},{5,1},{6,2},{7,3}} | collective-permute-start | bytes 7077896 | tf_op jit(solution)/shard_map/ppermute | solution.py:386
  626.8 105.0 %collective-permute-start.21 = (bf16[8,1152,128]{2,1,0:T(8,128)(2,1)}, bf16[8,1152,128]{2,1,0:T(8,128)(2,1)}, u32[]{:S(2)}, u32[]{:S(2)}) collective-permute-start(bf16[8,1152,128]{2,1,0:T(8,128)(2,1)} %get-tuple-element.992), channel_id=1, source_target_pairs={{0,6},{1,7},{2,4},{3,5},{4,2},{5,3},{6,0},{7,1}} | collective-permute-start | bytes 7077896 | tf_op jit(solution)/shard_map/ppermute | solution.py:386
  630.3 101.7 %collective-permute-start.69 = (bf16[8,1152,128]{2,1,0:T(8,128)(2,1)}, bf16[8,1152,128]{2,1,0:T(8,128)(2,1)}, u32[]{:S(2)}, u32[]{:S(2)}) collective-permute-start(bf16[8,1152,128]{2,1,0:T(8,128)(2,1)} %get-tuple-element.1053.refs_0_), channel_id=1, source_target_pairs={{0,1},{1,0},{2,3},{3,2},{4,5},{5,4},{6,7},{7,6}} | collective-permute-start | bytes 7077896 | tf_op jit(solution)/shard_map/ppermute | solution.py:386
  652.0 82.5 %collective-permute-start.74 = (bf16[8,1152,128]{2,1,0:T(8,128)(2,1)}, bf16[8,1152,128]{2,1,0:T(8,128)(2,1)}, u32[]{:S(2)}, u32[]{:S(2)}) collective-permute-start(bf16[8,1152,128]{2,1,0:T(8,128)(2,1)} %collective-permute-done.41.refs_2_), channel_id=1, source_target_pairs={{0,1},{1,0},{2,3},{3,2},{4,5},{5,4},{6,7},{7,6}} | collective-permute-start | bytes 7077896 | tf_op jit(solution)/shard_map/ppermute | solution.py:386
  677.0 57.5 %collective-permute-start.75 = (bf16[8,1152,128]{2,1,0:T(8,128)(2,1)}, bf16[8,1152,128]{2,1,0:T(8,128)(2,1)}, u32[]{:S(2)}, u32[]{:S(2)}) collective-permute-start(bf16[8,1152,128]{2,1,0:T(8,128)(2,1)} %collective-permute-done.42.refs_4_), channel_id=1, source_target_pairs={{0,1},{1,0},{2,3},{3,2},{4,5},{5,4},{6,7},{7,6}} | collective-permute-start | bytes 7077896 | tf_op jit(solution)/shard_map/ppermute | solution.py:386
  731.0 54.4 %collective-permute-start.44 = (bf16[8,1152,128]{2,1,0:T(8,128)(2,1)}, bf16[8,1152,128]{2,1,0:T(8,128)(2,1)}, u32[]{:S(2)}, u32[]{:S(2)}) collective-permute-start(bf16[8,1152,128]{2,1,0:T(8,128)(2,1)} %get-tuple-element.1031), channel_id=1, source_target_pairs={{0,2},{1,3},{2,0},{3,1},{4,6},{5,7},{6,4},{7,5}} | collective-permute-start | bytes 7077896 | tf_op jit(solution)/shard_map/ppermute | solution.py:386
  731.8 103.0 %collective-permute-start.45 = (bf16[8,1152,128]{2,1,0:T(8,128)(2,1)}, bf16[8,1152,128]{2,1,0:T(8,128)(2,1)}, u32[]{:S(2)}, u32[]{:S(2)}) collective-permute-start(bf16[8,1152,128]{2,1,0:T(8,128)(2,1)} %get-tuple-element.1032), channel_id=1, source_target_pairs={{0,4},{1,5},{2,6},{3,7},{4,0},{5,1},{6,2},{7,3}} | collective-permute-start | bytes 7077896 | tf_op jit(solution)/shard_map/ppermute | solution.py:386
  732.1 103.7 %collective-permute-start.46 = (bf16[8,1152,128]{2,1,0:T(8,128)(2,1)}, bf16[8,1152,128]{2,1,0:T(8,128)(2,1)}, u32[]{:S(2)}, u32[]{:S(2)}) collective-permute-start(bf16[8,1152,128]{2,1,0:T(8,128)(2,1)} %get-tuple-element.1033), channel_id=1, source_target_pairs={{0,6},{1,7},{2,4},{3,5},{4,2},{5,3},{6,0},{7,1}} | collective-permute-start | bytes 7077896 | tf_op jit(solution)/shard_map/ppermute | solution.py:386
  734.5 115.5 %collective-permute-start.76 = (bf16[8,1152,128]{2,1,0:T(8,128)(2,1)}, bf16[8,1152,128]{2,1,0:T(8,128)(2,1)}, u32[]{:S(2)}, u32[]{:S(2)}) collective-permute-start(bf16[8,1152,128]{2,1,0:T(8,128)(2,1)} %collective-permute-done.43.refs_6_), channel_id=1, source_target_pairs={{0,1},{1,0},{2,3},{3,2},{4,5},{5,4},{6,7},{7,6}} | collective-permute-start | bytes 7077896 | tf_op jit(solution)/shard_map/ppermute | solution.py:386
  734.5 115.5 %collective-permute-start.65 = (bf16[8,1152,128]{2,1,0:T(8,128)(2,1)}, bf16[8,1152,128]{2,1,0:T(8,128)(2,1)}, u32[]{:S(2)}, u32[]{:S(2)}) collective-permute-start(bf16[8,1152,128]{2,1,0:T(8,128)(2,1)} %get-tuple-element.1049.refs_0_), channel_id=1, source_target_pairs={{0,1},{1,0},{2,3},{3,2},{4,5},{5,4},{6,7},{7,6}} | collective-permute-start | bytes 7077896 | tf_op jit(solution)/shard_map/ppermute | solution.py:386
  785.4 88.5 %collective-permute-start.22 = (bf16[6,1152,128]{2,1,0:T(8,128)(2,1)}, bf16[6,1152,128]{2,1,0:T(8,128)(2,1)}, u32[]{:S(2)}, u32[]{:S(2)}) collective-permute-start(bf16[6,1152,128]{2,1,0:T(8,128)(2,1)} %get-tuple-element.993), channel_id=1, source_target_pairs={{0,2},{1,3},{2,0},{3,1},{4,6},{5,7},{6,4},{7,5}} | collective-permute-start | bytes 5308424 | tf_op jit(solution)/shard_map/ppermute | solution.py:386
  834.8 79.7 %collective-permute-start.23 = (bf16[6,1152,128]{2,1,0:T(8,128)(2,1)}, bf16[6,1152,128]{2,1,0:T(8,128)(2,1)}, u32[]{:S(2)}, u32[]{:S(2)}) collective-permute-start(bf16[6,1152,128]{2,1,0:T(8,128)(2,1)} %get-tuple-element.994), channel_id=1, source_target_pairs={{0,4},{1,5},{2,6},{3,7},{4,0},{5,1},{6,2},{7,3}} | collective-permute-start | bytes 5308424 | tf_op jit(solution)/shard_map/ppermute | solution.py:386
  835.7 78.8 %collective-permute-start.24 = (bf16[6,1152,128]{2,1,0:T(8,128)(2,1)}, bf16[6,1152,128]{2,1,0:T(8,128)(2,1)}, u32[]{:S(2)}, u32[]{:S(2)}) collective-permute-start(bf16[6,1152,128]{2,1,0:T(8,128)(2,1)} %get-tuple-element.995), channel_id=1, source_target_pairs={{0,6},{1,7},{2,4},{3,5},{4,2},{5,3},{6,0},{7,1}} | collective-permute-start | bytes 5308424 | tf_op jit(solution)/shard_map/ppermute | solution.py:386
  850.0 87.1 %collective-permute-start.47 = (bf16[4,1152,128]{2,1,0:T(8,128)(2,1)}, bf16[4,1152,128]{2,1,0:T(8,128)(2,1)S(1)}, u32[]{:S(2)}, u32[]{:S(2)}) collective-permute-start(bf16[4,1152,128]{2,1,0:T(8,128)(2,1)} %get-tuple-element.1034), channel_id=1, source_target_pairs={{0,2},{1,3},{2,0},{3,1},{4,5},{5,4},{6,7},{7,6}} | collective-permute-start | bytes 3538952 | tf_op jit(solution)/shard_map/ppermute | solution.py:386
  850.0 87.1 %collective-permute-start.48 = (bf16[4,1152,128]{2,1,0:T(8,128)(2,1)}, bf16[4,1152,128]{2,1,0:T(8,128)(2,1)S(1)}, u32[]{:S(2)}, u32[]{:S(2)}) collective-permute-start(bf16[4,1152,128]{2,1,0:T(8,128)(2,1)} %get-tuple-element.1035), channel_id=1, source_target_pairs={{0,4},{1,5},{2,6},{3,7},{4,0},{5,1},{6,2},{7,3}} | collective-permute-start | bytes 3538952 | tf_op jit(solution)/shard_map/ppermute | solution.py:386
  873.9 85.2 %collective-permute-start.49 = (bf16[4,1152,128]{2,1,0:T(8,128)(2,1)}, bf16[4,1152,128]{2,1,0:T(8,128)(2,1)S(1)}, u32[]{:S(2)}, u32[]{:S(2)}) collective-permute-start(bf16[4,1152,128]{2,1,0:T(8,128)(2,1)} %get-tuple-element.1036), channel_id=1, source_target_pairs={{0,6},{1,7},{2,4},{3,5}} | collective-permute-start | bytes 3538952 | tf_op jit(solution)/shard_map/ppermute | solution.py:386
  914.5 59.1 %collective-permute-start.70 = (bf16[8,1152,128]{2,1,0:T(8,128)(2,1)}, bf16[8,1152,128]{2,1,0:T(8,128)(2,1)}, u32[]{:S(2)}, u32[]{:S(2)}) collective-permute-start(bf16[8,1152,128]{2,1,0:T(8,128)(2,1)} %collective-permute-done.19.refs_2_), channel_id=1, source_target_pairs={{0,1},{1,0},{2,3},{3,2},{4,5},{5,4},{6,7},{7,6}} | collective-permute-start | bytes 7077896 | tf_op jit(solution)/shard_map/ppermute | solution.py:386
  914.5 65.2 %collective-permute-start.71 = (bf16[8,1152,128]{2,1,0:T(8,128)(2,1)}, bf16[8,1152,128]{2,1,0:T(8,128)(2,1)}, u32[]{:S(2)}, u32[]{:S(2)}) collective-permute-start(bf16[8,1152,128]{2,1,0:T(8,128)(2,1)} %collective-permute-done.20.refs_4_), channel_id=1, source_target_pairs={{0,1},{1,0},{2,3},{3,2},{4,5},{5,4},{6,7},{7,6}} | collective-permute-start | bytes 7077896 | tf_op jit(solution)/shard_map/ppermute | solution.py:386
  937.1 42.7 %collective-permute-start.72 = (bf16[8,1152,128]{2,1,0:T(8,128)(2,1)}, bf16[8,1152,128]{2,1,0:T(8,128)(2,1)}, u32[]{:S(2)}, u32[]{:S(2)}) collective-permute-start(bf16[8,1152,128]{2,1,0:T(8,128)(2,1)} %collective-permute-done.21.refs_6_), channel_id=1, source_target_pairs={{0,1},{1,0},{2,3},{3,2},{4,5},{5,4},{6,7},{7,6}} | collective-permute-start | bytes 7077896 | tf_op jit(solution)/shard_map/ppermute | solution.py:386
  989.9 44.8 %collective-permute-start.66 = (bf16[8,1152,128]{2,1,0:T(8,128)(2,1)}, bf16[8,1152,128]{2,1,0:T(8,128)(2,1)}, u32[]{:S(2)}, u32[]{:S(2)}) collective-permute-start(bf16[8,1152,128]{2,1,0:T(8,128)(2,1)} %collective-permute-done.44.refs_2_), channel_id=1, source_target_pairs={{0,1},{1,0},{2,3},{3,2},{4,5},{5,4},{6,7},{7,6}} | collective-permute-start | bytes 7077896 | tf_op jit(solution)/shard_map/ppermute | solution.py:386
  1026.1 47.8 %collective-permute-start.67 = (bf16[8,1152,128]{2,1,0:T(8,128)(2,1)}, bf16[8,1152,128]{2,1,0:T(8,128)(2,1)}, u32[]{:S(2)}, u32[]{:S(2)}) collective-permute-start(bf16[8,1152,128]{2,1,0:T(8,128)(2,1)} %collective-permute-done.45.refs_4_), channel_id=1, source_target_pairs={{0,1},{1,0},{2,3},{3,2},{4,5},{5,4},{6,7},{7,6}} | collective-permute-start | bytes 7077896 | tf_op jit(solution)/shard_map/ppermute | solution.py:386
  1028.9 51.7 %collective-permute-start.68 = (bf16[8,1152,128]{2,1,0:T(8,128)(2,1)}, bf16[8,1152,128]{2,1,0:T(8,128)(2,1)}, u32[]{:S(2)}, u32[]{:S(2)}) collective-permute-start(bf16[8,1152,128]{2,1,0:T(8,128)(2,1)} %collective-permute-done.46.refs_6_), channel_id=1, source_target_pairs={{0,1},{1,0},{2,3},{3,2},{4,5},{5,4},{6,7},{7,6}} | collective-permute-start | bytes 7077896 | tf_op jit(solution)/shard_map/ppermute | solution.py:386
  1034.2 47.0 %collective-permute-start.62 = (bf16[6,1152,128]{2,1,0:T(8,128)(2,1)}, bf16[6,1152,128]{2,1,0:T(8,128)(2,1)S(1)}, u32[]{:S(2)}, u32[]{:S(2)}) collective-permute-start(bf16[6,1152,128]{2,1,0:T(8,128)(2,1)} %collective-permute-done.22.refs_2_), channel_id=1, source_target_pairs={{0,1},{1,0},{2,3},{3,2},{4,5},{5,4},{6,7},{7,6}} | collective-permute-start | bytes 5308424 | tf_op jit(solution)/shard_map/ppermute | solution.py:386
  1034.4 47.6 %collective-permute-start.63 = (bf16[6,1152,128]{2,1,0:T(8,128)(2,1)}, bf16[6,1152,128]{2,1,0:T(8,128)(2,1)}, u32[]{:S(2)}, u32[]{:S(2)}) collective-permute-start(bf16[6,1152,128]{2,1,0:T(8,128)(2,1)} %collective-permute-done.23.refs_4_), channel_id=1, source_target_pairs={{0,1},{1,0},{2,3},{3,2},{4,5},{5,4},{6,7},{7,6}} | collective-permute-start | bytes 5308424 | tf_op jit(solution)/shard_map/ppermute | solution.py:386
  1034.7 47.3 %collective-permute-start.64 = (bf16[6,1152,128]{2,1,0:T(8,128)(2,1)}, bf16[6,1152,128]{2,1,0:T(8,128)(2,1)}, u32[]{:S(2)}, u32[]{:S(2)}) collective-permute-start(bf16[6,1152,128]{2,1,0:T(8,128)(2,1)} %collective-permute-done.24.refs_6_), channel_id=1, source_target_pairs={{0,1},{1,0},{2,3},{3,2},{4,5},{5,4},{6,7},{7,6}} | collective-permute-start | bytes 5308424 | tf_op jit(solution)/shard_map/ppermute | solution.py:386
  1080.6 192.1 %collective-permute-start.54 = (bf16[2,1152,128]{2,1,0:T(8,128)(2,1)}, bf16[2,1152,128]{2,1,0:T(8,128)(2,1)}, u32[]{:S(2)}, u32[]{:S(2)}) collective-permute-start(bf16[2,1152,128]{2,1,0:T(8,128)(2,1)} %copy-done.35), channel_id=1, source_target_pairs={{0,1},{1,0},{2,3},{3,2},{4,5},{5,4},{6,7},{7,6}} | collective-permute-start | bytes 1769480 | tf_op jit(solution)/shard_map/ppermute | solution.py:386
  1080.7 192.1 %collective-permute-start.56 = (bf16[2,1152,128]{2,1,0:T(8,128)(2,1)}, bf16[2,1152,128]{2,1,0:T(8,128)(2,1)}, u32[]{:S(2)}, u32[]{:S(2)}) collective-permute-start(bf16[2,1152,128]{2,1,0:T(8,128)(2,1)} %collective-permute-done.55.refs_14_), channel_id=1, source_target_pairs={{0,1},{1,0},{2,3},{3,2},{4,5},{5,4},{6,7},{7,6}} | collective-permute-start | bytes 1769480 | tf_op jit(solution)/shard_map/ppermute | solution.py:386
  1081.5 191.3 %collective-permute-start.27 = (bf16[2,1152,128]{2,1,0:T(8,128)(2,1)}, bf16[2,1152,128]{2,1,0:T(8,128)(2,1)}, u32[]{:S(2)}, u32[]{:S(2)}) collective-permute-start(bf16[2,1152,128]{2,1,0:T(8,128)(2,1)} %collective-permute-done.26.refs_2_), channel_id=1, source_target_pairs={{0,1},{1,0},{2,3},{3,2},{4,5},{5,4},{6,7},{7,6}} | collective-permute-start | bytes 1769480 | tf_op jit(solution)/shard_map/ppermute | solution.py:386
  1082.0 190.8 %collective-permute-start.29 = (bf16[2,1152,128]{2,1,0:T(8,128)(2,1)}, bf16[2,1152,128]{2,1,0:T(8,128)(2,1)}, u32[]{:S(2)}, u32[]{:S(2)}) collective-permute-start(bf16[2,1152,128]{2,1,0:T(8,128)(2,1)} %collective-permute-done.28.refs_4_), channel_id=1, source_target_pairs={{0,1},{1,0},{2,3},{3,2},{4,5},{5,4},{6,7},{7,6}} | collective-permute-start | bytes 1769480 | tf_op jit(solution)/shard_map/ppermute | solution.py:386
  1082.0 190.8 %collective-permute-start.31 = (bf16[2,1152,128]{2,1,0:T(8,128)(2,1)}, bf16[2,1152,128]{2,1,0:T(8,128)(2,1)}, u32[]{:S(2)}, u32[]{:S(2)}) collective-permute-start(bf16[2,1152,128]{2,1,0:T(8,128)(2,1)} %collective-permute-done.30.refs_6_), channel_id=1, source_target_pairs={{0,1},{1,0},{2,3},{3,2},{4,5},{5,4},{6,7},{7,6}} | collective-permute-start | bytes 1769480 | tf_op jit(solution)/shard_map/ppermute | solution.py:386
  (89 other events, 2994.2 us)
